TPU v7x, 16 devices: a whole 2x2x2 slice. The times are simulated.
16 devices in a mesh: tp: 16 (over z, y, x, core).
Axes of the slice: x: 2, y: 2, z: 2, core: 2. Of those that a mesh axis runs over, the one named last changes fastest.
Arguments:
- x_input: bfloat16 [2, 2048, 4096], P(None, 'tp')
- w_query: bfloat16 [4096, 4096], P(None, 'tp')
- w_key: bfloat16 [4096, 4096], P(None, 'tp')
- w_value: bfloat16 [4096, 4096], P(None, 'tp')
- w_out: bfloat16 [4096, 4096], P('tp')
- g_query: bfloat16 [4096], P('tp')
- g_key: bfloat16 [4096], P('tp')
- g_attn: bfloat16 [4096], replicated
- grad_y: bfloat16 [2, 2048, 4096], P(None, 'tp')
Outputs:
- output 1: bfloat16 [2, 2048, 4096], P(None, 'tp')
- output 2: bfloat16 [2, 2048, 4096], P(None, 'tp')
- output 3: bfloat16 [4096, 4096], P(None, 'tp')
- output 4: bfloat16 [4096, 4096], P(None, 'tp')
- output 5: bfloat16 [4096, 4096], P(None, 'tp')
- output 6: bfloat16 [4096, 4096], P('tp')
- output 7: bfloat16 [4096], P('tp')
- output 8: bfloat16 [4096], P('tp')
- output 9: bfloat16 [4096], replicated
All inputs are finite; a program needn't handle non-finite values.
Results may differ from a plain program's by a relative error of at most 0.0178161.
Values are sent between devices in bfloat16 or wider.
A program may use at most 1 GiB of HBM per device.

v0:
```python
import jax
import jax.numpy as jnp
from jax import lax
from jax.sharding import PartitionSpec as P

HEAD_SIZE = 128
ROPE_THETA = 500000.0
NORM_EPS = 1e-6


def rope_tables(seq_len):
    half_dim = HEAD_SIZE // 2
    inv_freq = 1.0 / (ROPE_THETA ** (jnp.arange(half_dim, dtype=jnp.float32) / half_dim))
    angles = jnp.arange(seq_len, dtype=jnp.float32)[:, None] * inv_freq[None, :]
    return jnp.cos(angles)[:, None, :], jnp.sin(angles)[:, None, :]


def rotate(values, cos_t, sin_t):
    lower_half, upper_half = jnp.split(values, 2, axis=-1)
    return jnp.concatenate([lower_half * cos_t - upper_half * sin_t, upper_half * cos_t + lower_half * sin_t], axis=-1)


def rotate_back(values, cos_t, sin_t):
    lower_half, upper_half = jnp.split(values, 2, axis=-1)
    return jnp.concatenate([lower_half * cos_t + upper_half * sin_t, upper_half * cos_t - lower_half * sin_t], axis=-1)


def local_block(x_loc, wq_loc, wk_loc, wv_loc, wo_loc, gq_loc, gk_loc, g_attn, dy_loc):
    batch_size, seq_loc, model_dim = x_loc.shape
    local_dim = wq_loc.shape[1]
    x_full = lax.all_gather(x_loc, 'tp', axis=1, tiled=True)
    seq_len = x_full.shape[1]
    head_shape = (batch_size, seq_len, local_dim // HEAD_SIZE, HEAD_SIZE)
    flat_shape = (batch_size, seq_len, local_dim)
    cos_t, sin_t = rope_tables(seq_len)
    causal = jnp.arange(seq_len)[:, None] >= jnp.arange(seq_len)[None, :]
    attn_scale = HEAD_SIZE ** -0.5
    q_raw = jnp.einsum('bsd,de->bse', x_full, wq_loc, preferred_element_type=jnp.float32)
    k_raw = jnp.einsum('bsd,de->bse', x_full, wk_loc, preferred_element_type=jnp.float32)
    v_heads = jnp.einsum('bsd,de->bse', x_full, wv_loc, preferred_element_type=jnp.float32).astype(jnp.bfloat16).reshape(head_shape)
    sq_sums = lax.psum(jnp.stack([jnp.sum(q_raw * q_raw, axis=-1), jnp.sum(k_raw * k_raw, axis=-1)]), 'tp')
    inv_rms = lax.rsqrt(sq_sums / model_dim + NORM_EPS)[..., None]
    q_unit = q_raw * inv_rms[0]
    k_unit = k_raw * inv_rms[1]
    gq_f = gq_loc.astype(jnp.float32)
    gk_f = gk_loc.astype(jnp.float32)
    q_rot = rotate((q_unit * gq_f).reshape(head_shape), cos_t, sin_t).astype(jnp.bfloat16)
    k_rot = rotate((k_unit * gk_f).reshape(head_shape), cos_t, sin_t).astype(jnp.bfloat16)
    scores = jnp.einsum('bqhd,bkhd->bhqk', q_rot, k_rot, preferred_element_type=jnp.float32) * attn_scale
    attn_probs = jax.nn.softmax(jnp.where(causal, scores, -1e30), axis=-1)
    probs_low = attn_probs.astype(jnp.bfloat16)
    attn_heads = jnp.einsum('bhqk,bkhd->bqhd', probs_low, v_heads, preferred_element_type=jnp.float32).astype(jnp.bfloat16).reshape(flat_shape)
    attn_part = jnp.einsum('bse,ed->bsd', attn_heads, wo_loc, preferred_element_type=jnp.float32)
    attn_loc = lax.psum_scatter(attn_part, 'tp', scatter_dimension=1, tiled=True)
    post_rms = lax.rsqrt(jnp.mean(attn_loc * attn_loc, axis=-1, keepdims=True) + NORM_EPS)
    normed = attn_loc * post_rms
    ga_f = g_attn.astype(jnp.float32)
    dy_f = dy_loc.astype(jnp.float32)
    y_loc = (x_loc.astype(jnp.float32) + normed * ga_f).astype(jnp.bfloat16)

    grad_ga = lax.psum(jnp.sum(dy_f * normed, axis=(0, 1)), 'tp')
    g_normed = dy_f * ga_f
    d_attn = post_rms * (g_normed - normed * jnp.mean(g_normed * normed, axis=-1, keepdims=True))
    d_attn_full = lax.all_gather(d_attn.astype(jnp.bfloat16), 'tp', axis=1, tiled=True)
    grad_wo = jnp.einsum('bse,bsd->ed', attn_heads, d_attn_full, preferred_element_type=jnp.float32)
    d_heads = jnp.einsum('bsd,ed->bse', d_attn_full, wo_loc, preferred_element_type=jnp.float32).astype(jnp.bfloat16).reshape(head_shape)
    d_probs = jnp.einsum('bqhd,bkhd->bhqk', d_heads, v_heads, preferred_element_type=jnp.float32)
    d_value = jnp.einsum('bhqk,bqhd->bkhd', probs_low, d_heads, preferred_element_type=jnp.float32).astype(jnp.bfloat16).reshape(flat_shape)
    d_scores = (attn_probs * (d_probs - jnp.sum(attn_probs * d_probs, axis=-1, keepdims=True)) * attn_scale).astype(jnp.bfloat16)
    dq_rot = jnp.einsum('bhqk,bkhd->bqhd', d_scores, k_rot, preferred_element_type=jnp.float32)
    dk_rot = jnp.einsum('bhqk,bqhd->bkhd', d_scores, q_rot, preferred_element_type=jnp.float32)
    dq_hat = rotate_back(dq_rot, cos_t, sin_t).reshape(flat_shape)
    dk_hat = rotate_back(dk_rot, cos_t, sin_t).reshape(flat_shape)
    grad_gq = jnp.sum(dq_hat * q_unit, axis=(0, 1))
    grad_gk = jnp.sum(dk_hat * k_unit, axis=(0, 1))
    dq_unit = dq_hat * gq_f
    dk_unit = dk_hat * gk_f
    unit_dots = lax.psum(jnp.stack([jnp.sum(dq_unit * q_unit, axis=-1), jnp.sum(dk_unit * k_unit, axis=-1)]), 'tp')[..., None] / model_dim
    dq_raw = (inv_rms[0] * (dq_unit - q_unit * unit_dots[0])).astype(jnp.bfloat16)
    dk_raw = (inv_rms[1] * (dk_unit - k_unit * unit_dots[1])).astype(jnp.bfloat16)
    grad_wq = jnp.einsum('bsd,bse->de', x_full, dq_raw, preferred_element_type=jnp.float32)
    grad_wk = jnp.einsum('bsd,bse->de', x_full, dk_raw, preferred_element_type=jnp.float32)
    grad_wv = jnp.einsum('bsd,bse->de', x_full, d_value, preferred_element_type=jnp.float32)
    dx_part = (jnp.einsum('bse,de->bsd', dq_raw, wq_loc, preferred_element_type=jnp.float32)
               + jnp.einsum('bse,de->bsd', dk_raw, wk_loc, preferred_element_type=jnp.float32)
               + jnp.einsum('bse,de->bsd', d_value, wv_loc, preferred_element_type=jnp.float32))
    grad_x = lax.psum_scatter(dx_part, 'tp', scatter_dimension=1, tiled=True) + dy_f
    return (y_loc, grad_x.astype(jnp.bfloat16), grad_wq.astype(jnp.bfloat16), grad_wk.astype(jnp.bfloat16),
            grad_wv.astype(jnp.bfloat16), grad_wo.astype(jnp.bfloat16), grad_gq.astype(jnp.bfloat16),
            grad_gk.astype(jnp.bfloat16), grad_ga.astype(jnp.bfloat16))


def solution(mesh):
    act_spec = P(None, 'tp', None)
    col_spec = P(None, 'tp')
    row_spec = P('tp', None)
    vec_spec = P('tp')
    in_specs = (act_spec, col_spec, col_spec, col_spec, row_spec, vec_spec, vec_spec, P(), act_spec)
    out_specs = (act_spec, act_spec, col_spec, col_spec, col_spec, row_spec, vec_spec, vec_spec, P())
    return jax.shard_map(local_block, mesh=mesh, in_specs=in_specs, out_specs=out_specs, check_vma=False)
```

profile of v0, /device:TPU:0, one launch (start us, length us, event | category | flops | bytes accessed | tf_op | source)
XLA Modules:
  0.0 2313.9 jit_solution(12316045837869392695)
XLA Ops:
  9.3 4.7 fusion.63
  14.0 4.1 iota_compare_fusion
  18.0 126.5 %all-gather.3.cloned.1.call-done = bf16[2,2048,4096]{2,1,0:T(8,128)(2,1)} async-done(((bf16[2,128,4096]{2,1,0:T(8,128)(2,1)}), bf16[2,2048,4096]{2,1,0:T(8,128)(2,1)}) %all-gather.3.cloned.1.call-update) | async-done | bytes 33554448 | tf_op jit(solution)/shard_map/all_gather | solution.py:31
  144.5 17.2 multiply_reduce_fusion.4
  161.7 16.6 multiply_reduce_fusion.5
  178.4 32.2 %psum.21 = f32[2,2,2048]{2,1,0:T(2,128)S(1)} all-reduce(f32[2,2,2048]{2,1,0:T(2,128)S(1)} %pad_maximum_fusion.4), channel_id=1, replica_groups=mesh['tp'=16] {'tp'}, use_global_device_ids=true, to_apply=%region_2.0 | all-reduce | flops 8192 | bytes 65536 | tf_op jit(solution)/shard_map/psum | solution.py:41
  210.6 2.8 multiply_multiply_fusion.1
  215.7 3.9 copy.65
  219.6 3.8 copy.64
  223.4 2.8 multiply_multiply_fusion
  228.4 3.8 copy.67
  232.2 3.7 copy.66
  235.9 10.2 subtract_convert_fusion.1
  246.2 39.6 %fusion.80 = (f32[2,2,2048]{2,1,0:T(2,128)S(1)}, f32[2,2,2048,2048]{2,3,1,0:T(8,128)}) fusion(pred[2048,2048]{0,1:T(8,128)(4,1)} %iota_compare_fusion, bf16[2,2048,2,64]{3,1,2,0:T(8,128)(2,1)} %get-tuple-element.42, bf16[2,2048,2,64]{3,1,2,0:T(8,128)(2,1)} %get-tuple-element.43, bf16[2,2048,2,64]{3,1,2,0:T(8,128)(2,1)} %get-tuple-element.27, ...), kind=kOutput, calls=%fused_computation.111 | convolution fusion | flops 4370466816 | bytes 75530240 | tf_op jit(solution)/shard_map/sub | solution.py:50
  285.8 17.4 convolution_convert_fusion.1
  303.2 39.5 %fusion.43 = bf16[2,2,128,2048]{3,2,1,0:T(8,128)(2,1)} fusion(bf16[2,2048,2,128]{1,3,2,0:T(8,128)(2,1)} %bitcast.130, f32[2,2,2048]{2,1,0:T(2,128)S(1)} %get-tuple-element.54, pred[2048,2048]{0,1:T(8,128)(4,1)} %iota_compare_fusion, bf16[2,2048,2,64]{3,1,2,0:T(8,128)(2,1)} %get-tuple-element.42, bf16[2,2048,2,64]{3,1,2,0:T(8,128)(2,1)} %get-tuple-element.43, ...), kind=kOutput, calls=%fused_computation.70 | convolution fusion | flops 8683268096 | bytes 12615680 | tf_op jit(solution)/shard_map/bhqk,bkhd->bqhd/dot_general | solution.py:52
  342.8 26.6 %fusion.50 = f32[2,2048,4096]{2,1,0:T(8,128)} fusion(bf16[2,2048,256]{1,2,0:T(8,128)(2,1)} %bitcast.132, bf16[256,4096]{1,0:T(8,128)(2,1)} %param.13), kind=kOutput, calls=%fused_computation.77 | convolution fusion | flops 8589934592 | bytes 71303168 | tf_op jit(solution)/shard_map/bse,ed->bsd/dot_general | solution.py:53
  370.0 683.2 %reduce-scatter.3.cloned.1.call-done = f32[2,128,4096]{2,1,0:T(8,128)} async-done(((f32[2,2048,4096]{2,1,0:T(8,128)}), f32[2,128,4096]{2,1,0:T(8,128)}) %reduce-scatter.3.cloned.1.call-update) | async-done | bytes 4194320 | tf_op jit(solution)/shard_map/reduce_scatter | solution.py:54
  1053.2 2.7 multiply_reduce_fusion.3
  1056.6 4.1 fusion.34
  1060.8 3.9 fusion.32
  1064.7 40.0 %fusion.115 = bf16[2,2,2048,2048]{2,3,1,0:T(8,128)(2,1)} fusion(f32[2,2,2048]{2,1,0:T(2,128)S(1)} %get-tuple-element.54, pred[2048,2048]{0,1:T(8,128)(4,1)} %iota_compare_fusion, bf16[2,2048,2,64]{3,1,2,0:T(8,128)(2,1)} %get-tuple-element.42, bf16[2,2048,2,64]{3,1,2,0:T(8,128)(2,1)} %get-tuple-element.43, ...), kind=kOutput, calls=%fused_computation.16.clone.clone.clone.1 | convolution fusion | flops 4387252224 | bytes 41975808 | tf_op jit(solution)/shard_map/sub | solution.py:50
  1104.7 89.8 %all-gather.5.cloned.1.call-done = bf16[2,2048,4096]{2,1,0:T(8,128)(2,1)} async-done(((bf16[2,128,4096]{2,1,0:T(8,128)(2,1)}), bf16[2,2048,4096]{2,1,0:T(8,128)(2,1)}) %all-gather.5.cloned.1.call-update) | async-done | bytes 33554448 | tf_op jit(solution)/shard_map/all_gather | solution.py:64
  1194.4 15.8 convolution_convert_fusion
  1210.3 23.1 fusion.81
  1233.4 84.7 %fusion.37 = f32[2,2048,2,128]{3,1,2,0:T(8,128)} fusion(f32[2,2,2048,2048]{2,3,1,0:T(8,128)} %fusion.81, bf16[2,2048,2,64]{3,1,2,0:T(8,128)(2,1)} %get-tuple-element.42, bf16[2,2048,2,64]{3,1,2,0:T(8,128)(2,1)} %get-tuple-element.43, f32[2,2,2048,2048]{2,3,1,0:T(8,128)} %get-tuple-element.55, f32[2,2,2048]{2,1,0:T(2,128)S(1)} %get-tuple-element.54), kind=kOutput, calls=%fused_computation.68 | convolution fusion | flops 4416612352 | bytes 140541952 | tf_op jit(solution)/shard_map/bhqk,bkhd->bqhd/dot_general | solution.py:70
  1318.1 84.9 %fusion.40 = f32[2,2048,2,128]{3,1,2,0:T(8,128)} fusion(f32[2,2,2048,2048]{2,3,1,0:T(8,128)} %fusion.81, bf16[2,2048,2,64]{3,1,2,0:T(8,128)(2,1)} %get-tuple-element.27, bf16[2,2048,2,64]{3,1,2,0:T(8,128)(2,1)} %get-tuple-element.26, f32[2,2,2048,2048]{2,3,1,0:T(8,128)} %get-tuple-element.55, f32[2,2,2048]{2,1,0:T(2,128)S(1)} %get-tuple-element.54), kind=kOutput, calls=%fused_computation.69 | convolution fusion | flops 4416612352 | bytes 140541952 | tf_op jit(solution)/shard_map/bhqk,bqhd->bkhd/dot_general | solution.py:71
  1403.0 18.9 fusion.46
  1421.9 10.2 multiply_add_fusion
  1432.2 3.1 pad_maximum_fusion.1
  1435.3 5.4 copy.36
  1440.7 6.6 pad_maximum_fusion
  1447.3 5.6 copy.32
  1452.9 7.9 fusion.35
  1460.9 32.8 %all-reduce = (f32[2,2,2048]{2,1,0:T(2,128)S(1)}, bf16[4096]{0:T(1024)(128)(2,1)}) all-reduce(f32[2,2,2048]{2,1,0:T(2,128)S(1)} %pad_maximum_fusion.5, f32[4096]{0:T(1024)S(1)} %copy-done.15), channel_id=1, replica_groups=mesh['tp'=16] {'tp'}, use_global_device_ids=true, to_apply=%region_11.12 | all-reduce | flops 12288 | bytes 90112 | tf_op jit(solution)/shard_map/psum | solution.py:78
  1493.7 4.8 multiply_convert_fusion.2
  1502.4 23.1 fusion.56
  1525.5 26.4 %fusion.52 = f32[2,2048,4096]{2,1,0:T(8,128)} fusion(bf16[2,2048,256]{1,2,0:T(8,128)(2,1)} %multiply_convert_fusion.1, bf16[4096,256]{1,0:T(8,128)(2,1)} %param.11), kind=kOutput, calls=%fused_computation.79 | convolution fusion | flops 8589934592 | bytes 71303168 | tf_op jit(solution)/shard_map/bse,de->bsd/dot_general | solution.py:85
  1551.9 66.3 %add_add_fusion = f32[2,2048,4096]{2,1,0:T(8,128)} fusion(f32[2,2048,4096]{2,1,0:T(8,128)} %fusion.56, f32[2,2048,4096]{2,1,0:T(8,128)} %fusion.52, bf16[2,2048,256]{1,2,0:T(8,128)(2,1)} %bitcast.126, bf16[4096,256]{1,0:T(8,128)(2,1)} %param.12), kind=kOutput, calls=%fused_computation.2 | convolution fusion | flops 8623489024 | bytes 205520896 | tf_op jit(solution)/shard_map/bse,de->bsd/dot_general | solution.py:86
  1618.3 16.8 fusion.27
  1635.1 4.1 copy.43
  1639.2 16.6 fusion.29
  1655.8 4.1 copy.41
  1659.9 16.6 fusion.28
  1676.5 4.1 copy.42
  1680.5 16.8 fusion.24
  1697.4 604.8 %reduce-scatter.5.cloned.1.call-done = f32[2,128,4096]{2,1,0:T(8,128)} async-done(((f32[2,2048,4096]{2,1,0:T(8,128)}), f32[2,128,4096]{2,1,0:T(8,128)}) %reduce-scatter.5.cloned.1.call-update) | async-done | bytes 4194320 | tf_op jit(solution)/shard_map/reduce_scatter | solution.py:87
  2302.2 4.7 fusion.33
  (65 shorter events, 12.2 us)
Async XLA Ops:
  7.2 154.6 %copy-start = (bf16[4096,256]{1,0:T(8,128)(2,1)S(1)}, bf16[4096,256]{1,0:T(8,128)(2,1)}, u32[]{:S(2)}) copy-start(bf16[4096,256]{1,0:T(8,128)(2,1)} %param.10) | copy-start | bytes 6291460
  7.2 137.4 %all-gather.3.cloned.1.call-start = ((), (), s32[]{:S(2)}) async-start(), calls=%async_computation.2 | async-start | bytes 35651584 | tf_op jit(solution)/shard_map/all_gather | solution.py:31
  7.9 1045.3 %reduce-scatter.3.cloned.1.call-start = ((), (), s32[]{:S(2)}) async-start(), calls=%async_computation.3 | async-start | bytes 71303168 | tf_op jit(solution)/shard_map/reduce_scatter | solution.py:54
  8.6 202.0 %copy-start.18 = (f32[256]{0:T(256)}, f32[256]{0:T(256)S(1)}, u32[]{:S(2)}) copy-start(f32[256]{0:T(256)S(1)} %convert_element_type.88) | copy-start | bytes 3076
  9.3 214.1 %copy-start.16 = (f32[256]{0:T(256)}, f32[256]{0:T(256)S(1)}, u32[]{:S(2)}) copy-start(f32[256]{0:T(256)S(1)} %convert_element_type.89) | copy-start | bytes 3076
  14.0 222.0 %copy-start.7 = (f32[2048,64]{1,0:T(8,128)}, f32[2048,64]{1,0:T(8,128)S(1)}, u32[]{:S(2)}) copy-start(f32[2048,64]{1,0:T(8,128)S(1)} %get-tuple-element.48) | copy-start | bytes 1572868
  210.6 2.8 copy-start.13
  210.6 12.7 copy-start.11
  369.3 0.7 copy-start.20
  369.4 825.1 %all-gather.5.cloned.1.call-start = ((), (), s32[]{:S(2)}) async-start(), calls=%async_computation.4 | async-start | bytes 35651584 | tf_op jit(solution)/shard_map/all_gather | solution.py:64
  1053.2 3.4 copy-start.4
  1055.9 4.9 copy-start.5
  1055.9 4.9 copy-start.9
  1064.7 1237.5 %reduce-scatter.5.cloned.1.call-start = ((), (), s32[]{:S(2)}) async-start(), calls=%async_computation.5 | async-start | bytes 71303168 | tf_op jit(solution)/shard_map/reduce_scatter | solution.py:87
  1194.4 15.9 copy-start.10
  1210.3 23.2 %copy-start.1 = (bf16[2,2048,256]{1,2,0:T(8,128)(2,1)}, bf16[2,2048,256]{1,2,0:T(8,128)(2,1)S(1)}, u32[]{:S(2)}) copy-start(bf16[2,2048,256]{1,2,0:T(8,128)(2,1)S(1)} %convolution_convert_fusion) | copy-start | bytes 6291460
  1403.0 18.9 copy-start.8
  1447.3 5.6 copy-start.12
  1447.3 5.6 copy-start.14
  1447.3 5.6 copy-start.17
  1447.3 5.6 copy-start.19
  1452.9 7.9 copy-start.15
  1493.7 4.8 copy-start.2
  1493.7 6.1 copy-start.3
  1498.5 3.9 copy-start.6
Sparse Core Ops, SparseCore 0:
  10.3 134.2 all-gather.2
  369.5 683.6 reduce-scatter.2
  1064.8 129.5 all-gather.4
  1618.4 683.6 reduce-scatter.4
where the time goes:
time: 2320 us; the launch traced here: 2310 us
  waiting for transfers between devices  1500 us (65%)
  matrix products  607 us (26%)
  other arithmetic  76.5 us (3%)
  blocking collectives  65 us (3%)
  local copies, waits for them, and re-layouts  45.7 us (2%)
    reduce_scatter x1, waiting for transfers between devices, local_block(): lax.psum_scatter(attn_part, 'tp', scatter_dimension=1, tiled=True)  683 us
    reduce_scatter x1, waiting for transfers between devices, local_block(): lax.psum_scatter(dx_part, 'tp', scatter_dimension=1, tiled=True) + dy_f  605 us
    all_gather x1, waiting for transfers between devices, local_block(): x_full = lax.all_gather(x_loc, 'tp', axis=1, tiled=True)  127 us
    all_gather x1, waiting for transfers between devices, local_block(): lax.all_gather(d_attn.astype(jnp.bfloat16), 'tp', axis=1, tiled=True)  89.8 us
    dot_general x1, matrix products, local_block(): jnp.einsum('bhqk,bqhd->bkhd', d_scores, q_rot, preferred_element_type=jnp...  84.9 us
    dot_general x1, matrix products, local_block(): jnp.einsum('bhqk,bkhd->bqhd', d_scores, k_rot, preferred_element_type=jnp...  84.7 us
    sub x2, matrix products, local_block(): attn_probs = jax.nn.softmax(jnp.where(causal, scores, -1e+30), axis=-1)  79.6 us
    dot_general x1, matrix products, local_block(): jnp.einsum('bse,de->bsd', d_value, wv_loc, preferred_element_type=jnp.flo...  66.3 us
  transfers between devices with their start and end apart: 4, of which 4 were waited for; matrix products, arithmetic and copies ran while one was open for 6% of the time, Pallas kernels for 0%

commit v1 on v0

v1 whole, which is shorter than its diff:
```python
import functools
import math

import jax
import jax.numpy as jnp
from jax import lax
from jax.experimental import pallas as pl
from jax.experimental.pallas import tpu as pltpu
from jax.sharding import PartitionSpec as P

HEAD_SIZE = 128
ROPE_THETA = 500000.0
NORM_EPS = 1e-6
N_DEV = 16
Q_BLOCK = 256
LOG2E = math.log2(math.e)
ATTN_SCALE = HEAD_SIZE ** -0.5
NT = (((1,), (1,)), ((), ()))
NN = (((1,), (0,)), ((), ()))


def rope_tables(seq_len):
    half_dim = HEAD_SIZE // 2
    inv_freq = 1.0 / (ROPE_THETA ** (jnp.arange(half_dim, dtype=jnp.float32) / half_dim))
    angles = jnp.arange(seq_len, dtype=jnp.float32)[:, None] * inv_freq[None, :]
    cos_t, sin_t = jnp.cos(angles), jnp.sin(angles)
    return jnp.concatenate([cos_t, cos_t], axis=-1), jnp.concatenate([-sin_t, sin_t], axis=-1)


def vmem_spec():
    return pl.BlockSpec(memory_space=pltpu.VMEM)


def sum_kernel(part_ref, out_ref, slots, send_sems, recv_sems):
    me = lax.axis_index('tp')
    copies = []
    for step in range(1, N_DEV):
        peer = lax.rem(me + step, N_DEV)
        copy = pltpu.make_async_remote_copy(
            src_ref=part_ref, dst_ref=slots.at[step], send_sem=send_sems.at[step], recv_sem=recv_sems.at[step],
            device_id=(peer,), device_id_type=pl.DeviceIdType.MESH)
        copy.start()
        copies.append(copy)
    slots[0] = part_ref[...]
    for copy in copies:
        copy.wait()
    total = jnp.zeros(part_ref.shape, jnp.float32)
    for owner in range(N_DEV):
        total = total + slots[lax.rem(me - owner + N_DEV, N_DEV)]
    out_ref[...] = total


def sum_devices(part):
    return pl.pallas_call(
        sum_kernel,
        out_shape=jax.ShapeDtypeStruct(part.shape, jnp.float32),
        in_specs=[vmem_spec()],
        out_specs=vmem_spec(),
        scratch_shapes=[pltpu.VMEM((N_DEV,) + part.shape, jnp.float32),
                        pltpu.SemaphoreType.DMA((N_DEV,)), pltpu.SemaphoreType.DMA((N_DEV,))],
        compiler_params=pltpu.CompilerParams(has_side_effects=True),
        cost_estimate=pl.CostEstimate(flops=int(1e9), bytes_accessed=int(1e6), transcendentals=0),
        name='sum_devices',
    )(part)


def to_tokens_kernel(n_arr, tok, cols, *refs):
    ins, outs = refs[:n_arr], refs[n_arr:-2]
    send_sems, recv_sems = refs[-2:]
    me = lax.axis_index('tp')
    copies = []
    my_cols = pl.ds(pl.multiple_of(me * cols, cols), cols)
    for step in range(1, N_DEV):
        peer = lax.rem(me + step, N_DEV)
        rows = pl.ds(pl.multiple_of(peer * tok, tok), tok)
        for i in range(n_arr):
            copy = pltpu.make_async_remote_copy(
                src_ref=ins[i].at[rows, :], dst_ref=outs[i // 2].at[i % 2, :, my_cols],
                send_sem=send_sems.at[i, step], recv_sem=recv_sems.at[i, step],
                device_id=(peer,), device_id_type=pl.DeviceIdType.MESH)
            copy.start()
            copies.append(copy)
    my_rows = pl.ds(pl.multiple_of(me * tok, tok), tok)
    for i in range(n_arr):
        outs[i // 2][i % 2, :, my_cols] = ins[i][my_rows, :]
    for copy in copies:
        copy.wait()


def to_tokens(*arrs):
    seq_len, cols = arrs[0].shape
    tok = seq_len // N_DEV
    n_arr = len(arrs)
    outs = pl.pallas_call(
        functools.partial(to_tokens_kernel, n_arr, tok, cols),
        out_shape=[jax.ShapeDtypeStruct((2, tok, cols * N_DEV), jnp.bfloat16)] * (n_arr // 2),
        in_specs=[vmem_spec()] * n_arr,
        out_specs=[vmem_spec()] * (n_arr // 2),
        scratch_shapes=[pltpu.SemaphoreType.DMA((n_arr, N_DEV)), pltpu.SemaphoreType.DMA((n_arr, N_DEV))],
        compiler_params=pltpu.CompilerParams(has_side_effects=True),
        cost_estimate=pl.CostEstimate(flops=int(5e9) * n_arr, bytes_accessed=int(4e6) * n_arr, transcendentals=0),
        name='to_tokens',
    )(*arrs)
    return [o.reshape(2 * tok, cols * N_DEV) for o in outs]


def to_heads_kernel(tok, cols, in_ref, out0_ref, out1_ref, send_sems, recv_sems):
    me = lax.axis_index('tp')
    outs = (out0_ref, out1_ref)
    my_rows = pl.ds(pl.multiple_of(me * tok, tok), tok)
    copies = []
    for b in range(2):
        for step in range(1, N_DEV):
            peer = lax.rem(me + step, N_DEV)
            copy = pltpu.make_async_remote_copy(
                src_ref=in_ref.at[b, :, pl.ds(pl.multiple_of(peer * cols, cols), cols)], dst_ref=outs[b].at[my_rows, :],
                send_sem=send_sems.at[b, step], recv_sem=recv_sems.at[b, step],
                device_id=(peer,), device_id_type=pl.DeviceIdType.MESH)
            copy.start()
            copies.append(copy)
    for b in range(2):
        outs[b][my_rows, :] = in_ref[b, :, pl.ds(pl.multiple_of(me * cols, cols), cols)]
    for copy in copies:
        copy.wait()


def to_heads(arr):
    _, tok, width = arr.shape
    cols = width // N_DEV
    return pl.pallas_call(
        functools.partial(to_heads_kernel, tok, cols),
        out_shape=[jax.ShapeDtypeStruct((tok * N_DEV, cols), jnp.bfloat16)] * 2,
        in_specs=[vmem_spec()],
        out_specs=[vmem_spec()] * 2,
        scratch_shapes=[pltpu.SemaphoreType.DMA((2, N_DEV)), pltpu.SemaphoreType.DMA((2, N_DEV))],
        compiler_params=pltpu.CompilerParams(has_side_effects=True),
        cost_estimate=pl.CostEstimate(flops=int(1e10), bytes_accessed=int(8e6), transcendentals=0),
        name='to_heads',
    )(arr)


def causal_tile(scores, first_key_row):
    ext = scores.shape[0]
    diag = scores[first_key_row:, :]
    key_pos = lax.broadcasted_iota(jnp.int32, diag.shape, 0)
    query_pos = lax.broadcasted_iota(jnp.int32, diag.shape, 1)
    diag = jnp.where(key_pos <= query_pos, diag, -1e30)
    if first_key_row == 0:
        return diag
    return jnp.concatenate([scores[:first_key_row, :], diag], axis=0)


def fwd_kernel(q_ref, k_ref, v_ref, iq_ref, ik_ref, gq_ref, gk_ref, cos_ref, sin_ref,
               o_ref, qr_ref, kr_ref, lse_ref, vt_ref):
    seq_len = q_ref.shape[0]
    cos_t, sin_t = cos_ref[...], sin_ref[...]
    for src, inv, gain, dst in ((q_ref, iq_ref, gq_ref, qr_ref), (k_ref, ik_ref, gk_ref, kr_ref)):
        hat = src[...] * inv[...] * gain[...].astype(jnp.float32)
        dst[...] = (hat * cos_t + pltpu.roll(hat, HEAD_SIZE // 2, 1) * sin_t).astype(jnp.bfloat16)
    vt_ref[...] = v_ref[...].astype(jnp.float32).T.astype(jnp.bfloat16)
    for first in range(0, seq_len, Q_BLOCK):
        ext = first + Q_BLOCK
        scores = lax.dot_general(kr_ref[:ext, :], qr_ref[first:ext, :], NT,
                                 preferred_element_type=jnp.float32) * (ATTN_SCALE * LOG2E)
        scores = causal_tile(scores, first)
        top = jnp.max(scores, axis=0, keepdims=True)
        expd = jnp.exp2(scores - top)
        total = jnp.sum(expd, axis=0, keepdims=True)
        probs = (expd * (1.0 / total)).astype(jnp.bfloat16)
        out_t = lax.dot_general(vt_ref[:, :ext], probs, NN, preferred_element_type=jnp.float32)
        o_ref[first:ext, :] = out_t.T.astype(jnp.bfloat16)
        lse_ref[:, first:ext] = top + jnp.log2(total)


def attention_fwd(q_raw, k_raw, v_heads, inv_q, inv_k, gq, gk, cos_t, sin_t):
    seq_len, cols = q_raw.shape
    heads = cols // HEAD_SIZE
    head_spec = pl.BlockSpec((seq_len, HEAD_SIZE), lambda h: (0, h))
    col_spec = pl.BlockSpec((seq_len, 1), lambda h: (0, 0))
    gain_spec = pl.BlockSpec((1, HEAD_SIZE), lambda h: (0, h))
    table_spec = pl.BlockSpec((seq_len, HEAD_SIZE), lambda h: (0, 0))
    lse_spec = pl.BlockSpec((None, 1, seq_len), lambda h: (h, 0, 0))
    return pl.pallas_call(
        fwd_kernel,
        grid=(heads,),
        in_specs=[head_spec, head_spec, head_spec, col_spec, col_spec, gain_spec, gain_spec, table_spec, table_spec],
        out_specs=[head_spec, head_spec, head_spec, lse_spec],
        out_shape=[jax.ShapeDtypeStruct((seq_len, cols), jnp.bfloat16)] * 3
        + [jax.ShapeDtypeStruct((heads, 1, seq_len), jnp.float32)],
        scratch_shapes=[pltpu.VMEM((HEAD_SIZE, seq_len), jnp.bfloat16)],
        compiler_params=pltpu.CompilerParams(dimension_semantics=('arbitrary',), vmem_limit_bytes=56 * 2 ** 20),
        cost_estimate=pl.CostEstimate(flops=int(8e9), bytes_accessed=int(1e7), transcendentals=int(5e6)),
        name='attention_fwd',
    )(q_raw, k_raw, v_heads, inv_q, inv_k, gq, gk, cos_t, sin_t)


def bwd_kernel(q_ref, k_ref, v_ref, do_ref, lse_ref, cos_ref, sin_ref, dq_ref, dk_ref, dv_ref, kt_ref, dva_ref):
    seq_len = q_ref.shape[0]
    kt_ref[...] = k_ref[...].astype(jnp.float32).T.astype(jnp.bfloat16)
    dk_ref[...] = jnp.zeros_like(dk_ref)
    dva_ref[...] = jnp.zeros_like(dva_ref)
    for first in range(0, seq_len, Q_BLOCK):
        ext = first + Q_BLOCK
        q_blk, do_blk = q_ref[first:ext, :], do_ref[first:ext, :]
        scores = lax.dot_general(k_ref[:ext, :], q_blk, NT,
                                 preferred_element_type=jnp.float32) * (ATTN_SCALE * LOG2E)
        scores = causal_tile(scores, first)
        probs = jnp.exp2(scores - lse_ref[:, first:ext])
        d_probs = lax.dot_general(v_ref[:ext, :], do_blk, NT, preferred_element_type=jnp.float32)
        delta = jnp.sum(probs * d_probs, axis=0, keepdims=True)
        d_scores = (probs * (d_probs - delta) * ATTN_SCALE).astype(jnp.bfloat16)
        dva_ref[:ext, :] += lax.dot_general(probs.astype(jnp.bfloat16), do_blk, NN, preferred_element_type=jnp.float32)
        dk_ref[:ext, :] += lax.dot_general(d_scores, q_blk, NN, preferred_element_type=jnp.float32)
        dq_t = lax.dot_general(kt_ref[:, :ext], d_scores, NN, preferred_element_type=jnp.float32)
        dq = dq_t.T
        dq_ref[first:ext, :] = dq * cos_ref[first:ext, :] - pltpu.roll(dq, HEAD_SIZE // 2, 1) * sin_ref[first:ext, :]
    dk = dk_ref[...]
    dk_ref[...] = dk * cos_ref[...] - pltpu.roll(dk, HEAD_SIZE // 2, 1) * sin_ref[...]
    dv_ref[...] = dva_ref[...].astype(jnp.bfloat16)


def attention_bwd(q_rot, k_rot, v_heads, d_heads, lse, cos_t, sin_t):
    seq_len, cols = q_rot.shape
    heads = cols // HEAD_SIZE
    head_spec = pl.BlockSpec((seq_len, HEAD_SIZE), lambda h: (0, h))
    table_spec = pl.BlockSpec((seq_len, HEAD_SIZE), lambda h: (0, 0))
    lse_spec = pl.BlockSpec((None, 1, seq_len), lambda h: (h, 0, 0))
    return pl.pallas_call(
        bwd_kernel,
        grid=(heads,),
        in_specs=[head_spec, head_spec, head_spec, head_spec, lse_spec, table_spec, table_spec],
        out_specs=[head_spec, head_spec, head_spec],
        out_shape=[jax.ShapeDtypeStruct((seq_len, cols), jnp.float32)] * 2
        + [jax.ShapeDtypeStruct((seq_len, cols), jnp.bfloat16)],
        scratch_shapes=[pltpu.VMEM((HEAD_SIZE, seq_len), jnp.bfloat16), pltpu.VMEM((seq_len, HEAD_SIZE), jnp.float32)],
        compiler_params=pltpu.CompilerParams(dimension_semantics=('arbitrary',), vmem_limit_bytes=56 * 2 ** 20),
        cost_estimate=pl.CostEstimate(flops=int(2e10), bytes_accessed=int(1e7), transcendentals=int(5e6)),
        name='attention_bwd',
    )(q_rot, k_rot, v_heads, d_heads, lse, cos_t, sin_t)


def dot_f32(spec, lhs, rhs):
    return jnp.einsum(spec, lhs, rhs, preferred_element_type=jnp.float32)


def after(value, *others):
    return lax.optimization_barrier((value,) + others)[0]


def local_block(x_loc, wq_loc, wk_loc, wv_loc, wo_loc, gq_loc, gk_loc, g_attn, dy_loc):
    batch_size, seq_loc, model_dim = x_loc.shape
    seq_len = seq_loc * N_DEV
    batches = range(batch_size)
    cos_t, sin_t = rope_tables(seq_len)
    gq_row, gk_row = gq_loc[None, :], gk_loc[None, :]
    gq_f, gk_f = gq_row.astype(jnp.float32), gk_row.astype(jnp.float32)

    x_full = [lax.all_gather(x_loc[b], 'tp', axis=0, tiled=True) for b in batches]
    wo_full = lax.all_gather(wo_loc, 'tp', axis=0, tiled=True)
    wq_t, wk_t, wv_t = [lax.all_gather(w.T, 'tp', axis=0, tiled=True) for w in (wq_loc, wk_loc, wv_loc)]

    q_raw, k_raw, v_heads, inv_q, inv_k, saved = [], [], [], [], [], []
    for b in batches:
        q_b, k_b = dot_f32('sd,de->se', x_full[b], wq_loc), dot_f32('sd,de->se', x_full[b], wk_loc)
        part = jnp.stack([jnp.sum(q_b * q_b, axis=-1), jnp.sum(k_b * k_b, axis=-1)])
        v_b = dot_f32('sd,de->se', x_full[b], wv_loc).astype(jnp.bfloat16)
        sums = sum_devices(part.reshape(-1, 128)).reshape(2, seq_len, 1)
        inv = lax.rsqrt(sums / model_dim + NORM_EPS)
        saved.append(attention_fwd(q_b, k_b, v_b, inv[0], inv[1], gq_row, gk_row, cos_t, sin_t))
        q_raw.append(q_b)
        k_raw.append(k_b)
        v_heads.append(v_b)
        inv_q.append(inv[0])
        inv_k.append(inv[1])
    heads_out = [s[0] for s in saved]

    o_loc, = to_tokens(*heads_out)
    attn_loc = dot_f32('te,ed->td', o_loc, wo_full)
    x_f = x_loc.reshape(-1, model_dim).astype(jnp.float32)
    dy_f = dy_loc.reshape(-1, model_dim).astype(jnp.float32)
    post_rms = lax.rsqrt(jnp.mean(attn_loc * attn_loc, axis=-1, keepdims=True) + NORM_EPS)
    normed = attn_loc * post_rms
    ga_f = g_attn.astype(jnp.float32)
    y_loc = (x_f + normed * ga_f).astype(jnp.bfloat16)

    ga_part = jnp.sum(dy_f * normed, axis=0)
    g_normed = dy_f * ga_f
    d_attn = (post_rms * (g_normed - normed * jnp.mean(g_normed * normed, axis=-1, keepdims=True))).astype(jnp.bfloat16)
    d_o_loc = dot_f32('td,ed->te', d_attn, wo_full).astype(jnp.bfloat16)
    d_heads = to_heads(d_o_loc.reshape(batch_size, seq_loc, model_dim))
    d_attn_full = lax.all_gather(d_attn.reshape(batch_size, seq_loc, model_dim), 'tp', axis=1, tiled=True)

    dq_hat, dk_hat, d_value = [], [], []
    for b in batches:
        dq_b, dk_b, dv_b = attention_bwd(saved[b][1], saved[b][2], v_heads[b], d_heads[b], saved[b][3], cos_t, sin_t)
        dq_hat.append(dq_b)
        dk_hat.append(dk_b)
        d_value.append(dv_b)
    grad_wo = sum(dot_f32('se,sd->ed', heads_out[b], d_attn_full[b]) for b in batches)
    grad_gq = sum(jnp.sum(dq_hat[b] * (q_raw[b] * inv_q[b]), axis=0) for b in batches)
    grad_gk = sum(jnp.sum(dk_hat[b] * (k_raw[b] * inv_k[b]), axis=0) for b in batches)
    dots = [jnp.sum(dq_hat[b] * gq_f * (q_raw[b] * inv_q[b]), axis=-1) for b in batches]
    dots += [jnp.sum(dk_hat[b] * gk_f * (k_raw[b] * inv_k[b]), axis=-1) for b in batches]
    sums = sum_devices(jnp.concatenate(dots + [ga_part]).reshape(-1, 128)).reshape(-1)
    unit_dots = (sums[:2 * batch_size * seq_len] / model_dim).reshape(2, batch_size, seq_len, 1)
    grad_ga = sums[2 * batch_size * seq_len:]
    dq_raw = [(inv_q[b] * (dq_hat[b] * gq_f - q_raw[b] * inv_q[b] * unit_dots[0, b])).astype(jnp.bfloat16) for b in batches]
    dk_raw = [(inv_k[b] * (dk_hat[b] * gk_f - k_raw[b] * inv_k[b] * unit_dots[1, b])).astype(jnp.bfloat16) for b in batches]
    dq_loc, dk_loc, dv_loc = to_tokens(*dq_raw, *dk_raw, *d_value)
    grad_wq = sum(dot_f32('sd,se->de', x_full[b], dq_raw[b]) for b in batches)
    grad_wk = sum(dot_f32('sd,se->de', x_full[b], dk_raw[b]) for b in batches)
    grad_wv = sum(dot_f32('sd,se->de', x_full[b], d_value[b]) for b in batches)
    grad_x = (dot_f32('te,ed->td', dq_loc, wq_t) + dot_f32('te,ed->td', dk_loc, wk_t)
              + dot_f32('te,ed->td', dv_loc, wv_t) + dy_f)
    return (y_loc.reshape(x_loc.shape), grad_x.astype(jnp.bfloat16).reshape(x_loc.shape), grad_wq.astype(jnp.bfloat16),
            grad_wk.astype(jnp.bfloat16), grad_wv.astype(jnp.bfloat16), grad_wo.astype(jnp.bfloat16),
            grad_gq.astype(jnp.bfloat16), grad_gk.astype(jnp.bfloat16), grad_ga.astype(jnp.bfloat16))


def solution(mesh):
    act_spec = P(None, 'tp', None)
    col_spec = P(None, 'tp')
    row_spec = P('tp', None)
    vec_spec = P('tp')
    in_specs = (act_spec, col_spec, col_spec, col_spec, row_spec, vec_spec, vec_spec, P(), act_spec)
    out_specs = (act_spec, act_spec, col_spec, col_spec, col_spec, row_spec, vec_spec, vec_spec, P())
    return jax.shard_map(local_block, mesh=mesh, in_specs=in_specs, out_specs=out_specs, check_vma=False)
```

time: 2320 us -> 1160 us (0.50)
  waiting for transfers between devices: 1500 us -> 509 us
  matrix products: 607 us -> 219 us
  Pallas kernels: 0 us -> 347 us
  blocking collectives: 65 us -> 0 us
  other arithmetic: 76.5 us -> 30.2 us
    reduce_scatter x2 -> x0, waiting for transfers between devices: 1290 us -> none  [the longest x1 683 us: local_block(): lax.psum_scatter(attn_part, 'tp', scatter_dimension=1, tiled=True)]
    pallas_call x0 -> x10, Pallas kernels: none -> 347 us  [the longest x2 175 us: to_tokens(): pl.pallas_call(functools.partial(to_tokens_kernel, n_arr, tok, cols), out...]
    dot_general x17 -> x19, matrix products: 527 us -> 219 us  [dot_f32(): return jnp.einsum(spec, lhs, rhs, preferred_element_type=jnp.float32)]
    all_gather x2 -> x7, waiting for transfers between devices: 216 us -> 506 us  [the longest x3 277 us: local_block(): lax.all_gather(w.T, 'tp', axis=0, tiled=True)]
    sub x2 -> x0, matrix products: 79.6 us -> none  [local_block(): attn_probs = jax.nn.softmax(jnp.where(causal, scores, -1e+30), axis=-1)]
    psum x2 -> x0, blocking collectives: 65 us -> none  [the longest x1 32.8 us: local_block(): lax.psum(jnp.stack([jnp.sum(dq_unit * q_unit, axis=-1), jnp.sum(dk_unit *...]
  transfers between devices with their start and end apart: 4 -> 7, of which waited for: 4 -> 6; matrix products, arithmetic and copies ran while one was open for 6% -> 22% of each run, Pallas kernels for 0% -> 30%
where the time goes in v1:
time: 1160 us
  waiting for transfers between devices  509 us (44%)
  Pallas kernels  347 us (30%)
  matrix products  219 us (19%)
  local copies, waits for them, and re-layouts  35.9 us (3%)
  other arithmetic  30.2 us (3%)
  between operations  15.1 us (1%)
    all_gather x3, waiting for transfers between devices, local_block(): lax.all_gather(w.T, 'tp', axis=0, tiled=True)  277 us
    dot_general x19, matrix products, dot_f32(): return jnp.einsum(spec, lhs, rhs, preferred_element_type=jnp.float32)  219 us
    pallas_call x2, Pallas kernels, to_tokens(): pl.pallas_call(functools.partial(to_tokens_kernel, n_arr, tok, cols), out...  175 us
    all_gather x1, waiting for transfers between devices, local_block(): lax.all_gather(d_attn.reshape(batch_size, seq_loc, model_dim), 'tp', axis...  116 us
    all_gather x2, waiting for transfers between devices, local_block(): lax.all_gather(x_loc[b], 'tp', axis=0, tiled=True)  105 us
    pallas_call x1, Pallas kernels, to_heads(): pl.pallas_call(functools.partial(to_heads_kernel, tok, cols), out_shape=[...  47.2 us
    pallas_call x3, Pallas kernels, sum_devices(): pl.pallas_call(sum_kernel, out_shape=jax.ShapeDtypeStruct(part.shape, jnp...  46.8 us
    pallas_call x2, Pallas kernels, attention_bwd(): pl.pallas_call(bwd_kernel, grid=(heads,), in_specs=[head_spec, head_spec,...  40.3 us
  transfers between devices with their start and end apart: 7, of which 6 were waited for; matrix products, arithmetic and copies ran while one was open for 22% of the time, Pallas kernels for 30%

profile of v1, /device:TPU:0, one launch (start us, length us, event | category | flops | bytes accessed | tf_op | source)
XLA Modules:
  0.0 1157.2 jit_solution(17466658879153925407)
XLA Ops:
  7.2 3.1 fusion.73
  14.8 3.9 fusion.71
  21.4 68.4 %all-gather.20.cloned.1.call-done = bf16[1,2048,4096]{2,1,0:T(8,128)(2,1)} async-done(((bf16[1,128,4096]{2,1,0:T(8,128)(2,1)}), bf16[1,2048,4096]{2,1,0:T(8,128)(2,1)}) %all-gather.20.cloned.1.call-update) | async-done | bytes 16777232 | tf_op jit(solution)/shard_map/all_gather | solution.py:258
  89.7 9.9 multiply_reduce_fusion.12
  99.6 2.9 copy.31.q_ref
  102.5 12.2 %multiply_reduce_fusion.11 = (f32[2048]{0:T(1024)S(1)}, f32[2048,256]{0,1:T(8,128)}) fusion(bf16[4096,256]{1,0:T(8,128)(2,1)} %param.11, bf16[1,2048,4096]{2,1,0:T(8,128)(2,1)} %all-gather.20.cloned.1.call-done), kind=kOutput, calls=%fused_computation.71 | convolution fusion | flops 4296013824 | bytes 20979712 | tf_op jit(solution)/shard_map/sd,de->se/dot_general | solution.py:243
  114.7 2.9 copy.32.k_ref
  118.2 12.5 %sum_devices.3 = f32[32,128]{1,0:T(8,128)} custom-call(f32[32,128]{1,0:T(8,128)} %reshape.169.part_ref), custom_call_target="tpu_custom_call" | custom-call | flops 1000000000 | bytes 1000000 | tf_op jit(solution)/shard_map/sum_devices/pallas_call | solution.py:54
  134.8 36.7 %all-gather.22.cloned.1.call-done = bf16[1,2048,4096]{2,1,0:T(8,128)(2,1)} async-done(((bf16[1,128,4096]{2,1,0:T(8,128)(2,1)}), bf16[1,2048,4096]{2,1,0:T(8,128)(2,1)}) %all-gather.22.cloned.1.call-update) | async-done | bytes 16777232 | tf_op jit(solution)/shard_map/all_gather | solution.py:258
  171.5 9.9 multiply_reduce_fusion.10
  181.4 3.0 copy.35.q_ref
  184.5 9.7 multiply_reduce_fusion.9
  194.2 2.9 copy.36.k_ref
  197.7 10.5 sum_devices.4
  211.7 9.7 fusion.63.v_ref
  221.4 18.9 %attention_fwd.2 = (bf16[2048,256]{1,0:T(8,128)(2,1)}, bf16[2048,256]{1,0:T(8,128)(2,1)}, bf16[2048,256]{1,0:T(8,128)(2,1)}, f32[2,1,2048]{2,1,0:T(1,128)}) custom-call(f32[2048,256]{1,0:T(8,128)} %copy.31.q_ref, f32[2048,256]{1,0:T(8,128)} %copy.32.k_ref, bf16[2048,256]{1,0:T(8,128)(2,1)} %fusion.63.v_ref, f32[2048,1]{1,0:T(8,128)} %copy.33.iq_ref, ...), custom_call_target="tpu_custom_call" | custom-call | flops 8000000000 | bytes 10000000 | tf_op jit(solution)/shard_map/attention_fwd/pallas_call | solution.py:183
  240.3 9.2 fusion.66.v_ref
  249.5 19.0 %attention_fwd.3 = (bf16[2048,256]{1,0:T(8,128)(2,1)}, bf16[2048,256]{1,0:T(8,128)(2,1)}, bf16[2048,256]{1,0:T(8,128)(2,1)}, f32[2,1,2048]{2,1,0:T(1,128)}) custom-call(f32[2048,256]{1,0:T(8,128)} %copy.35.q_ref, f32[2048,256]{1,0:T(8,128)} %copy.36.k_ref, bf16[2048,256]{1,0:T(8,128)(2,1)} %fusion.66.v_ref, f32[2048,1]{1,0:T(8,128)} %copy.37.iq_ref, ...), custom_call_target="tpu_custom_call" | custom-call | flops 8000000000 | bytes 10000000 | tf_op jit(solution)/shard_map/attention_fwd/pallas_call | solution.py:183
  268.5 52.1 %to_tokens.2 = bf16[2,128,4096]{2,1,0:T(8,128)(2,1)} custom-call(bf16[2048,256]{1,0:T(8,128)(2,1)} %get-tuple-element.28.refs_0_, bf16[2048,256]{1,0:T(8,128)(2,1)} %get-tuple-element.29.refs_1_), custom_call_target="tpu_custom_call" | custom-call | flops 10000000000 | bytes 8000000 | tf_op jit(solution)/shard_map/to_tokens/pallas_call | solution.py:94
  320.7 8.0 all-gather.10.cloned.1.call-done
  328.7 16.0 %multiply_reduce_fusion = (f32[256]{0:T(256)S(1)}, f32[256,4096]{1,0:T(8,128)S(1)}) fusion(bf16[256,4096]{1,0:T(8,128)(2,1)} %bitcast.165, bf16[4096,4096]{1,0:T(8,128)(2,1)} %all-gather.10.cloned.1.call-done), kind=kOutput, calls=%fused_computation.54 | convolution fusion | flops 8592031744 | bytes 39846912 | tf_op jit(solution)/shard_map/te,ed->td/dot_general | solution.py:243
  346.5 4.2 fusion.60
  352.3 15.8 %convolution_convert_fusion = bf16[256,4096]{1,0:T(8,128)(2,1)} fusion(bf16[256,4096]{1,0:T(8,128)(2,1)S(1)} %copy-done.6, bf16[4096,4096]{1,0:T(8,128)(2,1)} %all-gather.10.cloned.1.call-done), kind=kOutput, calls=%fused_computation.42 | convolution fusion | flops 8590983168 | bytes 37748736 | tf_op jit(solution)/shard_map/td,ed->te/dot_general | solution.py:243
  368.1 47.2 %to_heads.1 = (bf16[2048,256]{1,0:T(8,128)(2,1)}, bf16[2048,256]{1,0:T(8,128)(2,1)}) custom-call(bf16[2,128,4096]{2,1,0:T(8,128)(2,1)} %bitcast.166), custom_call_target="tpu_custom_call" | custom-call | flops 10000000000 | bytes 8000000 | tf_op jit(solution)/shard_map/to_heads/pallas_call | solution.py:130
  415.2 20.0 %attention_bwd.3 = (f32[2048,256]{1,0:T(8,128)}, f32[2048,256]{1,0:T(8,128)}, bf16[2048,256]{1,0:T(8,128)(2,1)}) custom-call(bf16[2048,256]{1,0:T(8,128)(2,1)} %get-tuple-element.35.q_ref, bf16[2048,256]{1,0:T(8,128)(2,1)} %get-tuple-element.36.k_ref, bf16[2048,256]{1,0:T(8,128)(2,1)} %fusion.66.v_ref, bf16[2048,256]{1,0:T(8,128)(2,1)} %get-tuple-element.37.do_ref, ...), custom_call_target="tpu_custom_call" | custom-call | flops 20000000000 | bytes 10000000 | tf_op jit(solution)/shard_map/attention_bwd/pallas_call | solution.py:228
  435.2 20.4 %attention_bwd.2 = (f32[2048,256]{1,0:T(8,128)}, f32[2048,256]{1,0:T(8,128)}, bf16[2048,256]{1,0:T(8,128)(2,1)}) custom-call(bf16[2048,256]{1,0:T(8,128)(2,1)} %get-tuple-element.30.q_ref, bf16[2048,256]{1,0:T(8,128)(2,1)} %get-tuple-element.31.k_ref, bf16[2048,256]{1,0:T(8,128)(2,1)} %fusion.63.v_ref, bf16[2048,256]{1,0:T(8,128)(2,1)} %get-tuple-element.32.do_ref, ...), custom_call_target="tpu_custom_call" | custom-call | flops 20000000000 | bytes 10000000 | tf_op jit(solution)/shard_map/attention_bwd/pallas_call | solution.py:228
  455.6 5.7 multiply_reduce_fusion.1
  462.0 23.8 %sum_devices.5 = f32[96,128]{1,0:T(8,128)} custom-call(f32[96,128]{1,0:T(8,128)} %bitcast.160), custom_call_target="tpu_custom_call" | custom-call | flops 1000000000 | bytes 1000000 | tf_op jit(solution)/shard_map/sum_devices/pallas_call | solution.py:54
  486.7 4.4 multiply_convert_fusion.2
  491.1 11.4 fusion.6
  502.6 7.3 fusion.49
  509.9 4.1 copy.43
  513.9 4.4 multiply_convert_fusion
  518.3 8.9 fusion.4
  527.3 6.0 fusion.52
  533.3 2.5 copy.44
  535.7 8.2 fusion.2
  544.0 10.7 fusion.55
  554.7 2.5 copy.45
  559.5 122.6 %to_tokens.3 = (bf16[2,128,4096]{2,1,0:T(8,128)(2,1)}, bf16[2,128,4096]{2,1,0:T(8,128)(2,1)}, bf16[2,128,4096]{2,1,0:T(8,128)(2,1)}) custom-call(bf16[2048,256]{1,0:T(8,128)(2,1)} %copy-done.8, bf16[2048,256]{1,0:T(8,128)(2,1)} %copy-done.7, bf16[2048,256]{1,0:T(8,128)(2,1)} %get-tuple-element.92.refs_2_, bf16[2048,256]{1,0:T(8,128)(2,1)} %copy-done.9, ...), custom_call_target="tpu_custom_call" | custom-call | flops 30000001024 | bytes 24000000 | tf_op jit(solution)/shard_map/to_tokens/pallas_call | solution.py:94
  682.1 17.7 %fusion.75 = f32[256,4096]{1,0:T(8,128)} fusion(bf16[256,4096]{1,0:T(8,128)(2,1)} %bitcast.164, bf16[4096,4096]{0,1:T(8,128)(2,1)} %all-gather.12.cloned.1.call-done), kind=kOutput, calls=%fused_computation.102 | convolution fusion | flops 8589934592 | bytes 39845888 | tf_op jit(solution)/shard_map/te,ed->td/dot_general | solution.py:243
  699.8 104.3 %all-gather.14.cloned.1.call-done = bf16[4096,4096]{0,1:T(8,128)(2,1)} async-done(((bf16[256,4096]{0,1:T(8,128)(2,1)}), bf16[4096,4096]{0,1:T(8,128)(2,1)}) %all-gather.14.cloned.1.call-update) | async-done | bytes 33554448 | tf_op jit(solution)/shard_map/all_gather | solution.py:260
  804.1 18.8 %convolution_add_fusion.1 = f32[256,4096]{1,0:T(8,128)} fusion(f32[256,4096]{1,0:T(8,128)} %fusion.75, bf16[256,4096]{1,0:T(8,128)(2,1)} %bitcast.163, bf16[4096,4096]{0,1:T(8,128)(2,1)} %all-gather.14.cloned.1.call-done), kind=kOutput, calls=%fused_computation.36 | convolution fusion | flops 8590983168 | bytes 44040192 | tf_op jit(solution)/shard_map/te,ed->td/dot_general | solution.py:243
  822.9 172.5 %all-gather.16.cloned.1.call-done = bf16[4096,4096]{0,1:T(8,128)(2,1)} async-done(((bf16[256,4096]{0,1:T(8,128)(2,1)}), bf16[4096,4096]{0,1:T(8,128)(2,1)}) %all-gather.16.cloned.1.call-update) | async-done | bytes 33554448 | tf_op jit(solution)/shard_map/all_gather | solution.py:260
  995.4 17.8 %fusion.46 = bf16[256,4096]{1,0:T(8,128)(2,1)} fusion(bf16[256,4096]{1,0:T(8,128)(2,1)S(1)} %bitcast.142, f32[256,4096]{1,0:T(8,128)} %convolution_add_fusion.1, bf16[256,4096]{1,0:T(8,128)(2,1)} %bitcast.162, bf16[4096,4096]{0,1:T(8,128)(2,1)} %all-gather.16.cloned.1.call-done), kind=kOutput, calls=%fused_computation.41 | convolution fusion | flops 8594128896 | bytes 44040192 | tf_op jit(solution)/shard_map/te,ed->td/dot_general | solution.py:243
  1013.2 116.5 %all-gather.18.cloned.1.call-done = bf16[2,2048,4096]{2,1,0:T(8,128)(2,1)} async-done(((bf16[2,128,4096]{2,1,0:T(8,128)(2,1)}), bf16[2,2048,4096]{2,1,0:T(8,128)(2,1)}) %all-gather.18.cloned.1.call-update) | async-done | bytes 33554448 | tf_op jit(solution)/shard_map/all_gather | solution.py:291
  1129.7 8.4 fusion
  1138.1 11.9 %fusion.45 = bf16[256,4096]{1,0:T(8,128)(2,1)} fusion(f32[256,4096]{1,0:T(8,128)S(1)} %fusion, bf16[2048,256]{1,0:T(8,128)(2,1)S(1)} %copy-done.22, bf16[2,2048,4096]{2,1,0:T(8,128)(2,1)} %all-gather.18.cloned.1.call-done), kind=kOutput, calls=%fused_computation.40 | convolution fusion | flops 4297064448 | bytes 24117248 | tf_op jit(solution)/shard_map/se,sd->ed/dot_general | solution.py:243
  (113 shorter events, 23.2 us)
Async XLA Ops:
  7.2 82.6 %all-gather.20.cloned.1.call-start = ((), (), s32[]{:S(2)}) async-start(), calls=%async_computation.5 | async-start | bytes 17825792 | tf_op jit(solution)/shard_map/all_gather | solution.py:258
  10.3 161.2 %all-gather.22.cloned.1.call-start = ((), (), s32[]{:S(2)}) async-start(), calls=%async_computation.6 | async-start | bytes 17825792 | tf_op jit(solution)/shard_map/all_gather | solution.py:258
  11.1 317.6 %all-gather.10.cloned.1.call-start = ((), (), s32[]{:S(2)}) async-start(), calls=%async_computation | async-start | bytes 35651584 | tf_op jit(solution)/shard_map/all_gather | solution.py:259
  11.8 670.3 %all-gather.12.cloned.1.call-start = ((), (), s32[]{:S(2)}) async-start(), calls=%async_computation.1 | async-start | bytes 35651584 | tf_op jit(solution)/shard_map/all_gather | solution.py:260
  12.4 791.7 %all-gather.14.cloned.1.call-start = ((), (), s32[]{:S(2)}) async-start(), calls=%async_computation.2 | async-start | bytes 35651584 | tf_op jit(solution)/shard_map/all_gather | solution.py:260
  12.4 1.2 copy-start.20
  12.4 1.8 copy-start.19
  12.5 2.3 copy-start.17
  13.0 982.4 %all-gather.16.cloned.1.call-start = ((), (), s32[]{:S(2)}) async-start(), calls=%async_computation.3 | async-start | bytes 35651584 | tf_op jit(solution)/shard_map/all_gather | solution.py:260
  13.6 1116.1 %all-gather.18.cloned.1.call-start = ((), (), s32[]{:S(2)}) async-start(), calls=%async_computation.4 | async-start | bytes 35651584 | tf_op jit(solution)/shard_map/all_gather | solution.py:291
  20.0 69.7 %copy-start.10 = (bf16[4096,256]{1,0:T(8,128)(2,1)S(1)}, bf16[4096,256]{1,0:T(8,128)(2,1)}, u32[]{:S(2)}) copy-start(bf16[4096,256]{1,0:T(8,128)(2,1)} %param.10) | copy-start | bytes 6291460
  181.4 3.0 copy-start.11
  197.7 14.0 %copy-start.12 = (bf16[4096,256]{1,0:T(8,128)(2,1)S(1)}, bf16[4096,256]{1,0:T(8,128)(2,1)}, u32[]{:S(2)}) copy-start(bf16[4096,256]{1,0:T(8,128)(2,1)} %param.12) | copy-start | bytes 6291460
  328.7 16.1 %copy-start.4 = (bf16[2,128,4096]{2,1,0:T(8,128)(2,1)S(1)}, bf16[2,128,4096]{2,1,0:T(8,128)(2,1)}, u32[]{:S(2)}) copy-start(bf16[2,128,4096]{2,1,0:T(8,128)(2,1)} %param.17) | copy-start | bytes 6291460
  344.8 1.8 copy-start.3
  350.7 1.6 copy-start.6
  435.2 20.4 %copy-start = (f32[2048,256]{1,0:T(8,128)S(1)}, f32[2048,256]{1,0:T(8,128)}, u32[]{:S(2)}) copy-start(f32[2048,256]{1,0:T(8,128)} %copy.32.k_ref) | copy-start | bytes 6291460
  435.2 20.4 %copy-start.1 = (f32[2048,256]{1,0:T(8,128)S(1)}, f32[2048,256]{1,0:T(8,128)}, u32[]{:S(2)}) copy-start(f32[2048,256]{1,0:T(8,128)} %copy.31.q_ref) | copy-start | bytes 6291460
  435.2 20.4 %copy-start.2 = (f32[2048,256]{1,0:T(8,128)S(1)}, f32[2048,256]{1,0:T(8,128)}, u32[]{:S(2)}) copy-start(f32[2048,256]{1,0:T(8,128)} %copy.36.k_ref) | copy-start | bytes 6291460
  435.2 20.4 %copy-start.15 = (f32[2048]{0:T(1024)S(1)}, f32[2048]{0:T(1024)}, u32[]{:S(2)}) copy-start(f32[2048]{0:T(1024)} %get-tuple-element.87) | copy-start | bytes 24580
  435.2 20.4 %copy-start.16 = (f32[2048]{0:T(1024)S(1)}, f32[2048]{0:T(1024)}, u32[]{:S(2)}) copy-start(f32[2048]{0:T(1024)} %get-tuple-element.88) | copy-start | bytes 24580
  461.4 0.6 copy-start.18
  486.6 15.9 %slice-start = ((s8[16777216]{0:T(1024)(128)(4,1)}), s8[4194304]{0:T(1024)(128)(4,1)S(1)}, s32[]{:S(2)}) async-start(s8[16777216]{0:T(1024)(128)(4,1)} %bitcast.138), calls=%async_computation.7 | async-start | bytes 8388608
  486.7 15.9 %slice-start.1 = ((s8[16777216]{0:T(1024)(128)(4,1)}), s8[4194304]{0:T(1024)(128)(4,1)S(1)}, s32[]{:S(2)}) async-start(s8[16777216]{0:T(1024)(128)(4,1)} %bitcast.138), calls=%async_computation.8 | async-start | bytes 8388608
  491.0 11.5 copy-start.7
  491.0 11.5 copy-start.8
  491.1 11.5 slice-start.2
  491.1 11.5 slice-start.3
  513.9 13.3 %slice-start.4 = ((s8[16777216]{0:T(1024)(128)(4,1)}), s8[4194304]{0:T(1024)(128)(4,1)S(1)}, s32[]{:S(2)}) async-start(s8[16777216]{0:T(1024)(128)(4,1)} %bitcast.140), calls=%async_computation.11 | async-start | bytes 8388608
  513.9 13.3 %slice-start.5 = ((s8[16777216]{0:T(1024)(128)(4,1)}), s8[4194304]{0:T(1024)(128)(4,1)S(1)}, s32[]{:S(2)}) async-start(s8[16777216]{0:T(1024)(128)(4,1)} %bitcast.140), calls=%async_computation.12 | async-start | bytes 8388608
  518.3 8.9 copy-start.9
  518.3 8.9 slice-start.6
  518.3 9.0 slice-start.7
  533.3 2.5 copy-start.13
  535.7 8.2 copy-start.14
  804.1 191.3 %copy-start.5 = (bf16[2,128,4096]{2,1,0:T(8,128)(2,1)S(1)}, bf16[2,128,4096]{2,1,0:T(8,128)(2,1)}, u32[]{:S(2)}) copy-start(bf16[2,128,4096]{2,1,0:T(8,128)(2,1)} %param.17) | copy-start | bytes 6291460
  995.4 134.3 %copy-start.21 = (bf16[2048,256]{1,0:T(8,128)(2,1)S(1)}, bf16[2048,256]{1,0:T(8,128)(2,1)}, u32[]{:S(2)}) copy-start(bf16[2048,256]{1,0:T(8,128)(2,1)} %get-tuple-element.29.refs_1_) | copy-start | bytes 3145732
  1013.2 124.9 %copy-start.22 = (bf16[2048,256]{1,0:T(8,128)(2,1)S(1)}, bf16[2048,256]{1,0:T(8,128)(2,1)}, u32[]{:S(2)}) copy-start(bf16[2048,256]{1,0:T(8,128)(2,1)} %get-tuple-element.28.refs_0_) | copy-start | bytes 3145732
Sparse Core Ops, SparseCore 0:
  10.8 78.8 all-gather.19
  92.5 78.9 all-gather.21
  173.8 154.8 all-gather.9
  330.8 220.2 all-gather.11
  553.1 250.9 all-gather.13
  806.2 189.2 all-gather.15
  998.3 131.3 all-gather.17

commit v2 on v1

--- a/solution.py
+++ b/solution.py
@@ -7,6 +7,7 @@
 from jax.experimental import pallas as pl
 from jax.experimental.pallas import tpu as pltpu
 from jax.sharding import PartitionSpec as P
+
 
 HEAD_SIZE = 128
 ROPE_THETA = 500000.0
@@ -140,7 +141,6 @@
 
 
 def causal_tile(scores, first_key_row):
-    ext = scores.shape[0]
     diag = scores[first_key_row:, :]
     key_pos = lax.broadcasted_iota(jnp.int32, diag.shape, 0)
     query_pos = lax.broadcasted_iota(jnp.int32, diag.shape, 1)
@@ -239,6 +239,62 @@
     )(q_rot, k_rot, v_heads, d_heads, lse, cos_t, sin_t)
 
 
+COLUMN_PARTS = ((0, 1408), (1408, 2816), (2816, 4096))
+AXIS_ORDERS = ((0, 1, 2), (1, 2, 0), (2, 0, 1))
+
+
+def by_distance_kernel(me_ref, dq_ref, dk_ref, dv_ref, out_ref):
+    cols = dq_ref.shape[-1]
+    for i, ref in enumerate((dq_ref, dk_ref, dv_ref)):
+        out_ref[:, i * cols:(i + 1) * cols] = ref[...]
+
+
+def by_distance(dq, dk, dv):
+    seq_len, cols = dq.shape
+    tok = seq_len // N_DEV
+    in_spec = pl.BlockSpec((tok, cols), lambda i, me: (((i % 8) * 2 + i // 8) ^ me[0], 0))
+    out = pl.pallas_call(
+        by_distance_kernel,
+        grid_spec=pltpu.PrefetchScalarGridSpec(
+            num_scalar_prefetch=1, grid=(N_DEV,), in_specs=[in_spec] * 3,
+            out_specs=pl.BlockSpec((tok, 3 * cols), lambda i, me: (i, 0))),
+        out_shape=jax.ShapeDtypeStruct((seq_len, 3 * cols), jnp.bfloat16),
+        cost_estimate=pl.CostEstimate(flops=int(1e9), bytes_accessed=int(6e6), transcendentals=0),
+        name='by_distance',
+    )(lax.axis_index('tp').astype(jnp.int32).reshape(1), dq, dk, dv)
+    return out[seq_len // 2:], out[:seq_len // 2]
+
+
+def flip(value, bit):
+    return lax.ppermute(value, 'tp', [(i, i ^ bit) for i in range(N_DEV)])
+
+
+def start_sums(far, near):
+    shape = (2, 2, 2, near[0].shape[0] // 8)
+    return [[n.reshape(shape + n.shape[1:]), flip(f, 1).reshape(shape + n.shape[1:])] for f, n in zip(far, near)]
+
+
+def cross_axis(sums, stage):
+    aways, kept = [], []
+    for pieces, order in zip(sums, AXIS_ORDERS):
+        axis = order[stage]
+        away = sum(lax.slice_in_dim(p, 1, 2, axis=axis) for p in pieces)
+        aways.append(away)
+        came = flip(away, 8 >> axis)
+        kept.append([sum(lax.slice_in_dim(p, 0, 1, axis=axis) for p in pieces), came])
+    return kept, aways
+
+
+def sums_after(sums, gate):
+    flat = lax.optimization_barrier(tuple(p for pieces in sums for p in pieces) + tuple(gate))
+    size = len(sums[0])
+    return [list(flat[i * size:(i + 1) * size]) for i in range(len(sums))]
+
+
+def finish_sums(sums):
+    return jnp.concatenate([sum(pieces)[0, 0, 0] for pieces in sums], axis=-1)
+
+
 def dot_f32(spec, lhs, rhs):
     return jnp.einsum(spec, lhs, rhs, preferred_element_type=jnp.float32)
 
@@ -257,14 +313,15 @@
 
     x_full = [lax.all_gather(x_loc[b], 'tp', axis=0, tiled=True) for b in batches]
     wo_full = lax.all_gather(wo_loc, 'tp', axis=0, tiled=True)
-    wq_t, wk_t, wv_t = [lax.all_gather(w.T, 'tp', axis=0, tiled=True) for w in (wq_loc, wk_loc, wv_loc)]
+    w_cat = jnp.concatenate([wq_loc, wk_loc, wv_loc], axis=1)
 
     q_raw, k_raw, v_heads, inv_q, inv_k, saved = [], [], [], [], [], []
     for b in batches:
+        x_full[b] = after(x_full[b], saved[b - 1][0] if b else w_cat)
         q_b, k_b = dot_f32('sd,de->se', x_full[b], wq_loc), dot_f32('sd,de->se', x_full[b], wk_loc)
         part = jnp.stack([jnp.sum(q_b * q_b, axis=-1), jnp.sum(k_b * k_b, axis=-1)])
         v_b = dot_f32('sd,de->se', x_full[b], wv_loc).astype(jnp.bfloat16)
-        sums = sum_devices(part.reshape(-1, 128)).reshape(2, seq_len, 1)
+        sums = sum_devices(after(part.reshape(-1, 128), v_b)).reshape(2, seq_len, 1)
         inv = lax.rsqrt(sums / model_dim + NORM_EPS)
         saved.append(attention_fwd(q_b, k_b, v_b, inv[0], inv[1], gq_row, gk_row, cos_t, sin_t))
         q_raw.append(q_b)
@@ -290,30 +347,45 @@
     d_heads = to_heads(d_o_loc.reshape(batch_size, seq_loc, model_dim))
     d_attn_full = lax.all_gather(d_attn.reshape(batch_size, seq_loc, model_dim), 'tp', axis=1, tiled=True)
 
-    dq_hat, dk_hat, d_value = [], [], []
+    dq_raw, dk_raw, d_value, dx_sums, gate = [], [], [], [], []
+    grad_gq, grad_gk = 0.0, 0.0
     for b in batches:
-        dq_b, dk_b, dv_b = attention_bwd(saved[b][1], saved[b][2], v_heads[b], d_heads[b], saved[b][3], cos_t, sin_t)
-        dq_hat.append(dq_b)
-        dk_hat.append(dk_b)
+        dq_b, dk_b, dv_b = attention_bwd(saved[b][1], saved[b][2], v_heads[b], after(d_heads[b], *gate),
+                                         saved[b][3], cos_t, sin_t)
+        q_unit, k_unit = q_raw[b] * inv_q[b], k_raw[b] * inv_k[b]
+        dq_unit, dk_unit = dq_b * gq_f, dk_b * gk_f
+        grad_gq += jnp.sum(dq_b * q_unit, axis=0)
+        grad_gk += jnp.sum(dk_b * k_unit, axis=0)
+        parts = [jnp.sum(dq_unit * q_unit, axis=-1), jnp.sum(dk_unit * k_unit, axis=-1)]
+        if b == 0:
+            parts.append(ga_part)
+        sums = sum_devices(jnp.concatenate(parts).reshape(-1, 128)).reshape(-1)
+        if b == 0:
+            grad_ga = sums[2 * seq_len:]
+        unit_dots = (sums[:2 * seq_len] / model_dim).reshape(2, seq_len, 1)
+        dq_raw.append((inv_q[b] * (dq_unit - q_unit * unit_dots[0])).astype(jnp.bfloat16))
+        dk_raw.append((inv_k[b] * (dk_unit - k_unit * unit_dots[1])).astype(jnp.bfloat16))
         d_value.append(dv_b)
-    grad_wo = sum(dot_f32('se,sd->ed', heads_out[b], d_attn_full[b]) for b in batches)
-    grad_gq = sum(jnp.sum(dq_hat[b] * (q_raw[b] * inv_q[b]), axis=0) for b in batches)
-    grad_gk = sum(jnp.sum(dk_hat[b] * (k_raw[b] * inv_k[b]), axis=0) for b in batches)
-    dots = [jnp.sum(dq_hat[b] * gq_f * (q_raw[b] * inv_q[b]), axis=-1) for b in batches]
-    dots += [jnp.sum(dk_hat[b] * gk_f * (k_raw[b] * inv_k[b]), axis=-1) for b in batches]
-    sums = sum_devices(jnp.concatenate(dots + [ga_part]).reshape(-1, 128)).reshape(-1)
-    unit_dots = (sums[:2 * batch_size * seq_len] / model_dim).reshape(2, batch_size, seq_len, 1)
-    grad_ga = sums[2 * batch_size * seq_len:]
-    dq_raw = [(inv_q[b] * (dq_hat[b] * gq_f - q_raw[b] * inv_q[b] * unit_dots[0, b])).astype(jnp.bfloat16) for b in batches]
-    dk_raw = [(inv_k[b] * (dk_hat[b] * gk_f - k_raw[b] * inv_k[b] * unit_dots[1, b])).astype(jnp.bfloat16) for b in batches]
-    dq_loc, dk_loc, dv_loc = to_tokens(*dq_raw, *dk_raw, *d_value)
-    grad_wq = sum(dot_f32('sd,se->de', x_full[b], dq_raw[b]) for b in batches)
-    grad_wk = sum(dot_f32('sd,se->de', x_full[b], dk_raw[b]) for b in batches)
-    grad_wv = sum(dot_f32('sd,se->de', x_full[b], d_value[b]) for b in batches)
-    grad_x = (dot_f32('te,ed->td', dq_loc, wq_t) + dot_f32('te,ed->td', dk_loc, wk_t)
-              + dot_f32('te,ed->td', dv_loc, wv_t) + dy_f)
-    return (y_loc.reshape(x_loc.shape), grad_x.astype(jnp.bfloat16).reshape(x_loc.shape), grad_wq.astype(jnp.bfloat16),
-            grad_wk.astype(jnp.bfloat16), grad_wv.astype(jnp.bfloat16), grad_wo.astype(jnp.bfloat16),
+        far, near = by_distance(dq_raw[b], dk_raw[b], dv_b)
+        far_parts = [dot_f32('te,de->td', far, w_cat[lo:hi]) for lo, hi in COLUMN_PARTS]
+        near_parts = [dot_f32('te,de->td', near, w_cat[lo:hi]) for lo, hi in COLUMN_PARTS]
+        sums_b = start_sums(far_parts, near_parts)
+        if b == 0:
+            sums_b, gate = cross_axis(sums_b, 0)
+        dx_sums.append(sums_b)
+    dx_sums[0], gate = cross_axis(dx_sums[0], 1)
+    dx_sums[1], gate = cross_axis(sums_after(dx_sums[1], gate), 0)
+    first_grads = [dot_f32('sd,se->de', after(x_full[0], *gate), cot[0]) for cot in (dq_raw, dk_raw, d_value)]
+    x_last = after(x_full[1], *first_grads)
+    weight_grads = [(g + dot_f32('sd,se->de', x_last, cot[1])).astype(jnp.bfloat16)
+                    for g, cot in zip(first_grads, (dq_raw, dk_raw, d_value))]
+    d_attn_full = after(d_attn_full, *weight_grads)
+    grad_wo = sum(dot_f32('se,sd->ed', heads_out[b], d_attn_full[b]) for b in batches).astype(jnp.bfloat16)
+    dx_sums[1], gate = cross_axis(sums_after(dx_sums[1], [grad_wo]), 1)
+    dx_sums[0], gate = cross_axis(sums_after(dx_sums[0], gate), 2)
+    dx_sums[1], _ = cross_axis(sums_after(dx_sums[1], gate), 2)
+    grad_x = jnp.stack([finish_sums(dx_sums[b]) + dy_loc[b].astype(jnp.float32) for b in batches])
+    return (y_loc.reshape(x_loc.shape), grad_x.astype(jnp.bfloat16), *weight_grads, grad_wo,
             grad_gq.astype(jnp.bfloat16), grad_gk.astype(jnp.bfloat16), grad_ga.astype(jnp.bfloat16))
 
 
@@ -324,4 +396,5 @@
     vec_spec = P('tp')
     in_specs = (act_spec, col_spec, col_spec, col_spec, row_spec, vec_spec, vec_spec, P(), act_spec)
     out_specs = (act_spec, act_spec, col_spec, col_spec, col_spec, row_spec, vec_spec, vec_spec, P())
+
     return jax.shard_map(local_block, mesh=mesh, in_specs=in_specs, out_specs=out_specs, check_vma=False)

time: 1160 us -> 910 us (0.78)
  waiting for transfers between devices: 509 us -> 229 us
  Pallas kernels: 347 us -> 261 us
  other arithmetic: 30.2 us -> 85.2 us
  matrix products: 219 us -> 258 us
  starting transfers between devices: 0.27 us -> 23.2 us
    all_gather x3 -> x0, waiting for transfers between devices: 277 us -> none  [local_block(): lax.all_gather(w.T, 'tp', axis=0, tiled=True)]
    ppermute x0 -> x24, waiting for transfers between devices: none -> 126 us  [flip(): return lax.ppermute(value, 'tp', [(i, i ^ bit) for i in range(N_DEV)])]
    pallas_call x2 -> x1, Pallas kernels: 175 us -> 52.2 us  [to_tokens(): pl.pallas_call(functools.partial(to_tokens_kernel, n_arr, tok, cols), out...]
    all_gather x1, waiting for transfers between devices: 116 us -> 0.01 us  [local_block(): lax.all_gather(d_attn.reshape(batch_size, seq_loc, model_dim), 'tp', axis...]
    add x0 -> x18, other arithmetic: none -> 45.4 us  [the longest x12 22.8 us: cross_axis(): away = sum((lax.slice_in_dim(p, 1, 2, axis=axis) for p in pieces))]
    dot_general x19 -> x28, matrix products: 219 us -> 258 us  [dot_f32(): return jnp.einsum(spec, lhs, rhs, preferred_element_type=jnp.float32)]
    all_gather x2, waiting for transfers between devices: 105 us -> 68.7 us  [local_block(): lax.all_gather(x_loc[b], 'tp', axis=0, tiled=True)]
    all_gather x1, waiting for transfers between devices: 7.98 us -> 32.9 us  [local_block(): wo_full = lax.all_gather(wo_loc, 'tp', axis=0, tiled=True)]
  transfers between devices with their start and end apart: 7 -> 28, of which waited for: 6 -> 10; matrix products, arithmetic and copies ran while one was open for 22% -> 38% of each run, Pallas kernels for 30% -> 29%
where the time goes in v2:
time: 910 us; the launch traced here: 903 us
  Pallas kernels  261 us (29%)
  matrix products  258 us (28%)
  waiting for transfers between devices  229 us (25%)
  other arithmetic  85.2 us (9%)
  local copies, waits for them, and re-layouts  32.1 us (4%)
  starting transfers between devices  23.2 us (3%)
  between operations  14.6 us (2%)
    dot_general x28, matrix products, dot_f32(): return jnp.einsum(spec, lhs, rhs, preferred_element_type=jnp.float32)  258 us
    ppermute x24, waiting for transfers between devices, flip(): return lax.ppermute(value, 'tp', [(i, i ^ bit) for i in range(N_DEV)])  126 us
    pallas_call x4, Pallas kernels, sum_devices(): pl.pallas_call(sum_kernel, out_shape=jax.ShapeDtypeStruct(part.shape, jnp...  70.6 us
    all_gather x2, waiting for transfers between devices, local_block(): lax.all_gather(x_loc[b], 'tp', axis=0, tiled=True)  68.7 us
    pallas_call x1, Pallas kernels, to_tokens(): pl.pallas_call(functools.partial(to_tokens_kernel, n_arr, tok, cols), out...  52.2 us
    pallas_call x1, Pallas kernels, to_heads(): pl.pallas_call(functools.partial(to_heads_kernel, tok, cols), out_shape=[...  41 us
    pallas_call x2, Pallas kernels, attention_bwd(): pl.pallas_call(bwd_kernel, grid=(heads,), in_specs=[head_spec, head_spec,...  40 us
    pallas_call x2, Pallas kernels, attention_fwd(): pl.pallas_call(fwd_kernel, grid=(heads,), in_specs=[head_spec, head_spec,...  37.7 us
  transfers between devices with their start and end apart: 28, of which 10 were waited for; matrix products, arithmetic and copies ran while one was open for 38% of the time, Pallas kernels for 29%

profile of v2, /device:TPU:0, one launch (start us, length us, event | category | flops | bytes accessed | tf_op | source)
XLA Modules:
  0.0 902.9 jit_solution(18350169185788879482)
XLA Ops:
  26.1 64.0 %all-gather.11.cloned.1.call-done = bf16[1,2048,4096]{2,1,0:T(8,128)(2,1)} async-done(((bf16[1,128,4096]{2,1,0:T(8,128)(2,1)}), bf16[1,2048,4096]{2,1,0:T(8,128)(2,1)}) %all-gather.11.cloned.1.call-update) | async-done | bytes 16777232 | tf_op jit(solution)/shard_map/all_gather | solution.py:314
  90.1 10.1 %multiply_reduce_fusion.12 = (f32[2048]{0:T(1024)S(1)}, f32[2048,256]{0,1:T(8,128)}) fusion(bf16[2048,4096]{1,0:T(8,128)(2,1)} %bitcast.133, bf16[4096,256]{1,0:T(8,128)(2,1)S(1)} %copy-done.26), kind=kOutput, calls=%fused_computation.60 | convolution fusion | flops 4296013824 | bytes 20979712 | tf_op jit(solution)/shard_map/sd,de->se/dot_general | solution.py:299
  100.2 12.4 %multiply_reduce_fusion.11 = (f32[2048]{0:T(1024)S(1)}, f32[2048,256]{0,1:T(8,128)}) fusion(bf16[2048,4096]{1,0:T(8,128)(2,1)} %bitcast.134, bf16[4096,256]{1,0:T(8,128)(2,1)} %param.11), kind=kOutput, calls=%fused_computation.59 | convolution fusion | flops 4296013824 | bytes 20979712 | tf_op jit(solution)/shard_map/sd,de->se/dot_general | solution.py:299
  113.3 12.6 %convolution_convert_fusion.2.v_ref = bf16[2048,256]{1,0:T(8,128)(2,1)} fusion(bf16[2048,4096]{1,0:T(8,128)(2,1)} %bitcast.135, bf16[4096,256]{1,0:T(8,128)(2,1)} %param.12), kind=kOutput, calls=%fused_computation.39 | convolution fusion | flops 4295491584 | bytes 19922944 | tf_op jit(solution)/shard_map/sd,de->se/dot_general | solution.py:299
  125.8 10.8 %sum_devices.4 = f32[32,128]{1,0:T(8,128)} custom-call(f32[32,128]{1,0:T(8,128)} %reshape.260.part_ref), custom_call_target="tpu_custom_call" | custom-call | flops 1000000000 | bytes 1000000 | tf_op jit(solution)/shard_map/sum_devices/pallas_call | solution.py:55
  145.8 18.8 %attention_fwd.2 = (bf16[2048,256]{1,0:T(8,128)(2,1)}, bf16[2048,256]{1,0:T(8,128)(2,1)}, bf16[2048,256]{1,0:T(8,128)(2,1)}, f32[2,1,2048]{2,1,0:T(1,128)}) custom-call(f32[2048,256]{1,0:T(8,128)} %copy.18.q_ref, f32[2048,256]{1,0:T(8,128)} %copy.19.k_ref, bf16[2048,256]{1,0:T(8,128)(2,1)} %convolution_convert_fusion.2.v_ref, f32[2048,1]{1,0:T(8,128)} %copy.20.iq_ref, ...), custom_call_target="tpu_custom_call" | custom-call | flops 8000000000 | bytes 10000000 | tf_op jit(solution)/shard_map/attention_fwd/pallas_call | solution.py:183
  169.4 9.9 %multiply_reduce_fusion.10 = (f32[2048]{0:T(1024)S(1)}, f32[2048,256]{0,1:T(8,128)}) fusion(bf16[2048,4096]{1,0:T(8,128)(2,1)} %bitcast.141, bf16[4096,256]{1,0:T(8,128)(2,1)S(1)} %copy-done.26), kind=kOutput, calls=%fused_computation.58 | convolution fusion | flops 4296013824 | bytes 20979712 | tf_op jit(solution)/shard_map/sd,de->se/dot_general | solution.py:299
  179.3 13.1 %multiply_reduce_fusion.9 = (f32[2048]{0:T(1024)S(1)}, f32[2048,256]{0,1:T(8,128)}) fusion(bf16[2048,4096]{1,0:T(8,128)(2,1)} %bitcast.142, bf16[4096,256]{1,0:T(8,128)(2,1)} %param.11), kind=kOutput, calls=%fused_computation.57 | convolution fusion | flops 4296013824 | bytes 20979712 | tf_op jit(solution)/shard_map/sd,de->se/dot_general | solution.py:299
  193.0 9.2 %convolution_convert_fusion.1.v_ref = bf16[2048,256]{1,0:T(8,128)(2,1)} fusion(bf16[2048,4096]{1,0:T(8,128)(2,1)} %bitcast.143, bf16[4096,256]{1,0:T(8,128)(2,1)S(1)} %copy-done.29), kind=kOutput, calls=%fused_computation.38 | convolution fusion | flops 4295491584 | bytes 19922944 | tf_op jit(solution)/shard_map/sd,de->se/dot_general | solution.py:299
  202.2 12.9 %sum_devices.5 = f32[32,128]{1,0:T(8,128)} custom-call(f32[32,128]{1,0:T(8,128)} %reshape.261.part_ref), custom_call_target="tpu_custom_call" | custom-call | flops 1000000000 | bytes 1000000 | tf_op jit(solution)/shard_map/sum_devices/pallas_call | solution.py:55
  224.3 18.9 %attention_fwd.3 = (bf16[2048,256]{1,0:T(8,128)(2,1)}, bf16[2048,256]{1,0:T(8,128)(2,1)}, bf16[2048,256]{1,0:T(8,128)(2,1)}, f32[2,1,2048]{2,1,0:T(1,128)}) custom-call(f32[2048,256]{1,0:T(8,128)} %copy.22.q_ref, f32[2048,256]{1,0:T(8,128)} %copy.23.k_ref, bf16[2048,256]{1,0:T(8,128)(2,1)} %convolution_convert_fusion.1.v_ref, f32[2048,1]{1,0:T(8,128)} %copy.24.iq_ref, ...), custom_call_target="tpu_custom_call" | custom-call | flops 8000000000 | bytes 10000000 | tf_op jit(solution)/shard_map/attention_fwd/pallas_call | solution.py:183
  243.1 52.2 %to_tokens.1 = bf16[2,128,4096]{2,1,0:T(8,128)(2,1)} custom-call(bf16[2048,256]{1,0:T(8,128)(2,1)} %get-tuple-element.59.refs_0_, bf16[2048,256]{1,0:T(8,128)(2,1)} %get-tuple-element.62.refs_1_), custom_call_target="tpu_custom_call" | custom-call | flops 10000000000 | bytes 8000000 | tf_op jit(solution)/shard_map/to_tokens/pallas_call | solution.py:95
  295.3 32.9 %all-gather.7.cloned.1.call-done = bf16[4096,4096]{1,0:T(8,128)(2,1)} async-done(((bf16[256,4096]{1,0:T(8,128)(2,1)}), bf16[4096,4096]{1,0:T(8,128)(2,1)}) %all-gather.7.cloned.1.call-update) | async-done | bytes 33554448 | tf_op jit(solution)/shard_map/all_gather | solution.py:315
  328.2 16.0 %multiply_reduce_fusion = (f32[256]{0:T(256)S(1)}, f32[256,4096]{1,0:T(8,128)S(1)}) fusion(bf16[256,4096]{1,0:T(8,128)(2,1)} %bitcast.149, bf16[4096,4096]{1,0:T(8,128)(2,1)} %all-gather.7.cloned.1.call-done), kind=kOutput, calls=%fused_computation.25 | convolution fusion | flops 8592031744 | bytes 39846912 | tf_op jit(solution)/shard_map/te,ed->td/dot_general | solution.py:299
  350.3 18.0 %convolution_convert_fusion = bf16[256,4096]{1,0:T(8,128)(2,1)} fusion(bf16[256,4096]{1,0:T(8,128)(2,1)} %get-tuple-element.139, bf16[4096,4096]{1,0:T(8,128)(2,1)} %all-gather.7.cloned.1.call-done), kind=kOutput, calls=%fused_computation.16 | convolution fusion | flops 8590983168 | bytes 37748736 | tf_op jit(solution)/shard_map/td,ed->te/dot_general | solution.py:299
  368.3 41.0 %to_heads.1 = (bf16[2048,256]{1,0:T(8,128)(2,1)}, bf16[2048,256]{1,0:T(8,128)(2,1)}) custom-call(bf16[2,128,4096]{2,1,0:T(8,128)(2,1)} %bitcast.150), custom_call_target="tpu_custom_call" | custom-call | flops 10000000000 | bytes 8000000 | tf_op jit(solution)/shard_map/to_heads/pallas_call | solution.py:131
  409.2 20.0 %attention_bwd.2 = (f32[2048,256]{1,0:T(8,128)}, f32[2048,256]{1,0:T(8,128)}, bf16[2048,256]{1,0:T(8,128)(2,1)}) custom-call(bf16[2048,256]{1,0:T(8,128)(2,1)} %get-tuple-element.63.q_ref, bf16[2048,256]{1,0:T(8,128)(2,1)} %get-tuple-element.64.k_ref, bf16[2048,256]{1,0:T(8,128)(2,1)} %convolution_convert_fusion.2.v_ref, ...), custom_call_target="tpu_custom_call" | custom-call | flops 20000000000 | bytes 10000000 | tf_op jit(solution)/shard_map/attention_bwd/pallas_call | solution.py:228
  433.2 18.8 %sum_devices.6 = f32[64,128]{1,0:T(8,128)} custom-call(f32[64,128]{1,0:T(8,128)} %maximum_bitcast_fusion.part_ref), custom_call_target="tpu_custom_call" | custom-call | flops 1000000000 | bytes 1000000 | tf_op jit(solution)/shard_map/sum_devices/pallas_call | solution.py:55
  458.1 9.7 %by_distance.2 = bf16[2048,768]{1,0:T(8,128)(2,1)} custom-call(s32[1]{0:T(128)} %bitcast.13.me_ref, bf16[2048,256]{1,0:T(8,128)(2,1)} %multiply_convert_fusion.3.dq_ref, bf16[2048,256]{1,0:T(8,128)(2,1)} %multiply_convert_fusion.2.dk_ref, bf16[2048,256]{1,0:T(8,128)(2,1)} %get-tuple-element.69.dv_ref), custom_call_target="tpu_custom_call" | custom-call | flops 1000000000 | bytes 6000000 | tf_op jit(solution)/shard_map/by_distance/pallas_call | solution.py:256
  473.7 6.2 fusion.28
  479.8 6.0 fusion.36
  486.4 6.1 fusion.46
  492.5 6.0 fusion.30
  502.7 6.2 slice_add_fusion.9
  510.4 6.0 slice_add_fusion.1
  519.4 19.9 %attention_bwd.3 = (f32[2048,256]{1,0:T(8,128)}, f32[2048,256]{1,0:T(8,128)}, bf16[2048,256]{1,0:T(8,128)(2,1)}) custom-call(bf16[2048,256]{1,0:T(8,128)(2,1)} %get-tuple-element.70.q_ref, bf16[2048,256]{1,0:T(8,128)(2,1)} %get-tuple-element.71.k_ref, bf16[2048,256]{1,0:T(8,128)(2,1)} %convolution_convert_fusion.1.v_ref, ...), custom_call_target="tpu_custom_call" | custom-call | flops 20000000000 | bytes 10000000 | tf_op jit(solution)/shard_map/attention_bwd/pallas_call | solution.py:228
  543.6 28.1 %sum_devices.7 = f32[32,128]{1,0:T(8,128)} custom-call(f32[32,128]{1,0:T(8,128)} %pad_maximum_fusion.5.part_ref), custom_call_target="tpu_custom_call" | custom-call | flops 1000000000 | bytes 1000000 | tf_op jit(solution)/shard_map/sum_devices/pallas_call | solution.py:55
  577.6 9.6 %by_distance.3 = bf16[2048,768]{1,0:T(8,128)(2,1)} custom-call(s32[1]{0:T(128)} %bitcast.13.me_ref, bf16[2048,256]{1,0:T(8,128)(2,1)} %multiply_convert_fusion.1.dq_ref, bf16[2048,256]{1,0:T(8,128)(2,1)} %multiply_convert_fusion.dk_ref, bf16[2048,256]{1,0:T(8,128)(2,1)} %get-tuple-element.77.dv_ref), custom_call_target="tpu_custom_call" | custom-call | flops 1000000000 | bytes 6000000 | tf_op jit(solution)/shard_map/by_distance/pallas_call | solution.py:256
  587.2 7.3 fusion.24
  594.6 6.0 fusion.32
  601.1 6.3 fusion.40
  612.2 6.1 fusion.42
  618.3 6.4 fusion.26
  632.8 39.5 %collective-permute-done.4 = f32[2,1,2,128,1408]{4,3,2,1,0:T(8,128)S(1)} collective-permute-done((f32[2,1,2,128,1408]{4,3,2,1,0:T(8,128)S(1)}, f32[2,1,2,128,1408]{4,3,2,1,0:T(8,128)S(1)}, u32[]{:S(2)}, u32[]{:S(2)}) %collective-permute-start.4) | collective-permute-done | bytes 2883616 | tf_op jit(solution)/shard_map/ppermute | solution.py:269
  679.6 5.6 slice_add_fusion.10
  686.1 5.1 slice_add_fusion.4
  696.4 12.5 %fusion.67 = f32[4096,256]{1,0:T(8,128)} fusion(bf16[2048,4096]{1,0:T(8,128)(2,1)} %bitcast.136, bf16[2048,256]{1,0:T(8,128)(2,1)S(1)} %copy-done.32), kind=kOutput, calls=%fused_computation.156 | convolution fusion | flops 4294967296 | bytes 22020096 | tf_op jit(solution)/shard_map/sd,se->de/dot_general | solution.py:299
  709.0 6.7 fusion.66
  715.7 6.8 fusion.65
  722.6 13.7 %fusion.14 = bf16[4096,256]{1,0:T(8,128)(2,1)} fusion(f32[4096,256]{1,0:T(8,128)} %fusion.67, bf16[2048,4096]{1,0:T(8,128)(2,1)} %bitcast.144, bf16[2048,256]{1,0:T(8,128)(2,1)S(1)} %copy-done.33), kind=kOutput, calls=%fused_computation.15 | convolution fusion | flops 4297064448 | bytes 24117248 | tf_op jit(solution)/shard_map/sd,se->de/dot_general | solution.py:299
  736.3 13.7 %fusion.13 = bf16[4096,256]{1,0:T(8,128)(2,1)} fusion(f32[4096,256]{1,0:T(8,128)} %fusion.66, bf16[2048,4096]{1,0:T(8,128)(2,1)} %bitcast.145, bf16[2048,256]{1,0:T(8,128)(2,1)S(1)} %copy-done.20), kind=kOutput, calls=%fused_computation.14 | convolution fusion | flops 4297064448 | bytes 24117248 | tf_op jit(solution)/shard_map/sd,se->de/dot_general | solution.py:299
  750.0 8.3 fusion.12
  758.3 12.8 %fusion = f32[256,4096]{1,0:T(8,128)} fusion(bf16[2048,256]{1,0:T(8,128)(2,1)} %get-tuple-element.62.refs_1_, bf16[2,2048,4096]{2,1,0:T(8,128)(2,1)} %all-gather.9.cloned.1.call-done), kind=kOutput, calls=%fused_computation | convolution fusion | flops 4294967296 | bytes 22020096 | tf_op jit(solution)/shard_map/se,sd->ed/dot_general | solution.py:299
  771.2 13.0 %fusion.9 = bf16[256,4096]{1,0:T(8,128)(2,1)} fusion(f32[256,4096]{1,0:T(8,128)} %fusion, bf16[2048,256]{1,0:T(8,128)(2,1)S(1)} %copy-done.39, bf16[2,2048,4096]{2,1,0:T(8,128)(2,1)} %all-gather.9.cloned.1.call-done), kind=kOutput, calls=%fused_computation.12 | convolution fusion | flops 4297064448 | bytes 24117248 | tf_op jit(solution)/shard_map/se,sd->ed/dot_general | solution.py:299
  795.2 23.5 %collective-permute-done.2 = f32[1,1,2,128,1408]{4,3,2,1,0:T(8,128)S(1)} collective-permute-done((f32[1,1,2,128,1408]{4,3,2,1,0:T(8,128)S(1)}, f32[1,1,2,128,1408]{4,3,2,1,0:T(8,128)S(1)}, u32[]{:S(2)}, u32[]{:S(2)}) %collective-permute-start.2) | collective-permute-done | bytes 1441824 | tf_op jit(solution)/shard_map/ppermute | solution.py:269
  823.6 36.7 %collective-permute-done.17 = f32[1,1,1,128,1280]{4,3,2,1,0:T(8,128)S(1)} collective-permute-done((f32[1,1,1,128,1280]{4,3,2,1,0:T(8,128)S(1)}, f32[1,1,1,128,1280]{4,3,2,1,0:T(8,128)S(1)}, u32[]{:S(2)}, u32[]{:S(2)}) %collective-permute-start.17) | collective-permute-done | bytes 655392 | tf_op jit(solution)/shard_map/ppermute | solution.py:269
  862.8 12.4 %collective-permute-done.16 = f32[1,1,1,128,1408]{4,3,2,1,0:T(8,128)S(1)} collective-permute-done((f32[1,1,1,128,1408]{4,3,2,1,0:T(8,128)S(1)}, f32[1,1,1,128,1408]{4,3,2,1,0:T(8,128)S(1)}, u32[]{:S(2)}, u32[]{:S(2)}) %collective-permute-start.16) | collective-permute-done | bytes 720928 | tf_op jit(solution)/shard_map/ppermute | solution.py:269
  879.7 9.7 %collective-permute-done.23 = f32[1,1,1,128,1280]{4,3,2,1,0:T(8,128)S(1)} collective-permute-done((f32[1,1,1,128,1280]{4,3,2,1,0:T(8,128)S(1)}, f32[1,1,1,128,1280]{4,3,2,1,0:T(8,128)S(1)}, u32[]{:S(2)}, u32[]{:S(2)}) %collective-permute-start.23) | collective-permute-done | bytes 655392 | tf_op jit(solution)/shard_map/ppermute | solution.py:269
  (225 shorter events, 140.6 us)
Async XLA Ops:
  7.2 82.9 %all-gather.11.cloned.1.call-start = ((), (), s32[]{:S(2)}) async-start(), calls=%async_computation.2 | async-start | bytes 17825792 | tf_op jit(solution)/shard_map/all_gather | solution.py:314
  10.3 159.1 %all-gather.13.cloned.1.call-start = ((), (), s32[]{:S(2)}) async-start(), calls=%async_computation.3 | async-start | bytes 17825792 | tf_op jit(solution)/shard_map/all_gather | solution.py:314
  11.1 317.1 %all-gather.7.cloned.1.call-start = ((), (), s32[]{:S(2)}) async-start(), calls=%async_computation | async-start | bytes 35651584 | tf_op jit(solution)/shard_map/all_gather | solution.py:315
  11.8 746.5 %all-gather.9.cloned.1.call-start = ((), (), s32[]{:S(2)}) async-start(), calls=%async_computation.1 | async-start | bytes 35651584 | tf_op jit(solution)/shard_map/all_gather | solution.py:348
  179.3 13.7 %copy-start.29 = (bf16[4096,256]{1,0:T(8,128)(2,1)S(1)}, bf16[4096,256]{1,0:T(8,128)(2,1)}, u32[]{:S(2)}) copy-start(bf16[4096,256]{1,0:T(8,128)(2,1)} %param.12) | copy-start | bytes 6291460
  202.2 17.0 %copy-start.30 = (f32[2048,256]{0,1:T(8,128)S(1)}, f32[2048,256]{0,1:T(8,128)}, u32[]{:S(2)}) copy-start(f32[2048,256]{0,1:T(8,128)} %get-tuple-element.167) | copy-start | bytes 6291460
  328.2 16.0 %copy-start.4 = (bf16[2,128,4096]{2,1,0:T(8,128)(2,1)S(1)}, bf16[2,128,4096]{2,1,0:T(8,128)(2,1)}, u32[]{:S(2)}) copy-start(bf16[2,128,4096]{2,1,0:T(8,128)(2,1)} %param.17) | copy-start | bytes 6291460
  409.2 20.1 %copy-start.2 = (f32[2048,256]{1,0:T(8,128)S(1)}, f32[2048,256]{1,0:T(8,128)}, u32[]{:S(2)}) copy-start(f32[2048,256]{1,0:T(8,128)} %copy.18.q_ref) | copy-start | bytes 6291460
  409.2 20.1 %copy-start.3 = (f32[2048,256]{1,0:T(8,128)S(1)}, f32[2048,256]{1,0:T(8,128)}, u32[]{:S(2)}) copy-start(f32[2048,256]{1,0:T(8,128)} %copy.19.k_ref) | copy-start | bytes 6291460
  472.2 30.5 %collective-permute-start.6 = (f32[1024,1280]{1,0:T(8,128)S(1)}, f32[1024,1280]{1,0:T(8,128)S(1)}, u32[]{:S(2)}, u32[]{:S(2)}) collective-permute-start(f32[1024,1280]{1,0:T(8,128)S(1)} %fusion.44), channel_id=1, source_target_pairs={{0,1},{1,0},{2,3},{3,2},{4,5},{5,4},{6,7},{7,6},{8,9},{9,8},{10,11... | collective-permute-start | bytes 15728648 | tf_op jit(solution)/shard_map/ppermute | solution.py:269
  479.8 30.5 %collective-permute-start.3 = (f32[1024,1408]{1,0:T(8,128)}, f32[1024,1408]{1,0:T(8,128)S(1)}, u32[]{:S(2)}, u32[]{:S(2)}) collective-permute-start(f32[1024,1408]{1,0:T(8,128)} %fusion.28), channel_id=1, source_target_pairs={{0,1},{1,0},{2,3},{3,2},{4,5},{5,4},{6,7},{7,6},{8,9},{9,8},{10,11... | collective-permute-start | bytes 17301512 | tf_op jit(solution)/shard_map/ppermute | solution.py:269
  485.9 30.5 %collective-permute-start = (f32[1024,1408]{1,0:T(8,128)}, f32[1024,1408]{1,0:T(8,128)S(1)}, u32[]{:S(2)}, u32[]{:S(2)}) collective-permute-start(f32[1024,1408]{1,0:T(8,128)} %fusion.36), channel_id=1, source_target_pairs={{0,1},{1,0},{2,3},{3,2},{4,5},{5,4},{6,7},{7,6},{8,9},{9,8},{10,11... | collective-permute-start | bytes 17301512 | tf_op jit(solution)/shard_map/ppermute | solution.py:269
  508.9 102.3 %collective-permute-start.7 = (f32[2,2,1,128,1280]{4,3,2,1,0:T(8,128)}, f32[2,2,1,128,1280]{4,3,2,1,0:T(8,128)}, u32[]{:S(2)}, u32[]{:S(2)}) collective-permute-start(f32[2,2,1,128,1280]{4,3,2,1,0:T(8,128)} %get-tuple-element.126), channel_id=1, source_target_pairs={{0,2},{1,3},{2,0},{3,1},{4,6},{5,7},{6,4},{7,5},{8,10},{9,11},{10,... | collective-permute-start | bytes 7864328 | tf_op jit(solution)/shard_map/ppermute | solution.py:269
  519.4 19.9 %copy-start = (f32[2048,256]{1,0:T(8,128)S(1)}, f32[2048,256]{1,0:T(8,128)}, u32[]{:S(2)}) copy-start(f32[2048,256]{1,0:T(8,128)} %copy.22.q_ref) | copy-start | bytes 6291460
  519.4 19.9 %copy-start.34 = (f32[2048]{0:T(1024)S(1)}, f32[2048]{0:T(1024)}, u32[]{:S(2)}) copy-start(f32[2048]{0:T(1024)} %get-tuple-element.147) | copy-start | bytes 24580
  600.6 79.0 %collective-permute-start.10 = (f32[1024,1408]{1,0:T(8,128)}, f32[1024,1408]{1,0:T(8,128)S(1)}, u32[]{:S(2)}, u32[]{:S(2)}) collective-permute-start(f32[1024,1408]{1,0:T(8,128)} %fusion.24), channel_id=1, source_target_pairs={{0,1},{1,0},{2,3},{3,2},{4,5},{5,4},{6,7},{7,6},{8,9},{9,8},{10,11... | collective-permute-start | bytes 17301512 | tf_op jit(solution)/shard_map/ppermute | solution.py:269
  600.7 78.9 %collective-permute-start.9 = (f32[1024,1408]{1,0:T(8,128)}, f32[1024,1408]{1,0:T(8,128)S(1)}, u32[]{:S(2)}, u32[]{:S(2)}) collective-permute-start(f32[1024,1408]{1,0:T(8,128)} %fusion.32), channel_id=1, source_target_pairs={{0,1},{1,0},{2,3},{3,2},{4,5},{5,4},{6,7},{7,6},{8,9},{9,8},{10,11... | collective-permute-start | bytes 17301512 | tf_op jit(solution)/shard_map/ppermute | solution.py:269
  607.4 72.2 %collective-permute-start.11 = (f32[1024,1280]{1,0:T(8,128)}, f32[1024,1280]{1,0:T(8,128)S(1)}, u32[]{:S(2)}, u32[]{:S(2)}) collective-permute-start(f32[1024,1280]{1,0:T(8,128)} %fusion.40), channel_id=1, source_target_pairs={{0,1},{1,0},{2,3},{3,2},{4,5},{5,4},{6,7},{7,6},{8,9},{9,8},{10,11... | collective-permute-start | bytes 15728648 | tf_op jit(solution)/shard_map/ppermute | solution.py:269
  607.5 64.8 %collective-permute-start.4 = (f32[2,1,2,128,1408]{4,3,2,1,0:T(8,128)S(1)}, f32[2,1,2,128,1408]{4,3,2,1,0:T(8,128)S(1)}, u32[]{:S(2)}, u32[]{:S(2)}) collective-permute-start(f32[2,1,2,128,1408]{4,3,2,1,0:T(8,128)S(1)} %copy-done.25), channel_id=1, source_target_pairs={{0,4},{1,5},{2,6},{3,7},{4,0},{5,1},{6,2},{7,3},{8,12},{9,13},{10,... | collective-permute-start | bytes 8650760 | tf_op jit(solution)/shard_map/ppermute | solution.py:269
  611.2 65.4 %collective-permute-start.1 = (f32[1,2,2,128,1408]{4,3,2,1,0:T(8,128)S(1)}, f32[1,2,2,128,1408]{4,3,2,1,0:T(8,128)S(1)}, u32[]{:S(2)}, u32[]{:S(2)}) collective-permute-start(f32[1,2,2,128,1408]{4,3,2,1,0:T(8,128)S(1)} %bitcast.121), channel_id=1, source_target_pairs={{0,8},{1,9},{2,10},{3,11},{4,12},{5,13},{6,14},{7,15},{8,0},{9,1},... | collective-permute-start | bytes 8650760 | tf_op jit(solution)/shard_map/ppermute | solution.py:269
  629.0 44.7 %copy-start.7 = (f32[2,1,2,128,1408]{4,3,2,1,0:T(8,128)S(1)}, f32[2,1,2,128,1408]{4,3,2,1,0:T(8,128)}, u32[]{:S(2)}) copy-start(f32[2,1,2,128,1408]{4,3,2,1,0:T(8,128)} %get-tuple-element.119) | copy-start | bytes 8650756
  672.3 121.7 %collective-permute-start.8 = (f32[1,2,1,128,1280]{4,3,2,1,0:T(8,128)}, f32[1,2,1,128,1280]{4,3,2,1,0:T(8,128)}, u32[]{:S(2)}, u32[]{:S(2)}) collective-permute-start(f32[1,2,1,128,1280]{4,3,2,1,0:T(8,128)} %get-tuple-element.136), channel_id=1, source_target_pairs={{0,8},{1,9},{2,10},{3,11},{4,12},{5,13},{6,14},{7,15},{8,0},{9,1},... | collective-permute-start | bytes 3932168 | tf_op jit(solution)/shard_map/ppermute | solution.py:269
  676.6 118.6 %collective-permute-start.5 = (f32[2,1,1,128,1408]{4,3,2,1,0:T(8,128)}, f32[2,1,1,128,1408]{4,3,2,1,0:T(8,128)}, u32[]{:S(2)}, u32[]{:S(2)}) collective-permute-start(f32[2,1,1,128,1408]{4,3,2,1,0:T(8,128)} %get-tuple-element.128), channel_id=1, source_target_pairs={{0,2},{1,3},{2,0},{3,1},{4,6},{5,7},{6,4},{7,5},{8,10},{9,11},{10,... | collective-permute-start | bytes 4325384 | tf_op jit(solution)/shard_map/ppermute | solution.py:269
  685.2 99.0 %collective-permute-start.14 = (f32[2,2,1,128,1280]{4,3,2,1,0:T(8,128)}, f32[2,2,1,128,1280]{4,3,2,1,0:T(8,128)}, u32[]{:S(2)}, u32[]{:S(2)}) collective-permute-start(f32[2,2,1,128,1280]{4,3,2,1,0:T(8,128)} %get-tuple-element.123), channel_id=1, source_target_pairs={{0,2},{1,3},{2,0},{3,1},{4,6},{5,7},{6,4},{7,5},{8,10},{9,11},{10,... | collective-permute-start | bytes 7864328 | tf_op jit(solution)/shard_map/ppermute | solution.py:269
  691.2 93.7 %collective-permute-start.13 = (f32[2,1,2,128,1408]{4,3,2,1,0:T(8,128)}, f32[2,1,2,128,1408]{4,3,2,1,0:T(8,128)}, u32[]{:S(2)}, u32[]{:S(2)}) collective-permute-start(f32[2,1,2,128,1408]{4,3,2,1,0:T(8,128)} %get-tuple-element.115), channel_id=1, source_target_pairs={{0,4},{1,5},{2,6},{3,7},{4,0},{5,1},{6,2},{7,3},{8,12},{9,13},{10,... | collective-permute-start | bytes 8650760 | tf_op jit(solution)/shard_map/ppermute | solution.py:269
  694.7 14.2 %slice-start = ((s8[16777216]{0:T(1024)(128)(4,1)}), s8[4194304]{0:T(1024)(128)(4,1)S(1)}, s32[]{:S(2)}) async-start(s8[16777216]{0:T(1024)(128)(4,1)} %bitcast.137), calls=%async_computation.4 | async-start | bytes 8388608
  694.7 14.2 %copy-start.18 = (bf16[2048,256]{1,0:T(8,128)(2,1)S(1)}, bf16[2048,256]{1,0:T(8,128)(2,1)}, u32[]{:S(2)}) copy-start(bf16[2048,256]{1,0:T(8,128)(2,1)} %multiply_convert_fusion.2.dk_ref) | copy-start | bytes 3145732
  694.7 14.2 %slice-start.1 = ((s8[16777216]{0:T(1024)(128)(4,1)}), s8[4194304]{0:T(1024)(128)(4,1)S(1)}, s32[]{:S(2)}) async-start(s8[16777216]{0:T(1024)(128)(4,1)} %bitcast.137), calls=%async_computation.5 | async-start | bytes 8388608
  694.7 14.2 %slice-start.2 = ((s8[16777216]{0:T(1024)(128)(4,1)}), s8[4194304]{0:T(1024)(128)(4,1)S(1)}, s32[]{:S(2)}) async-start(s8[16777216]{0:T(1024)(128)(4,1)} %bitcast.137), calls=%async_computation.6 | async-start | bytes 8388608
  694.7 14.2 %slice-start.3 = ((s8[16777216]{0:T(1024)(128)(4,1)}), s8[4194304]{0:T(1024)(128)(4,1)S(1)}, s32[]{:S(2)}) async-start(s8[16777216]{0:T(1024)(128)(4,1)} %bitcast.137), calls=%async_computation.7 | async-start | bytes 8388608
  694.7 90.2 %collective-permute-start.12 = (f32[1,2,2,128,1408]{4,3,2,1,0:T(8,128)}, f32[1,2,2,128,1408]{4,3,2,1,0:T(8,128)}, u32[]{:S(2)}, u32[]{:S(2)}) collective-permute-start(f32[1,2,2,128,1408]{4,3,2,1,0:T(8,128)} %get-tuple-element.117), channel_id=1, source_target_pairs={{0,8},{1,9},{2,10},{3,11},{4,12},{5,13},{6,14},{7,15},{8,0},{9,1},... | collective-permute-start | bytes 8650760 | tf_op jit(solution)/shard_map/ppermute | solution.py:269
  722.6 13.7 %copy-start.20 = (bf16[2048,256]{1,0:T(8,128)(2,1)S(1)}, bf16[2048,256]{1,0:T(8,128)(2,1)}, u32[]{:S(2)}) copy-start(bf16[2048,256]{1,0:T(8,128)(2,1)} %multiply_convert_fusion.dk_ref) | copy-start | bytes 3145732
  722.6 27.4 %slice-start.4 = ((s8[16777216]{0:T(1024)(128)(4,1)}), s8[4194304]{0:T(1024)(128)(4,1)S(1)}, s32[]{:S(2)}) async-start(s8[16777216]{0:T(1024)(128)(4,1)} %bitcast.146), calls=%async_computation.8 | async-start | bytes 8388608
  722.6 27.4 %slice-start.5 = ((s8[16777216]{0:T(1024)(128)(4,1)}), s8[4194304]{0:T(1024)(128)(4,1)S(1)}, s32[]{:S(2)}) async-start(s8[16777216]{0:T(1024)(128)(4,1)} %bitcast.146), calls=%async_computation.9 | async-start | bytes 8388608
  771.2 13.8 %copy-start.10 = (f32[2,2,1,128,1280]{4,3,2,1,0:T(8,128)S(1)}, f32[2,2,1,128,1280]{4,3,2,1,0:T(8,128)}, u32[]{:S(2)}) copy-start(f32[2,2,1,128,1280]{4,3,2,1,0:T(8,128)} %get-tuple-element.91) | copy-start | bytes 7864324
  784.2 34.5 %collective-permute-start.2 = (f32[1,1,2,128,1408]{4,3,2,1,0:T(8,128)S(1)}, f32[1,1,2,128,1408]{4,3,2,1,0:T(8,128)S(1)}, u32[]{:S(2)}, u32[]{:S(2)}) collective-permute-start(f32[1,1,2,128,1408]{4,3,2,1,0:T(8,128)S(1)} %copy-done.31), channel_id=1, source_target_pairs={{0,4},{1,5},{2,6},{3,7},{4,0},{5,1},{6,2},{7,3},{8,12},{9,13},{10,... | collective-permute-start | bytes 4325384 | tf_op jit(solution)/shard_map/ppermute | solution.py:269
  787.0 89.5 %collective-permute-start.20 = (f32[1,2,1,128,1280]{4,3,2,1,0:T(8,128)S(1)}, f32[1,2,1,128,1280]{4,3,2,1,0:T(8,128)S(1)}, u32[]{:S(2)}, u32[]{:S(2)}) collective-permute-start(f32[1,2,1,128,1280]{4,3,2,1,0:T(8,128)S(1)} %get-tuple-element.137), channel_id=1, source_target_pairs={{0,8},{1,9},{2,10},{3,11},{4,12},{5,13},{6,14},{7,15},{8,0},{9,1},... | collective-permute-start | bytes 3932168 | tf_op jit(solution)/shard_map/ppermute | solution.py:269
  790.4 28.3 %copy-start.17 = (f32[1,2,1,128,1280]{4,3,2,1,0:T(8,128)S(1)}, f32[1,2,1,128,1280]{4,3,2,1,0:T(8,128)}, u32[]{:S(2)}) copy-start(f32[1,2,1,128,1280]{4,3,2,1,0:T(8,128)} %get-tuple-element.97) | copy-start | bytes 3932164
  790.4 86.1 %collective-permute-start.19 = (f32[2,1,1,128,1408]{4,3,2,1,0:T(8,128)S(1)}, f32[2,1,1,128,1408]{4,3,2,1,0:T(8,128)S(1)}, u32[]{:S(2)}, u32[]{:S(2)}) collective-permute-start(f32[2,1,1,128,1408]{4,3,2,1,0:T(8,128)S(1)} %get-tuple-element.131), channel_id=1, source_target_pairs={{0,2},{1,3},{2,0},{3,1},{4,6},{5,7},{6,4},{7,5},{8,10},{9,11},{10,... | collective-permute-start | bytes 4325384 | tf_op jit(solution)/shard_map/ppermute | solution.py:269
  791.7 28.9 %copy-start.16 = (f32[1,1,2,128,1408]{4,3,2,1,0:T(8,128)S(1)}, f32[1,1,2,128,1408]{4,3,2,1,0:T(8,128)}, u32[]{:S(2)}) copy-start(f32[1,1,2,128,1408]{4,3,2,1,0:T(8,128)} %get-tuple-element.93) | copy-start | bytes 4325380
  793.9 28.5 %copy-start.15 = (f32[2,1,1,128,1408]{4,3,2,1,0:T(8,128)S(1)}, f32[2,1,1,128,1408]{4,3,2,1,0:T(8,128)}, u32[]{:S(2)}) copy-start(f32[2,1,1,128,1408]{4,3,2,1,0:T(8,128)} %get-tuple-element.95) | copy-start | bytes 4325380
  794.0 82.6 %collective-permute-start.18 = (f32[1,1,2,128,1408]{4,3,2,1,0:T(8,128)S(1)}, f32[1,1,2,128,1408]{4,3,2,1,0:T(8,128)S(1)}, u32[]{:S(2)}, u32[]{:S(2)}) collective-permute-start(f32[1,1,2,128,1408]{4,3,2,1,0:T(8,128)S(1)} %get-tuple-element.133), channel_id=1, source_target_pairs={{0,4},{1,5},{2,6},{3,7},{4,0},{5,1},{6,2},{7,3},{8,12},{9,13},{10,... | collective-permute-start | bytes 4325384 | tf_op jit(solution)/shard_map/ppermute | solution.py:269
  819.9 40.5 %collective-permute-start.17 = (f32[1,1,1,128,1280]{4,3,2,1,0:T(8,128)S(1)}, f32[1,1,1,128,1280]{4,3,2,1,0:T(8,128)S(1)}, u32[]{:S(2)}, u32[]{:S(2)}) collective-permute-start(f32[1,1,1,128,1280]{4,3,2,1,0:T(8,128)S(1)} %slice_add_fusion.29), channel_id=1, source_target_pairs={{0,4},{1,5},{2,6},{3,7},{4,0},{5,1},{6,2},{7,3},{8,12},{9,13},{10,... | collective-permute-start | bytes 1966088 | tf_op jit(solution)/shard_map/ppermute | solution.py:269
  820.7 42.0 %collective-permute-start.15 = (f32[1,1,1,128,1408]{4,3,2,1,0:T(8,128)S(1)}, f32[1,1,1,128,1408]{4,3,2,1,0:T(8,128)S(1)}, u32[]{:S(2)}, u32[]{:S(2)}) collective-permute-start(f32[1,1,1,128,1408]{4,3,2,1,0:T(8,128)S(1)} %slice_add_fusion.27), channel_id=1, source_target_pairs={{0,2},{1,3},{2,0},{3,1},{4,6},{5,7},{6,4},{7,5},{8,10},{9,11},{10,... | collective-permute-start | bytes 2162696 | tf_op jit(solution)/shard_map/ppermute | solution.py:269
  860.3 14.9 %collective-permute-start.16 = (f32[1,1,1,128,1408]{4,3,2,1,0:T(8,128)S(1)}, f32[1,1,1,128,1408]{4,3,2,1,0:T(8,128)S(1)}, u32[]{:S(2)}, u32[]{:S(2)}) collective-permute-start(f32[1,1,1,128,1408]{4,3,2,1,0:T(8,128)S(1)} %slice_add_fusion.26), channel_id=1, source_target_pairs={{0,8},{1,9},{2,10},{3,11},{4,12},{5,13},{6,14},{7,15},{8,0},{9,1},... | collective-permute-start | bytes 2162696 | tf_op jit(solution)/shard_map/ppermute | solution.py:269
  876.6 12.7 %collective-permute-start.23 = (f32[1,1,1,128,1280]{4,3,2,1,0:T(8,128)S(1)}, f32[1,1,1,128,1280]{4,3,2,1,0:T(8,128)S(1)}, u32[]{:S(2)}, u32[]{:S(2)}) collective-permute-start(f32[1,1,1,128,1280]{4,3,2,1,0:T(8,128)S(1)} %slice_add_fusion.28), channel_id=1, source_target_pairs={{0,4},{1,5},{2,6},{3,7},{4,0},{5,1},{6,2},{7,3},{8,12},{9,13},{10,... | collective-permute-start | bytes 1966088 | tf_op jit(solution)/shard_map/ppermute | solution.py:269
  878.2 14.2 %collective-permute-start.21 = (f32[1,1,1,128,1408]{4,3,2,1,0:T(8,128)S(1)}, f32[1,1,1,128,1408]{4,3,2,1,0:T(8,128)S(1)}, u32[]{:S(2)}, u32[]{:S(2)}) collective-permute-start(f32[1,1,1,128,1408]{4,3,2,1,0:T(8,128)S(1)} %slice_add_fusion.25), channel_id=1, source_target_pairs={{0,2},{1,3},{2,0},{3,1},{4,6},{5,7},{6,4},{7,5},{8,10},{9,11},{10,... | collective-permute-start | bytes 2162696 | tf_op jit(solution)/shard_map/ppermute | solution.py:269
  878.5 14.0 %collective-permute-start.22 = (f32[1,1,1,128,1408]{4,3,2,1,0:T(8,128)S(1)}, f32[1,1,1,128,1408]{4,3,2,1,0:T(8,128)S(1)}, u32[]{:S(2)}, u32[]{:S(2)}) collective-permute-start(f32[1,1,1,128,1408]{4,3,2,1,0:T(8,128)S(1)} %slice_add_fusion.24), channel_id=1, source_target_pairs={{0,8},{1,9},{2,10},{3,11},{4,12},{5,13},{6,14},{7,15},{8,0},{9,1},... | collective-permute-start | bytes 2162696 | tf_op jit(solution)/shard_map/ppermute | solution.py:269
  (28 other events, 162.9 us)
Sparse Core Ops, SparseCore 0:
  10.8 79.2 all-gather.10
  92.9 76.4 all-gather.12
  171.6 156.5 all-gather.6
  350.4 156.3 all-gather.8

commit v3 on v1

v3 whole, which is shorter than its diff:
```python
import functools
import math

import jax
import jax.numpy as jnp
from jax import lax
from jax.experimental import pallas as pl
from jax.experimental.pallas import tpu as pltpu
from jax.sharding import PartitionSpec as P


HEAD_SIZE = 128
ROPE_THETA = 500000.0
NORM_EPS = 1e-6
N_DEV = 16
Q_BLOCK = 256
LOG2E = math.log2(math.e)
ATTN_SCALE = HEAD_SIZE ** -0.5
NT = (((1,), (1,)), ((), ()))
NN = (((1,), (0,)), ((), ()))


def rope_tables(seq_len):
    half_dim = HEAD_SIZE // 2
    inv_freq = 1.0 / (ROPE_THETA ** (jnp.arange(half_dim, dtype=jnp.float32) / half_dim))
    angles = jnp.arange(seq_len, dtype=jnp.float32)[:, None] * inv_freq[None, :]
    cos_t, sin_t = jnp.cos(angles), jnp.sin(angles)
    return jnp.concatenate([cos_t, cos_t], axis=-1), jnp.concatenate([-sin_t, sin_t], axis=-1)


def vmem_spec():
    return pl.BlockSpec(memory_space=pltpu.VMEM)


def sum_kernel(part_ref, out_ref, slots, send_sems, recv_sems):
    me = lax.axis_index('tp')
    copies = []
    for step in range(1, N_DEV):
        peer = lax.rem(me + step, N_DEV)
        copy = pltpu.make_async_remote_copy(
            src_ref=part_ref, dst_ref=slots.at[step], send_sem=send_sems.at[step], recv_sem=recv_sems.at[step],
            device_id=(peer,), device_id_type=pl.DeviceIdType.MESH)
        copy.start()
        copies.append(copy)
    slots[0] = part_ref[...]
    for copy in copies:
        copy.wait()
    total = jnp.zeros(part_ref.shape, jnp.float32)
    for owner in range(N_DEV):
        total = total + slots[lax.rem(me - owner + N_DEV, N_DEV)]
    out_ref[...] = total


def sum_devices(part):
    return pl.pallas_call(
        sum_kernel,
        out_shape=jax.ShapeDtypeStruct(part.shape, jnp.float32),
        in_specs=[vmem_spec()],
        out_specs=vmem_spec(),
        scratch_shapes=[pltpu.VMEM((N_DEV,) + part.shape, jnp.float32),
                        pltpu.SemaphoreType.DMA((N_DEV,)), pltpu.SemaphoreType.DMA((N_DEV,))],
        compiler_params=pltpu.CompilerParams(has_side_effects=True),
        cost_estimate=pl.CostEstimate(flops=int(1e9), bytes_accessed=int(1e6), transcendentals=0),
        name='sum_devices',
    )(part)


def to_tokens_kernel(tok, cols, in_ref, out_ref, send_sems, recv_sems):
    me = lax.axis_index('tp')
    copies = []
    my_cols = pl.ds(pl.multiple_of(me * cols, cols), cols)
    for step in range(1, N_DEV):
        peer = lax.rem(me + step, N_DEV)
        copy = pltpu.make_async_remote_copy(
            src_ref=in_ref.at[:, pl.ds(pl.multiple_of(peer * tok, tok), tok), :], dst_ref=out_ref.at[:, :, my_cols],
            send_sem=send_sems.at[step], recv_sem=recv_sems.at[step],
            device_id=(peer,), device_id_type=pl.DeviceIdType.MESH)
        copy.start()
        copies.append(copy)
    out_ref[:, :, my_cols] = in_ref[:, pl.ds(pl.multiple_of(me * tok, tok), tok), :]
    for copy in copies:
        copy.wait()


def to_heads_kernel(tok, cols, in_ref, out_ref, send_sems, recv_sems):
    me = lax.axis_index('tp')
    my_rows = pl.ds(pl.multiple_of(me * tok, tok), tok)
    copies = []
    for step in range(1, N_DEV):
        peer = lax.rem(me + step, N_DEV)
        copy = pltpu.make_async_remote_copy(
            src_ref=in_ref.at[:, :, pl.ds(pl.multiple_of(peer * cols, cols), cols)], dst_ref=out_ref.at[:, my_rows, :],
            send_sem=send_sems.at[step], recv_sem=recv_sems.at[step],
            device_id=(peer,), device_id_type=pl.DeviceIdType.MESH)
        copy.start()
        copies.append(copy)
    out_ref[:, my_rows, :] = in_ref[:, :, pl.ds(pl.multiple_of(me * cols, cols), cols)]
    for copy in copies:
        copy.wait()


def exchange(kernel, arr, tok, cols, out_shape):
    return pl.pallas_call(
        functools.partial(kernel, tok, cols),
        out_shape=jax.ShapeDtypeStruct(out_shape, jnp.bfloat16),
        in_specs=[vmem_spec()],
        out_specs=vmem_spec(),
        scratch_shapes=[pltpu.SemaphoreType.DMA((N_DEV,)), pltpu.SemaphoreType.DMA((N_DEV,))],
        compiler_params=pltpu.CompilerParams(has_side_effects=True),
        cost_estimate=pl.CostEstimate(flops=int(1e10), bytes_accessed=int(8e6), transcendentals=0),
    )(arr)


def to_tokens(arr):
    batch_size, seq_len, cols = arr.shape
    tok = seq_len // N_DEV
    return exchange(to_tokens_kernel, arr, tok, cols, (batch_size, tok, cols * N_DEV))


def to_heads(arr):
    batch_size, tok, width = arr.shape
    cols = width // N_DEV
    return exchange(to_heads_kernel, arr, tok, cols, (batch_size, tok * N_DEV, cols))


def causal_tile(scores, first_key_row):
    diag = scores[first_key_row:, :]
    key_pos = lax.broadcasted_iota(jnp.int32, diag.shape, 0)
    query_pos = lax.broadcasted_iota(jnp.int32, diag.shape, 1)
    diag = jnp.where(key_pos <= query_pos, diag, -1e30)
    if first_key_row == 0:
        return diag
    return jnp.concatenate([scores[:first_key_row, :], diag], axis=0)


def fwd_kernel(q_ref, k_ref, v_ref, iq_ref, ik_ref, gq_ref, gk_ref, cos_ref, sin_ref,
               o_ref, qr_ref, kr_ref, lse_ref, vt_ref):
    seq_len = q_ref.shape[0]
    cos_t, sin_t = cos_ref[...], sin_ref[...]
    for src, inv, gain, dst in ((q_ref, iq_ref, gq_ref, qr_ref), (k_ref, ik_ref, gk_ref, kr_ref)):
        hat = src[...] * inv[...] * gain[...].astype(jnp.float32)
        dst[...] = (hat * cos_t + pltpu.roll(hat, HEAD_SIZE // 2, 1) * sin_t).astype(jnp.bfloat16)
    vt_ref[...] = v_ref[...].astype(jnp.float32).T.astype(jnp.bfloat16)
    for first in range(0, seq_len, Q_BLOCK):
        ext = first + Q_BLOCK
        scores = lax.dot_general(kr_ref[:ext, :], qr_ref[first:ext, :], NT,
                                 preferred_element_type=jnp.float32) * (ATTN_SCALE * LOG2E)
        scores = causal_tile(scores, first)
        top = jnp.max(scores, axis=0, keepdims=True)
        expd = jnp.exp2(scores - top)
        total = jnp.sum(expd, axis=0, keepdims=True)
        probs = (expd * (1.0 / total)).astype(jnp.bfloat16)
        out_t = lax.dot_general(vt_ref[:, :ext], probs, NN, preferred_element_type=jnp.float32)
        o_ref[first:ext, :] = out_t.T.astype(jnp.bfloat16)
        lse_ref[:, first:ext] = top + jnp.log2(total)


def attention_fwd(q_raw, k_raw, v_heads, inv_q, inv_k, gq, gk, cos_t, sin_t):
    batch_size, seq_len, cols = q_raw.shape
    heads = cols // HEAD_SIZE
    head_spec = pl.BlockSpec((None, seq_len, HEAD_SIZE), lambda b, h: (b, 0, h))
    col_spec = pl.BlockSpec((None, seq_len, 1), lambda b, h: (b, 0, 0))
    gain_spec = pl.BlockSpec((1, HEAD_SIZE), lambda b, h: (0, h))
    table_spec = pl.BlockSpec((seq_len, HEAD_SIZE), lambda b, h: (0, 0))
    lse_spec = pl.BlockSpec((None, None, 1, seq_len), lambda b, h: (b, h, 0, 0))
    return pl.pallas_call(
        fwd_kernel,
        grid=(batch_size, heads),
        in_specs=[head_spec, head_spec, head_spec, col_spec, col_spec, gain_spec, gain_spec, table_spec, table_spec],
        out_specs=[head_spec, head_spec, head_spec, lse_spec],
        out_shape=[jax.ShapeDtypeStruct((batch_size, seq_len, cols), jnp.bfloat16)] * 3
        + [jax.ShapeDtypeStruct((batch_size, heads, 1, seq_len), jnp.float32)],
        scratch_shapes=[pltpu.VMEM((HEAD_SIZE, seq_len), jnp.bfloat16)],
        compiler_params=pltpu.CompilerParams(dimension_semantics=('arbitrary', 'arbitrary'), vmem_limit_bytes=56 * 2 ** 20),
        cost_estimate=pl.CostEstimate(flops=int(8e9), bytes_accessed=int(1e7), transcendentals=int(5e6)),
        name='attention_fwd',
    )(q_raw, k_raw, v_heads, inv_q, inv_k, gq, gk, cos_t, sin_t)


def bwd_kernel(q_ref, k_ref, v_ref, do_ref, lse_ref, cos_ref, sin_ref, dq_ref, dk_ref, dv_ref, kt_ref, dva_ref):
    seq_len = q_ref.shape[0]
    kt_ref[...] = k_ref[...].astype(jnp.float32).T.astype(jnp.bfloat16)
    dk_ref[...] = jnp.zeros_like(dk_ref)
    dva_ref[...] = jnp.zeros_like(dva_ref)
    for first in range(0, seq_len, Q_BLOCK):
        ext = first + Q_BLOCK
        q_blk, do_blk = q_ref[first:ext, :], do_ref[first:ext, :]
        scores = lax.dot_general(k_ref[:ext, :], q_blk, NT,
                                 preferred_element_type=jnp.float32) * (ATTN_SCALE * LOG2E)
        scores = causal_tile(scores, first)
        probs = jnp.exp2(scores - lse_ref[:, first:ext])
        d_probs = lax.dot_general(v_ref[:ext, :], do_blk, NT, preferred_element_type=jnp.float32)
        delta = jnp.sum(probs * d_probs, axis=0, keepdims=True)
        d_scores = (probs * (d_probs - delta) * ATTN_SCALE).astype(jnp.bfloat16)
        dva_ref[:ext, :] += lax.dot_general(probs.astype(jnp.bfloat16), do_blk, NN, preferred_element_type=jnp.float32)
        dk_ref[:ext, :] += lax.dot_general(d_scores, q_blk, NN, preferred_element_type=jnp.float32)
        dq_t = lax.dot_general(kt_ref[:, :ext], d_scores, NN, preferred_element_type=jnp.float32)
        dq = dq_t.T
        dq_ref[first:ext, :] = dq * cos_ref[first:ext, :] - pltpu.roll(dq, HEAD_SIZE // 2, 1) * sin_ref[first:ext, :]
    dk = dk_ref[...]
    dk_ref[...] = dk * cos_ref[...] - pltpu.roll(dk, HEAD_SIZE // 2, 1) * sin_ref[...]
    dv_ref[...] = dva_ref[...].astype(jnp.bfloat16)


def attention_bwd(q_rot, k_rot, v_heads, d_heads, lse, cos_t, sin_t):
    batch_size, seq_len, cols = q_rot.shape
    heads = cols // HEAD_SIZE
    head_spec = pl.BlockSpec((None, seq_len, HEAD_SIZE), lambda b, h: (b, 0, h))
    table_spec = pl.BlockSpec((seq_len, HEAD_SIZE), lambda b, h: (0, 0))
    lse_spec = pl.BlockSpec((None, None, 1, seq_len), lambda b, h: (b, h, 0, 0))
    return pl.pallas_call(
        bwd_kernel,
        grid=(batch_size, heads),
        in_specs=[head_spec, head_spec, head_spec, head_spec, lse_spec, table_spec, table_spec],
        out_specs=[head_spec, head_spec, head_spec],
        out_shape=[jax.ShapeDtypeStruct((batch_size, seq_len, cols), jnp.float32)] * 2
        + [jax.ShapeDtypeStruct((batch_size, seq_len, cols), jnp.bfloat16)],
        scratch_shapes=[pltpu.VMEM((HEAD_SIZE, seq_len), jnp.bfloat16), pltpu.VMEM((seq_len, HEAD_SIZE), jnp.float32)],
        compiler_params=pltpu.CompilerParams(dimension_semantics=('arbitrary', 'arbitrary'), vmem_limit_bytes=56 * 2 ** 20),
        cost_estimate=pl.CostEstimate(flops=int(2e10), bytes_accessed=int(1e7), transcendentals=int(5e6)),
        name='attention_bwd',
    )(q_rot, k_rot, v_heads, d_heads, lse, cos_t, sin_t)


COLUMN_PARTS = ((0, 1408), (1408, 2816), (2816, 4096))
AXIS_ORDERS = ((0, 1, 2), (1, 2, 0), (2, 0, 1))


def by_distance_kernel(tok, cols, dq_ref, dk_ref, dv_ref, *out_refs):
    me = lax.axis_index('tp')
    for b in range(2):
        for side in range(2):
            for chip in range(N_DEV // 2):
                owner = (2 * chip + 1 - side) ^ me
                rows = pl.ds(pl.multiple_of(owner * tok, tok), tok)
                for i, ref in enumerate((dq_ref, dk_ref, dv_ref)):
                    out_refs[2 * b + side][chip * tok:(chip + 1) * tok, i * cols:(i + 1) * cols] = ref[b, rows, :]


def by_distance(dq, dk, dv):
    _, seq_len, cols = dq.shape
    far_0, near_0, far_1, near_1 = pl.pallas_call(
        functools.partial(by_distance_kernel, seq_len // N_DEV, cols),
        in_specs=[vmem_spec()] * 3,
        out_specs=[vmem_spec()] * 4,
        out_shape=[jax.ShapeDtypeStruct((seq_len // 2, 3 * cols), jnp.bfloat16)] * 4,
        compiler_params=pltpu.CompilerParams(vmem_limit_bytes=40 * 2 ** 20),
        cost_estimate=pl.CostEstimate(flops=int(1e9), bytes_accessed=int(12e6), transcendentals=0),
        name='by_distance',
    )(dq, dk, dv)
    return (far_0, far_1), (near_0, near_1)


def flip(value, bit):
    return lax.ppermute(value, 'tp', [(i, i ^ bit) for i in range(N_DEV)])


def start_sums(far, near):
    shape = (2, 2, 2, near[0].shape[0] // 8)
    return [[n.reshape(shape + n.shape[1:]), flip(f, 1).reshape(shape + n.shape[1:])] for f, n in zip(far, near)]


def cross_axis(sums, stage):
    aways, kept = [], []
    for pieces, order in zip(sums, AXIS_ORDERS):
        axis = order[stage]
        away = sum(lax.slice_in_dim(p, 1, 2, axis=axis) for p in pieces)
        aways.append(away)
        came = flip(away, 8 >> axis)
        kept.append([sum(lax.slice_in_dim(p, 0, 1, axis=axis) for p in pieces), came])
    return kept, aways


def sums_after(sums, gate):
    flat = lax.optimization_barrier(tuple(p for pieces in sums for p in pieces) + tuple(gate))
    size = len(sums[0])
    return [list(flat[i * size:(i + 1) * size]) for i in range(len(sums))]


def finish_sums(sums):
    return jnp.concatenate([sum(pieces)[0, 0, 0] for pieces in sums], axis=-1)


def dot_f32(spec, lhs, rhs):
    return jnp.einsum(spec, lhs, rhs, preferred_element_type=jnp.float32)


def after(value, *others):
    return lax.optimization_barrier((value,) + others)[0]


def local_block(x_loc, wq_loc, wk_loc, wv_loc, wo_loc, gq_loc, gk_loc, g_attn, dy_loc):
    batch_size, seq_loc, model_dim = x_loc.shape
    seq_len = seq_loc * N_DEV
    cos_t, sin_t = rope_tables(seq_len)
    gq_row, gk_row = gq_loc[None, :], gk_loc[None, :]
    gq_f, gk_f = gq_row.astype(jnp.float32), gk_row.astype(jnp.float32)

    x_full = lax.all_gather(x_loc, 'tp', axis=1, tiled=True)
    wo_full = lax.all_gather(wo_loc, 'tp', axis=0, tiled=True)
    w_cat = jnp.concatenate([wq_loc, wk_loc, wv_loc], axis=1)
    x_full = after(x_full, w_cat)
    q_raw, k_raw = dot_f32('bsd,de->bse', x_full, wq_loc), dot_f32('bsd,de->bse', x_full, wk_loc)
    v_heads = dot_f32('bsd,de->bse', x_full, wv_loc).astype(jnp.bfloat16)
    part = jnp.stack([jnp.sum(q_raw * q_raw, axis=-1), jnp.sum(k_raw * k_raw, axis=-1)])
    sums = sum_devices(part.reshape(-1, 128)).reshape(2, batch_size, seq_len, 1)
    inv_q, inv_k = lax.rsqrt(sums / model_dim + NORM_EPS)
    heads_out, q_rot, k_rot, lse = attention_fwd(q_raw, k_raw, v_heads, inv_q, inv_k, gq_row, gk_row, cos_t, sin_t)

    o_loc = to_tokens(heads_out).reshape(-1, model_dim)
    attn_loc = dot_f32('te,ed->td', o_loc, wo_full)
    x_f = x_loc.reshape(-1, model_dim).astype(jnp.float32)
    dy_f = dy_loc.reshape(-1, model_dim).astype(jnp.float32)
    post_rms = lax.rsqrt(jnp.mean(attn_loc * attn_loc, axis=-1, keepdims=True) + NORM_EPS)
    normed = attn_loc * post_rms
    ga_f = g_attn.astype(jnp.float32)
    y_loc = (x_f + normed * ga_f).astype(jnp.bfloat16)

    ga_part = jnp.sum(dy_f * normed, axis=0)
    g_normed = dy_f * ga_f
    d_attn = (post_rms * (g_normed - normed * jnp.mean(g_normed * normed, axis=-1, keepdims=True))).astype(jnp.bfloat16)
    d_o_loc = dot_f32('td,ed->te', d_attn, wo_full).astype(jnp.bfloat16)
    d_heads = to_heads(d_o_loc.reshape(batch_size, seq_loc, model_dim))
    d_attn_full = lax.all_gather(d_attn.reshape(batch_size, seq_loc, model_dim), 'tp', axis=1, tiled=True)

    dq_hat, dk_hat, d_value = attention_bwd(q_rot, k_rot, v_heads, d_heads, lse, cos_t, sin_t)
    q_unit, k_unit = q_raw * inv_q, k_raw * inv_k
    dq_unit, dk_unit = dq_hat * gq_f, dk_hat * gk_f
    grad_gq = jnp.sum(dq_hat * q_unit, axis=(0, 1))
    grad_gk = jnp.sum(dk_hat * k_unit, axis=(0, 1))
    part = jnp.stack([jnp.sum(dq_unit * q_unit, axis=-1), jnp.sum(dk_unit * k_unit, axis=-1)])
    sums = sum_devices(jnp.concatenate([part.reshape(-1, 128), ga_part.reshape(-1, 128)]))
    n_rows = part.size // 128
    unit_dots = (sums[:n_rows] / model_dim).reshape(2, batch_size, seq_len, 1)
    grad_ga = sums[n_rows:].reshape(-1)
    dq_raw = (inv_q * (dq_unit - q_unit * unit_dots[0])).astype(jnp.bfloat16)
    dk_raw = (inv_k * (dk_unit - k_unit * unit_dots[1])).astype(jnp.bfloat16)
    far, near = by_distance(dq_raw, dk_raw, d_value)

    def parts_of(lhs):
        return [dot_f32('te,de->td', lhs, w_cat[lo:hi]) for lo, hi in COLUMN_PARTS]

    sums_0, gate = cross_axis(start_sums(parts_of(far[0]), parts_of(near[0])), 0)
    far_parts = parts_of(after(far[1], *gate))
    near_parts = parts_of(after(near[1], *far_parts))
    sums_1 = start_sums(far_parts, near_parts)
    x_early = after(x_full, *near_parts)
    grad_wq, grad_wk = [dot_f32('bsd,bse->de', x_early, cot).astype(jnp.bfloat16) for cot in (dq_raw, dk_raw)]
    sums_0, gate = cross_axis(sums_after(sums_0, [grad_wq, grad_wk]), 1)
    sums_1, gate = cross_axis(sums_after(sums_1, gate), 0)
    grad_wv = dot_f32('bsd,bse->de', after(x_full, *gate), d_value).astype(jnp.bfloat16)
    grad_wo = dot_f32('bse,bsd->ed', heads_out, after(d_attn_full, grad_wv)).astype(jnp.bfloat16)
    sums_1, gate = cross_axis(sums_after(sums_1, [grad_wo]), 1)
    sums_0, gate = cross_axis(sums_after(sums_0, gate), 2)
    sums_1, gate = cross_axis(sums_after(sums_1, gate), 2)
    dx_sums = (sums_after(sums_0, gate), sums_1)
    grad_x = jnp.stack([finish_sums(dx_sums[b]) + dy_loc[b].astype(jnp.float32) for b in range(batch_size)])
    return (y_loc.reshape(x_loc.shape), grad_x.astype(jnp.bfloat16), grad_wq, grad_wk, grad_wv, grad_wo,
            grad_gq.astype(jnp.bfloat16), grad_gk.astype(jnp.bfloat16), grad_ga.astype(jnp.bfloat16))


def solution(mesh):
    act_spec = P(None, 'tp', None)
    col_spec = P(None, 'tp')
    row_spec = P('tp', None)
    vec_spec = P('tp')
    in_specs = (act_spec, col_spec, col_spec, col_spec, row_spec, vec_spec, vec_spec, P(), act_spec)
    out_specs = (act_spec, act_spec, col_spec, col_spec, col_spec, row_spec, vec_spec, vec_spec, P())

    return jax.shard_map(local_block, mesh=mesh, in_specs=in_specs, out_specs=out_specs, check_vma=False)
```

time: 1160 us -> 818 us (0.71)
  waiting for transfers between devices: 509 us -> 233 us
  Pallas kernels: 347 us -> 183 us
  other arithmetic: 30.2 us -> 88.3 us
  starting transfers between devices: 0.27 us -> 22.4 us
  matrix products: 219 us -> 233 us
    all_gather x5 -> x1, waiting for transfers between devices: 382 us -> 122 us  [local_block(): x_full = lax.all_gather(x_loc, 'tp', axis=1, tiled=True)]
    pallas_call x7 -> x5, Pallas kernels: 300 us -> 141 us  [the longest x2 70.9 us: exchange(): pl.pallas_call(functools.partial(kernel, tok, cols), out_shape=jax.ShapeD...]
    all_gather x1, waiting for transfers between devices: 116 us -> 0.01 us  [local_block(): lax.all_gather(d_attn.reshape(batch_size, seq_loc, model_dim), 'tp', axis...]
    ppermute x0 -> x24, waiting for transfers between devices: none -> 110 us  [flip(): return lax.ppermute(value, 'tp', [(i, i ^ bit) for i in range(N_DEV)])]
    add x0 -> x18, other arithmetic: none -> 58.4 us  [the longest x9 34.8 us: cross_axis(): sum((lax.slice_in_dim(p, 0, 1, axis=axis) for p in pieces))]
    ppermute x0 -> x24, starting transfers between devices: none -> 22.3 us  [flip(): return lax.ppermute(value, 'tp', [(i, i ^ bit) for i in range(N_DEV)])]
    dot_general x19 -> x21, matrix products: 219 us -> 233 us  [dot_f32(): return jnp.einsum(spec, lhs, rhs, preferred_element_type=jnp.float32)]
    pallas_call x3 -> x2, Pallas kernels: 46.8 us -> 41.4 us  [sum_devices(): pl.pallas_call(sum_kernel, out_shape=jax.ShapeDtypeStruct(part.shape, jnp...]
  transfers between devices with their start and end apart: 7 -> 27, of which waited for: 6 -> 7; matrix products, arithmetic and copies ran while one was open for 22% -> 40% of each run, Pallas kernels for 30% -> 23%
where the time goes in v3:
time: 818 us; the launch traced here: 808 us
  waiting for transfers between devices  233 us (28%)
  matrix products  233 us (28%)
  Pallas kernels  183 us (22%)
  other arithmetic  88.3 us (11%)
  local copies, waits for them, and re-layouts  33.9 us (4%)
  starting transfers between devices  22.4 us (3%)
  between operations  14.8 us (2%)
    dot_general x21, matrix products, dot_f32(): return jnp.einsum(spec, lhs, rhs, preferred_element_type=jnp.float32)  233 us
    all_gather x1, waiting for transfers between devices, local_block(): x_full = lax.all_gather(x_loc, 'tp', axis=1, tiled=True)  122 us
    ppermute x24, waiting for transfers between devices, flip(): return lax.ppermute(value, 'tp', [(i, i ^ bit) for i in range(N_DEV)])  110 us
    pallas_call x2, Pallas kernels, exchange(): pl.pallas_call(functools.partial(kernel, tok, cols), out_shape=jax.ShapeD...  70.9 us
    pallas_call x2, Pallas kernels, sum_devices(): pl.pallas_call(sum_kernel, out_shape=jax.ShapeDtypeStruct(part.shape, jnp...  41.4 us
    pallas_call x1, Pallas kernels, attention_bwd(): pl.pallas_call(bwd_kernel, grid=(batch_size, heads), in_specs=[head_spec,...  35.9 us
    add x9, other arithmetic, cross_axis(): sum((lax.slice_in_dim(p, 0, 1, axis=axis) for p in pieces))  34.8 us
    pallas_call x1, Pallas kernels, attention_fwd(): pl.pallas_call(fwd_kernel, grid=(batch_size, heads), in_specs=[head_spec,...  34 us
  transfers between devices with their start and end apart: 27, of which 7 were waited for; matrix products, arithmetic and copies ran while one was open for 40% of the time, Pallas kernels for 23%

profile of v3, /device:TPU:0, one launch (start us, length us, event | category | flops | bytes accessed | tf_op | source)
XLA Modules:
  0.0 808.1 jit_solution(3476339616180494517)
XLA Ops:
  9.9 3.9 fusion.44
  22.4 122.1 %all-gather.4.cloned.1.call-done = bf16[2,2048,4096]{2,1,0:T(8,128)(2,1)} async-done(((bf16[2,128,4096]{2,1,0:T(8,128)(2,1)}), bf16[2,2048,4096]{2,1,0:T(8,128)(2,1)}) %all-gather.4.cloned.1.call-update) | async-done | bytes 33554448 | tf_op jit(solution)/shard_map/all_gather | solution.py:299
  144.5 18.6 %multiply_reduce_fusion.6 = (f32[2,2048]{1,0:T(2,128)S(1)}, f32[2,2048,256]{1,2,0:T(8,128)}) fusion(bf16[2,2048,4096]{2,1,0:T(8,128)(2,1)} %all-gather.4.cloned.1.call-done, bf16[4096,256]{1,0:T(8,128)(2,1)S(1)} %copy-done.15), kind=kOutput, calls=%fused_computation.27 | convolution fusion | flops 8592027648 | bytes 39862272 | tf_op jit(solution)/shard_map/bsd,de->bse/dot_general | solution.py:285
  163.2 17.2 %multiply_reduce_fusion.5 = (f32[2,2048]{1,0:T(2,128)S(1)}, f32[2,2048,256]{1,2,0:T(8,128)}) fusion(bf16[2,2048,4096]{2,1,0:T(8,128)(2,1)} %all-gather.4.cloned.1.call-done, bf16[4096,256]{1,0:T(8,128)(2,1)} %param.11), kind=kOutput, calls=%fused_computation.26 | convolution fusion | flops 8592027648 | bytes 39862272 | tf_op jit(solution)/shard_map/bsd,de->bse/dot_general | solution.py:285
  181.0 17.7 %sum_devices.2 = f32[64,128]{1,0:T(8,128)} custom-call(f32[64,128]{1,0:T(8,128)} %reshape.203.part_ref), custom_call_target="tpu_custom_call" | custom-call | flops 1000000000 | bytes 1000000 | tf_op jit(solution)/shard_map/sum_devices/pallas_call | solution.py:55
  206.1 5.3 copy.20.q_ref
  211.5 5.5 copy.21.k_ref
  217.0 22.2 %convolution_convert_fusion.1.v_ref = bf16[2,2048,256]{2,1,0:T(8,128)(2,1)} fusion(bf16[2,2048,4096]{2,1,0:T(8,128)(2,1)} %all-gather.4.cloned.1.call-done, bf16[4096,256]{1,0:T(8,128)(2,1)S(1)} %copy-done.18), kind=kOutput, calls=%fused_computation.28 | convolution fusion | flops 8590983168 | bytes 37748736 | tf_op jit(solution)/shard_map/bsd,de->bse/dot_general | solution.py:285
  239.2 34.0 %attention_fwd.1 = (bf16[2,2048,256]{2,1,0:T(8,128)(2,1)}, bf16[2,2048,256]{2,1,0:T(8,128)(2,1)}, bf16[2,2048,256]{2,1,0:T(8,128)(2,1)}, f32[2,2,1,2048]{3,2,1,0:T(1,128)}) custom-call(f32[2,2048,256]{2,1,0:T(8,128)} %copy.20.q_ref, f32[2,2048,256]{2,1,0:T(8,128)} %copy.21.k_ref, bf16[2,2048,256]{2,1,0:T(8,128)(2,1)} %convolution_convert_fusion.1.v_ref, ...), custom_call_target="tpu_custom_call" | custom-call | flops 8000000000 | bytes 10000000 | tf_op jit(solution)/shard_map/attention_fwd/pallas_call | solution.py:166
  273.2 33.3 %shard_map.160 = bf16[2,128,4096]{2,1,0:T(8,128)(2,1)} custom-call(bf16[2,2048,256]{2,1,0:T(8,128)(2,1)} %get-tuple-element.63.in_ref), custom_call_target="tpu_custom_call" | custom-call | flops 10000000000 | bytes 8000000 | tf_op jit(solution)/shard_map/pallas_call | solution.py:103
  306.5 16.0 %multiply_reduce_fusion.4 = (f32[256]{0:T(256)S(1)}, f32[256,4096]{1,0:T(8,128)S(1)}) fusion(bf16[256,4096]{1,0:T(8,128)(2,1)} %bitcast.119, bf16[4096,4096]{1,0:T(8,128)(2,1)} %all-gather.6.cloned.1.call-done), kind=kOutput, calls=%fused_computation.25 | convolution fusion | flops 8592031744 | bytes 39846912 | tf_op jit(solution)/shard_map/te,ed->td/dot_general | solution.py:285
  324.3 4.2 fusion.8
  328.6 18.4 %convolution_convert_fusion = bf16[256,4096]{1,0:T(8,128)(2,1)} fusion(bf16[256,4096]{1,0:T(8,128)(2,1)} %get-tuple-element.145, bf16[4096,4096]{1,0:T(8,128)(2,1)} %all-gather.6.cloned.1.call-done), kind=kOutput, calls=%fused_computation.10 | convolution fusion | flops 8590983168 | bytes 37748736 | tf_op jit(solution)/shard_map/td,ed->te/dot_general | solution.py:285
  347.1 37.6 %shard_map.161.do_ref = bf16[2,2048,256]{2,1,0:T(8,128)(2,1)} custom-call(bf16[2,128,4096]{2,1,0:T(8,128)(2,1)} %bitcast.120), custom_call_target="tpu_custom_call" | custom-call | flops 10000000000 | bytes 8000000 | tf_op jit(solution)/shard_map/pallas_call | solution.py:103
  384.7 35.9 %attention_bwd.1 = (f32[2,2048,256]{2,1,0:T(8,128)}, f32[2,2048,256]{2,1,0:T(8,128)}, bf16[2,2048,256]{2,1,0:T(8,128)(2,1)}) custom-call(bf16[2,2048,256]{2,1,0:T(8,128)(2,1)} %get-tuple-element.64.q_ref, bf16[2,2048,256]{2,1,0:T(8,128)(2,1)} %get-tuple-element.65.k_ref, bf16[2,2048,256]{2,1,0:T(8,128)(2,1)} %convolution_convert_fusion.1.v_ref, ...), custom_call_target="tpu_custom_call" | custom-call | flops 20000000000 | bytes 10000000 | tf_op jit(solution)/shard_map/attention_bwd/pallas_call | solution.py:211
  420.6 4.9 multiply_reduce_fusion.1
  431.7 23.7 %sum_devices.3 = f32[96,128]{1,0:T(8,128)} custom-call(f32[96,128]{1,0:T(8,128)} %pad_maximum_fusion.3.part_ref), custom_call_target="tpu_custom_call" | custom-call | flops 1000000000 | bytes 1000000 | tf_op jit(solution)/shard_map/sum_devices/pallas_call | solution.py:55
  456.2 4.7 multiply_convert_fusion.dk_ref
  470.8 6.1 fusion.22
  476.9 6.0 fusion.30
  484.7 6.1 fusion.40
  490.8 6.0 fusion.24
  496.9 6.1 fusion.32
  503.0 7.0 slice_add_fusion.9
  511.1 6.6 slice_add_fusion.1
  519.1 6.0 slice_add_fusion.3
  525.5 6.2 fusion.36
  531.6 6.0 fusion.20
  538.2 6.0 fusion.28
  544.2 6.1 fusion.34
  550.3 6.0 fusion.18
  556.3 6.2 fusion.26
  562.5 6.7 collective-permute-done.5
  569.1 17.6 %fusion.2 = bf16[4096,256]{1,0:T(8,128)(2,1)} fusion(bf16[2,2048,4096]{2,1,0:T(8,128)(2,1)} %all-gather.4.cloned.1.call-done, bf16[2,2048,256]{2,1,0:T(8,128)(2,1)S(1)} %multiply_convert_fusion.dk_ref), kind=kOutput, calls=%fused_computation.8 | convolution fusion | flops 8590983168 | bytes 37748736 | tf_op jit(solution)/shard_map/bsd,bse->de/dot_general | solution.py:285
  586.7 17.6 %fusion.1 = bf16[4096,256]{1,0:T(8,128)(2,1)} fusion(bf16[2,2048,4096]{2,1,0:T(8,128)(2,1)} %all-gather.4.cloned.1.call-done, bf16[2,2048,256]{2,1,0:T(8,128)(2,1)S(1)} %multiply_convert_fusion.1.dq_ref), kind=kOutput, calls=%fused_computation.7 | convolution fusion | flops 8590983168 | bytes 37748736 | tf_op jit(solution)/shard_map/bsd,bse->de/dot_general | solution.py:285
  604.4 4.3 slice_add_fusion.23
  610.1 4.0 slice_add_fusion.17
  615.2 3.9 slice_add_fusion.19
  619.1 6.0 slice_add_fusion.10
  626.1 5.0 slice_add_fusion.4
  632.6 6.0 slice_add_fusion.6
  639.2 17.4 %fusion.3 = bf16[4096,256]{1,0:T(8,128)(2,1)} fusion(bf16[2,2048,4096]{2,1,0:T(8,128)(2,1)} %all-gather.4.cloned.1.call-done, bf16[2,2048,256]{2,1,0:T(8,128)(2,1)S(1)} %copy-done), kind=kOutput, calls=%fused_computation.9 | convolution fusion | flops 8590983168 | bytes 37748736 | tf_op jit(solution)/shard_map/bsd,bse->de/dot_general | solution.py:285
  656.6 17.0 %fusion = bf16[256,4096]{1,0:T(8,128)(2,1)} fusion(bf16[2,2048,256]{2,1,0:T(8,128)(2,1)} %get-tuple-element.63.in_ref, bf16[2,2048,4096]{2,1,0:T(8,128)(2,1)} %all-gather.8.cloned.1.call-done), kind=kOutput, calls=%fused_computation.6 | convolution fusion | flops 8590983168 | bytes 37748736 | tf_op jit(solution)/shard_map/bse,bsd->ed/dot_general | solution.py:285
  673.7 30.6 %collective-permute-done.14 = f32[2,2,1,128,1280]{4,3,2,1,0:T(8,128)} collective-permute-done((f32[2,2,1,128,1280]{4,3,2,1,0:T(8,128)}, f32[2,2,1,128,1280]{4,3,2,1,0:T(8,128)}, u32[]{:S(2)}, u32[]{:S(2)}) %collective-permute-start.14) | collective-permute-done | bytes 2621472 | tf_op jit(solution)/shard_map/ppermute | solution.py:255
  714.7 24.1 %collective-permute-done.6 = f32[1,1,2,128,1408]{4,3,2,1,0:T(8,128)S(1)} collective-permute-done((f32[1,1,2,128,1408]{4,3,2,1,0:T(8,128)S(1)}, f32[1,1,2,128,1408]{4,3,2,1,0:T(8,128)S(1)}, u32[]{:S(2)}, u32[]{:S(2)}) %collective-permute-start.6) | collective-permute-done | bytes 1441824 | tf_op jit(solution)/shard_map/ppermute | solution.py:255
  745.1 24.5 %collective-permute-done.18 = f32[1,1,2,128,1408]{4,3,2,1,0:T(8,128)S(1)} collective-permute-done((f32[1,1,2,128,1408]{4,3,2,1,0:T(8,128)S(1)}, f32[1,1,2,128,1408]{4,3,2,1,0:T(8,128)S(1)}, u32[]{:S(2)}, u32[]{:S(2)}) %collective-permute-start.18) | collective-permute-done | bytes 1441824 | tf_op jit(solution)/shard_map/ppermute | solution.py:255
  771.8 10.3 %collective-permute-done.17 = f32[1,1,1,128,1280]{4,3,2,1,0:T(8,128)S(1)} collective-permute-done((f32[1,1,1,128,1280]{4,3,2,1,0:T(8,128)S(1)}, f32[1,1,1,128,1280]{4,3,2,1,0:T(8,128)S(1)}, u32[]{:S(2)}, u32[]{:S(2)}) %collective-permute-start.17) | collective-permute-done | bytes 655392 | tf_op jit(solution)/shard_map/ppermute | solution.py:255
  783.8 13.5 %collective-permute-done.23 = f32[1,1,1,128,1280]{4,3,2,1,0:T(8,128)S(1)} collective-permute-done((f32[1,1,1,128,1280]{4,3,2,1,0:T(8,128)S(1)}, f32[1,1,1,128,1280]{4,3,2,1,0:T(8,128)S(1)}, u32[]{:S(2)}, u32[]{:S(2)}) %collective-permute-start.23) | collective-permute-done | bytes 655392 | tf_op jit(solution)/shard_map/ppermute | solution.py:255
  (161 shorter events, 73.0 us)
Async XLA Ops:
  7.2 137.3 %all-gather.4.cloned.1.call-start = ((), (), s32[]{:S(2)}) async-start(), calls=%async_computation | async-start | bytes 35651584 | tf_op jit(solution)/shard_map/all_gather | solution.py:299
  7.9 298.6 %all-gather.6.cloned.1.call-start = ((), (), s32[]{:S(2)}) async-start(), calls=%async_computation.1 | async-start | bytes 35651584 | tf_op jit(solution)/shard_map/all_gather | solution.py:300
  8.7 647.9 %all-gather.8.cloned.1.call-start = ((), (), s32[]{:S(2)}) async-start(), calls=%async_computation.2 | async-start | bytes 35651584 | tf_op jit(solution)/shard_map/all_gather | solution.py:324
  18.1 2.7 copy-start.17
  211.4 5.5 copy-start.18
  306.5 16.1 %copy-start.4 = (bf16[2,128,4096]{2,1,0:T(8,128)(2,1)S(1)}, bf16[2,128,4096]{2,1,0:T(8,128)(2,1)}, u32[]{:S(2)}) copy-start(bf16[2,128,4096]{2,1,0:T(8,128)(2,1)} %param.17) | copy-start | bytes 6291460
  384.7 35.9 %copy-start.1 = (f32[2,2048,256]{2,1,0:T(8,128)S(1)}, f32[2,2048,256]{2,1,0:T(8,128)}, u32[]{:S(2)}) copy-start(f32[2,2048,256]{2,1,0:T(8,128)} %copy.20.q_ref) | copy-start | bytes 12582916
  420.6 6.0 copy-start.3
  420.6 8.3 %copy-start.7 = (f32[2,2048,256]{2,1,0:T(8,128)S(1)}, f32[2,2048,256]{2,1,0:T(8,128)}, u32[]{:S(2)}) copy-start(f32[2,2048,256]{2,1,0:T(8,128)} %get-tuple-element.68) | copy-start | bytes 12582916
  456.2 4.8 copy-start.2
  456.2 6.5 copy-start.6
  468.5 34.5 %collective-permute-start.4 = (f32[1024,1280]{1,0:T(8,128)S(1)}, f32[1024,1280]{1,0:T(8,128)}, u32[]{:S(2)}, u32[]{:S(2)}) collective-permute-start(f32[1024,1280]{1,0:T(8,128)S(1)} %fusion.38), channel_id=1, source_target_pairs={{0,1},{1,0},{2,3},{3,2},{4,5},{5,4},{6,7},{7,6},{8,9},{9,8},{10,11... | collective-permute-start | bytes 15728648 | tf_op jit(solution)/shard_map/ppermute | solution.py:255
  476.8 34.3 %collective-permute-start.2 = (f32[1024,1408]{1,0:T(8,128)}, f32[1024,1408]{1,0:T(8,128)}, u32[]{:S(2)}, u32[]{:S(2)}) collective-permute-start(f32[1024,1408]{1,0:T(8,128)} %fusion.22), channel_id=1, source_target_pairs={{0,1},{1,0},{2,3},{3,2},{4,5},{5,4},{6,7},{7,6},{8,9},{9,8},{10,11... | collective-permute-start | bytes 17301512 | tf_op jit(solution)/shard_map/ppermute | solution.py:255
  482.9 36.2 %collective-permute-start = (f32[1024,1408]{1,0:T(8,128)}, f32[1024,1408]{1,0:T(8,128)S(1)}, u32[]{:S(2)}, u32[]{:S(2)}) collective-permute-start(f32[1024,1408]{1,0:T(8,128)} %fusion.30), channel_id=1, source_target_pairs={{0,1},{1,0},{2,3},{3,2},{4,5},{5,4},{6,7},{7,6},{8,9},{9,8},{10,11... | collective-permute-start | bytes 17301512 | tf_op jit(solution)/shard_map/ppermute | solution.py:255
  510.0 59.1 %collective-permute-start.5 = (f32[2,2,1,128,1280]{4,3,2,1,0:T(8,128)}, f32[2,2,1,128,1280]{4,3,2,1,0:T(8,128)}, u32[]{:S(2)}, u32[]{:S(2)}) collective-permute-start(f32[2,2,1,128,1280]{4,3,2,1,0:T(8,128)} %get-tuple-element.132), channel_id=1, source_target_pairs={{0,2},{1,3},{2,0},{3,1},{4,6},{5,7},{6,4},{7,5},{8,10},{9,11},{10,... | collective-permute-start | bytes 7864328 | tf_op jit(solution)/shard_map/ppermute | solution.py:255
  517.7 86.7 %collective-permute-start.3 = (f32[2,1,2,128,1408]{4,3,2,1,0:T(8,128)}, f32[2,1,2,128,1408]{4,3,2,1,0:T(8,128)}, u32[]{:S(2)}, u32[]{:S(2)}) collective-permute-start(f32[2,1,2,128,1408]{4,3,2,1,0:T(8,128)} %get-tuple-element.126), channel_id=1, source_target_pairs={{0,4},{1,5},{2,6},{3,7},{4,0},{5,1},{6,2},{7,3},{8,12},{9,13},{10,... | collective-permute-start | bytes 8650760 | tf_op jit(solution)/shard_map/ppermute | solution.py:255
  525.1 79.3 %collective-permute-start.1 = (f32[1,2,2,128,1408]{4,3,2,1,0:T(8,128)}, f32[1,2,2,128,1408]{4,3,2,1,0:T(8,128)}, u32[]{:S(2)}, u32[]{:S(2)}) collective-permute-start(f32[1,2,2,128,1408]{4,3,2,1,0:T(8,128)} %bitcast.112), channel_id=1, source_target_pairs={{0,8},{1,9},{2,10},{3,11},{4,12},{5,13},{6,14},{7,15},{8,0},{9,1},... | collective-permute-start | bytes 8650760 | tf_op jit(solution)/shard_map/ppermute | solution.py:255
  531.6 87.4 %collective-permute-start.11 = (f32[1024,1280]{1,0:T(8,128)}, f32[1024,1280]{1,0:T(8,128)}, u32[]{:S(2)}, u32[]{:S(2)}) collective-permute-start(f32[1024,1280]{1,0:T(8,128)} %fusion.36), channel_id=1, source_target_pairs={{0,1},{1,0},{2,3},{3,2},{4,5},{5,4},{6,7},{7,6},{8,9},{9,8},{10,11... | collective-permute-start | bytes 15728648 | tf_op jit(solution)/shard_map/ppermute | solution.py:255
  537.7 81.4 %collective-permute-start.10 = (f32[1024,1408]{1,0:T(8,128)}, f32[1024,1408]{1,0:T(8,128)}, u32[]{:S(2)}, u32[]{:S(2)}) collective-permute-start(f32[1024,1408]{1,0:T(8,128)} %fusion.20), channel_id=1, source_target_pairs={{0,1},{1,0},{2,3},{3,2},{4,5},{5,4},{6,7},{7,6},{8,9},{9,8},{10,11... | collective-permute-start | bytes 17301512 | tf_op jit(solution)/shard_map/ppermute | solution.py:255
  569.1 49.9 %collective-permute-start.9 = (f32[1024,1408]{1,0:T(8,128)}, f32[1024,1408]{1,0:T(8,128)}, u32[]{:S(2)}, u32[]{:S(2)}) collective-permute-start(f32[1024,1408]{1,0:T(8,128)} %fusion.28), channel_id=1, source_target_pairs={{0,1},{1,0},{2,3},{3,2},{4,5},{5,4},{6,7},{7,6},{8,9},{9,8},{10,11... | collective-permute-start | bytes 17301512 | tf_op jit(solution)/shard_map/ppermute | solution.py:255
  608.7 6.5 copy-start.8
  608.7 105.1 %collective-permute-start.8 = (f32[1,2,1,128,1280]{4,3,2,1,0:T(8,128)}, f32[1,2,1,128,1280]{4,3,2,1,0:T(8,128)}, u32[]{:S(2)}, u32[]{:S(2)}) collective-permute-start(f32[1,2,1,128,1280]{4,3,2,1,0:T(8,128)} %get-tuple-element.142), channel_id=1, source_target_pairs={{0,8},{1,9},{2,10},{3,11},{4,12},{5,13},{6,14},{7,15},{8,0},{9,1},... | collective-permute-start | bytes 3932168 | tf_op jit(solution)/shard_map/ppermute | solution.py:255
  610.1 9.0 %slice-start.4 = ((s8[5242880]{0:T(1024)(128)(4,1)}), s8[4194304]{0:T(1024)(128)(4,1)S(1)}, s32[]{:S(2)}) async-start(s8[5242880]{0:T(1024)(128)(4,1)} %bitcast.108), calls=%async_computation.7 | async-start | bytes 8388608
  614.1 5.0 slice-start.5
  614.1 100.6 %collective-permute-start.7 = (f32[2,1,1,128,1408]{4,3,2,1,0:T(8,128)}, f32[2,1,1,128,1408]{4,3,2,1,0:T(8,128)}, u32[]{:S(2)}, u32[]{:S(2)}) collective-permute-start(f32[2,1,1,128,1408]{4,3,2,1,0:T(8,128)} %get-tuple-element.134), channel_id=1, source_target_pairs={{0,2},{1,3},{2,0},{3,1},{4,6},{5,7},{6,4},{7,5},{8,10},{9,11},{10,... | collective-permute-start | bytes 4325384 | tf_op jit(solution)/shard_map/ppermute | solution.py:255
  619.1 7.0 slice-start.2
  619.1 7.0 slice-start.3
  619.1 13.4 %slice-start = ((s8[5767168]{0:T(1024)(128)(4,1)}), s8[4194304]{0:T(1024)(128)(4,1)S(1)}, s32[]{:S(2)}) async-start(s8[5767168]{0:T(1024)(128)(4,1)} %bitcast.101), calls=%async_computation.3 | async-start | bytes 8388608
  625.2 7.4 slice-start.1
  625.2 79.1 %collective-permute-start.14 = (f32[2,2,1,128,1280]{4,3,2,1,0:T(8,128)}, f32[2,2,1,128,1280]{4,3,2,1,0:T(8,128)}, u32[]{:S(2)}, u32[]{:S(2)}) collective-permute-start(f32[2,2,1,128,1280]{4,3,2,1,0:T(8,128)} %get-tuple-element.129), channel_id=1, source_target_pairs={{0,2},{1,3},{2,0},{3,1},{4,6},{5,7},{6,4},{7,5},{8,10},{9,11},{10,... | collective-permute-start | bytes 7864328 | tf_op jit(solution)/shard_map/ppermute | solution.py:255
  631.1 74.7 %collective-permute-start.13 = (f32[2,1,2,128,1408]{4,3,2,1,0:T(8,128)}, f32[2,1,2,128,1408]{4,3,2,1,0:T(8,128)}, u32[]{:S(2)}, u32[]{:S(2)}) collective-permute-start(f32[2,1,2,128,1408]{4,3,2,1,0:T(8,128)} %get-tuple-element.121), channel_id=1, source_target_pairs={{0,4},{1,5},{2,6},{3,7},{4,0},{5,1},{6,2},{7,3},{8,12},{9,13},{10,... | collective-permute-start | bytes 8650760 | tf_op jit(solution)/shard_map/ppermute | solution.py:255
  638.5 67.2 %collective-permute-start.12 = (f32[1,2,2,128,1408]{4,3,2,1,0:T(8,128)}, f32[1,2,2,128,1408]{4,3,2,1,0:T(8,128)}, u32[]{:S(2)}, u32[]{:S(2)}) collective-permute-start(f32[1,2,2,128,1408]{4,3,2,1,0:T(8,128)} %get-tuple-element.123), channel_id=1, source_target_pairs={{0,8},{1,9},{2,10},{3,11},{4,12},{5,13},{6,14},{7,15},{8,0},{9,1},... | collective-permute-start | bytes 8650760 | tf_op jit(solution)/shard_map/ppermute | solution.py:255
  656.6 47.6 %copy-start.19 = (f32[1,1,2,128,1408]{4,3,2,1,0:T(8,128)S(1)}, f32[1,1,2,128,1408]{4,3,2,1,0:T(8,128)}, u32[]{:S(2)}) copy-start(f32[1,1,2,128,1408]{4,3,2,1,0:T(8,128)} %get-tuple-element.136) | copy-start | bytes 4325380
  656.6 49.1 %copy-start.10 = (f32[2,2,1,128,1280]{4,3,2,1,0:T(8,128)S(1)}, f32[2,2,1,128,1280]{4,3,2,1,0:T(8,128)}, u32[]{:S(2)}) copy-start(f32[2,2,1,128,1280]{4,3,2,1,0:T(8,128)} %get-tuple-element.95) | copy-start | bytes 7864324
  704.3 34.5 %collective-permute-start.6 = (f32[1,1,2,128,1408]{4,3,2,1,0:T(8,128)S(1)}, f32[1,1,2,128,1408]{4,3,2,1,0:T(8,128)S(1)}, u32[]{:S(2)}, u32[]{:S(2)}) collective-permute-start(f32[1,1,2,128,1408]{4,3,2,1,0:T(8,128)S(1)} %copy-done.19), channel_id=1, source_target_pairs={{0,4},{1,5},{2,6},{3,7},{4,0},{5,1},{6,2},{7,3},{8,12},{9,13},{10,... | collective-permute-start | bytes 4325384 | tf_op jit(solution)/shard_map/ppermute | solution.py:255
  707.8 3.9 copy-start.9
  707.8 36.3 %collective-permute-start.20 = (f32[1,2,1,128,1280]{4,3,2,1,0:T(8,128)S(1)}, f32[1,2,1,128,1280]{4,3,2,1,0:T(8,128)S(1)}, u32[]{:S(2)}, u32[]{:S(2)}) collective-permute-start(f32[1,2,1,128,1280]{4,3,2,1,0:T(8,128)S(1)} %get-tuple-element.143), channel_id=1, source_target_pairs={{0,8},{1,9},{2,10},{3,11},{4,12},{5,13},{6,14},{7,15},{8,0},{9,1},... | collective-permute-start | bytes 3932168 | tf_op jit(solution)/shard_map/ppermute | solution.py:255
  710.8 28.0 %copy-start.14 = (f32[1,2,1,128,1280]{4,3,2,1,0:T(8,128)S(1)}, f32[1,2,1,128,1280]{4,3,2,1,0:T(8,128)}, u32[]{:S(2)}) copy-start(f32[1,2,1,128,1280]{4,3,2,1,0:T(8,128)} %get-tuple-element.101) | copy-start | bytes 3932164
  710.8 34.4 %collective-permute-start.19 = (f32[2,1,1,128,1408]{4,3,2,1,0:T(8,128)S(1)}, f32[2,1,1,128,1408]{4,3,2,1,0:T(8,128)S(1)}, u32[]{:S(2)}, u32[]{:S(2)}) collective-permute-start(f32[2,1,1,128,1408]{4,3,2,1,0:T(8,128)S(1)} %get-tuple-element.137), channel_id=1, source_target_pairs={{0,2},{1,3},{2,0},{3,1},{4,6},{5,7},{6,4},{7,5},{8,10},{9,11},{10,... | collective-permute-start | bytes 4325384 | tf_op jit(solution)/shard_map/ppermute | solution.py:255
  713.8 27.9 %copy-start.12 = (f32[2,1,1,128,1408]{4,3,2,1,0:T(8,128)S(1)}, f32[2,1,1,128,1408]{4,3,2,1,0:T(8,128)}, u32[]{:S(2)}) copy-start(f32[2,1,1,128,1408]{4,3,2,1,0:T(8,128)} %get-tuple-element.99) | copy-start | bytes 4325380
  713.8 55.8 %collective-permute-start.18 = (f32[1,1,2,128,1408]{4,3,2,1,0:T(8,128)S(1)}, f32[1,1,2,128,1408]{4,3,2,1,0:T(8,128)S(1)}, u32[]{:S(2)}, u32[]{:S(2)}) collective-permute-start(f32[1,1,2,128,1408]{4,3,2,1,0:T(8,128)S(1)} %get-tuple-element.139), channel_id=1, source_target_pairs={{0,4},{1,5},{2,6},{3,7},{4,0},{5,1},{6,2},{7,3},{8,12},{9,13},{10,... | collective-permute-start | bytes 4325384 | tf_op jit(solution)/shard_map/ppermute | solution.py:255
  740.2 3.8 copy-start.13
  740.2 41.9 %collective-permute-start.17 = (f32[1,1,1,128,1280]{4,3,2,1,0:T(8,128)S(1)}, f32[1,1,1,128,1280]{4,3,2,1,0:T(8,128)S(1)}, u32[]{:S(2)}, u32[]{:S(2)}) collective-permute-start(f32[1,1,1,128,1280]{4,3,2,1,0:T(8,128)S(1)} %get-tuple-element.152), channel_id=1, source_target_pairs={{0,4},{1,5},{2,6},{3,7},{4,0},{5,1},{6,2},{7,3},{8,12},{9,13},{10,... | collective-permute-start | bytes 1966088 | tf_op jit(solution)/shard_map/ppermute | solution.py:255
  743.2 40.4 %collective-permute-start.16 = (f32[1,1,1,128,1408]{4,3,2,1,0:T(8,128)S(1)}, f32[1,1,1,128,1408]{4,3,2,1,0:T(8,128)S(1)}, u32[]{:S(2)}, u32[]{:S(2)}) collective-permute-start(f32[1,1,1,128,1408]{4,3,2,1,0:T(8,128)S(1)} %get-tuple-element.148), channel_id=1, source_target_pairs={{0,8},{1,9},{2,10},{3,11},{4,12},{5,13},{6,14},{7,15},{8,0},{9,1},... | collective-permute-start | bytes 2162696 | tf_op jit(solution)/shard_map/ppermute | solution.py:255
  744.1 39.5 %collective-permute-start.15 = (f32[1,1,1,128,1408]{4,3,2,1,0:T(8,128)S(1)}, f32[1,1,1,128,1408]{4,3,2,1,0:T(8,128)S(1)}, u32[]{:S(2)}, u32[]{:S(2)}) collective-permute-start(f32[1,1,1,128,1408]{4,3,2,1,0:T(8,128)S(1)} %get-tuple-element.150), channel_id=1, source_target_pairs={{0,2},{1,3},{2,0},{3,1},{4,6},{5,7},{6,4},{7,5},{8,10},{9,11},{10,... | collective-permute-start | bytes 2162696 | tf_op jit(solution)/shard_map/ppermute | solution.py:255
  769.7 27.7 %collective-permute-start.21 = (f32[1,1,1,128,1408]{4,3,2,1,0:T(8,128)S(1)}, f32[1,1,1,128,1408]{4,3,2,1,0:T(8,128)S(1)}, u32[]{:S(2)}, u32[]{:S(2)}) collective-permute-start(f32[1,1,1,128,1408]{4,3,2,1,0:T(8,128)S(1)} %slice_add_fusion.25), channel_id=1, source_target_pairs={{0,2},{1,3},{2,0},{3,1},{4,6},{5,7},{6,4},{7,5},{8,10},{9,11},{10,... | collective-permute-start | bytes 2162696 | tf_op jit(solution)/shard_map/ppermute | solution.py:255
  771.0 26.6 %collective-permute-start.22 = (f32[1,1,1,128,1408]{4,3,2,1,0:T(8,128)S(1)}, f32[1,1,1,128,1408]{4,3,2,1,0:T(8,128)S(1)}, u32[]{:S(2)}, u32[]{:S(2)}) collective-permute-start(f32[1,1,1,128,1408]{4,3,2,1,0:T(8,128)S(1)} %slice_add_fusion.24), channel_id=1, source_target_pairs={{0,8},{1,9},{2,10},{3,11},{4,12},{5,13},{6,14},{7,15},{8,0},{9,1},... | collective-permute-start | bytes 2162696 | tf_op jit(solution)/shard_map/ppermute | solution.py:255
  782.1 15.2 %collective-permute-start.23 = (f32[1,1,1,128,1280]{4,3,2,1,0:T(8,128)S(1)}, f32[1,1,1,128,1280]{4,3,2,1,0:T(8,128)S(1)}, u32[]{:S(2)}, u32[]{:S(2)}) collective-permute-start(f32[1,1,1,128,1280]{4,3,2,1,0:T(8,128)S(1)} %slice_add_fusion.30), channel_id=1, source_target_pairs={{0,4},{1,5},{2,6},{3,7},{4,0},{5,1},{6,2},{7,3},{8,12},{9,13},{10,... | collective-permute-start | bytes 1966088 | tf_op jit(solution)/shard_map/ppermute | solution.py:255
  (8 other events, 15.6 us)
Sparse Core Ops, SparseCore 0:
  10.3 134.2 all-gather.3
  146.8 136.8 all-gather.5
  328.7 166.8 all-gather.7

commit v4 on v3

--- a/solution.py
+++ b/solution.py
@@ -32,37 +32,49 @@
     return pl.BlockSpec(memory_space=pltpu.VMEM)
 
 
-def sum_kernel(part_ref, out_ref, slots, send_sems, recv_sems):
+def sum_kernel(part_ref, out_ref, slots, own_sum, send_sems, recv_sems):
     me = lax.axis_index('tp')
     copies = []
     for step in range(1, N_DEV):
         peer = lax.rem(me + step, N_DEV)
         copy = pltpu.make_async_remote_copy(
-            src_ref=part_ref, dst_ref=slots.at[step], send_sem=send_sems.at[step], recv_sem=recv_sems.at[step],
-            device_id=(peer,), device_id_type=pl.DeviceIdType.MESH)
+            src_ref=part_ref.at[peer], dst_ref=slots.at[step], send_sem=send_sems.at[0, step],
+            recv_sem=recv_sems.at[0, step], device_id=(peer,), device_id_type=pl.DeviceIdType.MESH)
         copy.start()
         copies.append(copy)
-    slots[0] = part_ref[...]
+    slots[0] = part_ref[me]
     for copy in copies:
         copy.wait()
-    total = jnp.zeros(part_ref.shape, jnp.float32)
-    for owner in range(N_DEV):
-        total = total + slots[lax.rem(me - owner + N_DEV, N_DEV)]
-    out_ref[...] = total
+    total = slots[0]
+    for step in range(1, N_DEV):
+        total = total + slots[step]
+    own_sum[...] = total
+    out_ref[me] = total
+    copies = []
+    for step in range(1, N_DEV):
+        peer = lax.rem(me + step, N_DEV)
+        copy = pltpu.make_async_remote_copy(
+            src_ref=own_sum, dst_ref=out_ref.at[me], send_sem=send_sems.at[1, step],
+            recv_sem=recv_sems.at[1, step], device_id=(peer,), device_id_type=pl.DeviceIdType.MESH)
+        copy.start()
+        copies.append(copy)
+    for copy in copies:
+        copy.wait()
 
 
 def sum_devices(part):
+    part = part.reshape(N_DEV, -1, 128)
     return pl.pallas_call(
         sum_kernel,
         out_shape=jax.ShapeDtypeStruct(part.shape, jnp.float32),
         in_specs=[vmem_spec()],
         out_specs=vmem_spec(),
-        scratch_shapes=[pltpu.VMEM((N_DEV,) + part.shape, jnp.float32),
-                        pltpu.SemaphoreType.DMA((N_DEV,)), pltpu.SemaphoreType.DMA((N_DEV,))],
+        scratch_shapes=[pltpu.VMEM(part.shape, jnp.float32), pltpu.VMEM(part.shape[1:], jnp.float32),
+                        pltpu.SemaphoreType.DMA((2, N_DEV)), pltpu.SemaphoreType.DMA((2, N_DEV))],
         compiler_params=pltpu.CompilerParams(has_side_effects=True),
         cost_estimate=pl.CostEstimate(flops=int(1e9), bytes_accessed=int(1e6), transcendentals=0),
         name='sum_devices',
-    )(part)
+    )(part).reshape(-1, 128)
 
 
 def to_tokens_kernel(tok, cols, in_ref, out_ref, send_sems, recv_sems):
@@ -222,7 +234,7 @@
     )(q_rot, k_rot, v_heads, d_heads, lse, cos_t, sin_t)
 
 
-COLUMN_PARTS = ((0, 1408), (1408, 2816), (2816, 4096))
+COLUMN_PARTS = ((0, 1280), (1280, 2688), (2688, 4096))
 AXIS_ORDERS = ((0, 1, 2), (1, 2, 0), (2, 0, 1))
 
 
@@ -302,6 +314,7 @@
     x_full = after(x_full, w_cat)
     q_raw, k_raw = dot_f32('bsd,de->bse', x_full, wq_loc), dot_f32('bsd,de->bse', x_full, wk_loc)
     v_heads = dot_f32('bsd,de->bse', x_full, wv_loc).astype(jnp.bfloat16)
+    q_raw, k_raw = lax.optimization_barrier((q_raw, k_raw))
     part = jnp.stack([jnp.sum(q_raw * q_raw, axis=-1), jnp.sum(k_raw * k_raw, axis=-1)])
     sums = sum_devices(part.reshape(-1, 128)).reshape(2, batch_size, seq_len, 1)
     inv_q, inv_k = lax.rsqrt(sums / model_dim + NORM_EPS)
@@ -321,7 +334,7 @@
     d_attn = (post_rms * (g_normed - normed * jnp.mean(g_normed * normed, axis=-1, keepdims=True))).astype(jnp.bfloat16)
     d_o_loc = dot_f32('td,ed->te', d_attn, wo_full).astype(jnp.bfloat16)
     d_heads = to_heads(d_o_loc.reshape(batch_size, seq_loc, model_dim))
-    d_attn_full = lax.all_gather(d_attn.reshape(batch_size, seq_loc, model_dim), 'tp', axis=1, tiled=True)
+    d_attn_full = lax.all_gather(after(d_attn.reshape(batch_size, seq_loc, model_dim), d_heads), 'tp', axis=1, tiled=True)
 
     dq_hat, dk_hat, d_value = attention_bwd(q_rot, k_rot, v_heads, d_heads, lse, cos_t, sin_t)
     q_unit, k_unit = q_raw * inv_q, k_raw * inv_k
@@ -343,11 +356,10 @@
     sums_0, gate = cross_axis(start_sums(parts_of(far[0]), parts_of(near[0])), 0)
     far_parts = parts_of(after(far[1], *gate))
     near_parts = parts_of(after(near[1], *far_parts))
-    sums_1 = start_sums(far_parts, near_parts)
-    x_early = after(x_full, *near_parts)
+    sums_1, gate = cross_axis(start_sums(far_parts, near_parts), 0)
+    x_early = after(x_full, *gate)
     grad_wq, grad_wk = [dot_f32('bsd,bse->de', x_early, cot).astype(jnp.bfloat16) for cot in (dq_raw, dk_raw)]
     sums_0, gate = cross_axis(sums_after(sums_0, [grad_wq, grad_wk]), 1)
-    sums_1, gate = cross_axis(sums_after(sums_1, gate), 0)
     grad_wv = dot_f32('bsd,bse->de', after(x_full, *gate), d_value).astype(jnp.bfloat16)
     grad_wo = dot_f32('bse,bsd->ed', heads_out, after(d_attn_full, grad_wv)).astype(jnp.bfloat16)
     sums_1, gate = cross_axis(sums_after(sums_1, [grad_wo]), 1)

time: 818 us -> 762 us (0.932)
  waiting for transfers between devices: 233 us -> 215 us
  local copies, waits for them, and re-layouts: 33.9 us -> 19.3 us
  matrix products: 233 us -> 222 us
    ppermute x24, waiting for transfers between devices: 110 us -> 87.6 us  [flip(): return lax.ppermute(value, 'tp', [(i, i ^ bit) for i in range(N_DEV)])]
    pallas_call x2, Pallas kernels: 41.4 us -> 29 us  [sum_devices(): pl.pallas_call(sum_kernel, out_shape=jax.ShapeDtypeStruct(part.shape, jnp...]
    dot_general x2 -> x0, local copies, waits for them, and re-layouts: 10.9 us -> none  [dot_f32(): return jnp.einsum(spec, lhs, rhs, preferred_element_type=jnp.float32)]
    dot_general x21, matrix products: 233 us -> 222 us  [dot_f32(): return jnp.einsum(spec, lhs, rhs, preferred_element_type=jnp.float32)]
  transfers between devices with their start and end apart: 27 -> 27, of which waited for: 7 -> 9; matrix products, arithmetic and copies ran while one was open for 40% -> 38% of each run, Pallas kernels for 23% -> 19%
where the time goes in v4:
time: 762 us; the launch traced here: 757 us
  matrix products  222 us (29%)
  waiting for transfers between devices  215 us (28%)
  Pallas kernels  175 us (23%)
  other arithmetic  91.5 us (12%)
  local copies, waits for them, and re-layouts  19.3 us (3%)
  starting transfers between devices  18.9 us (2%)
  between operations  14.8 us (2%)
    dot_general x21, matrix products, dot_f32(): return jnp.einsum(spec, lhs, rhs, preferred_element_type=jnp.float32)  222 us
    all_gather x1, waiting for transfers between devices, local_block(): x_full = lax.all_gather(x_loc, 'tp', axis=1, tiled=True)  121 us
    ppermute x24, waiting for transfers between devices, flip(): return lax.ppermute(value, 'tp', [(i, i ^ bit) for i in range(N_DEV)])  87.6 us
    pallas_call x2, Pallas kernels, exchange(): pl.pallas_call(functools.partial(kernel, tok, cols), out_shape=jax.ShapeD...  76.2 us
    pallas_call x1, Pallas kernels, attention_bwd(): pl.pallas_call(bwd_kernel, grid=(batch_size, heads), in_specs=[head_spec,...  35.6 us
    add x9, other arithmetic, cross_axis(): sum((lax.slice_in_dim(p, 0, 1, axis=axis) for p in pieces))  34.6 us
    pallas_call x1, Pallas kernels, attention_fwd(): pl.pallas_call(fwd_kernel, grid=(batch_size, heads), in_specs=[head_spec,...  34.1 us
    pallas_call x2, Pallas kernels, sum_devices(): pl.pallas_call(sum_kernel, out_shape=jax.ShapeDtypeStruct(part.shape, jnp...  29 us
  transfers between devices with their start and end apart: 27, of which 9 were waited for; matrix products, arithmetic and copies ran while one was open for 38% of the time, Pallas kernels for 19%

profile of v4, /device:TPU:0, one launch (start us, length us, event | category | flops | bytes accessed | tf_op | source)
XLA Modules:
  0.0 756.6 jit_solution(2463606805614721221)
XLA Ops:
  9.9 3.9 fusion.44
  23.2 121.3 %all-gather.4.cloned.1.call-done = bf16[2,2048,4096]{2,1,0:T(8,128)(2,1)} async-done(((bf16[2,128,4096]{2,1,0:T(8,128)(2,1)}), bf16[2,2048,4096]{2,1,0:T(8,128)(2,1)}) %all-gather.4.cloned.1.call-update) | async-done | bytes 33554448 | tf_op jit(solution)/shard_map/all_gather | solution.py:311
  144.5 16.7 %fusion.14.k_ref = f32[2,2048,256]{2,1,0:T(8,128)S(1)} fusion(bf16[2,2048,4096]{2,1,0:T(8,128)(2,1)} %all-gather.4.cloned.1.call-done, bf16[4096,256]{1,0:T(8,128)(2,1)S(1)} %copy-done.18), kind=kOutput, calls=%fused_computation.47 | convolution fusion | flops 8589934592 | bytes 39845888 | tf_op jit(solution)/shard_map/bsd,de->bse/dot_general | solution.py:297
  161.3 17.1 %fusion.16.q_ref = f32[2,2048,256]{2,1,0:T(8,128)S(1)} fusion(bf16[2,2048,4096]{2,1,0:T(8,128)(2,1)} %all-gather.4.cloned.1.call-done, bf16[4096,256]{1,0:T(8,128)(2,1)} %param.10), kind=kOutput, calls=%fused_computation.49 | convolution fusion | flops 8589934592 | bytes 39845888 | tf_op jit(solution)/shard_map/bsd,de->bse/dot_general | solution.py:297
  181.1 12.9 %sum_devices.2 = f32[16,4,128]{2,1,0:T(4,128)} custom-call(f32[16,4,128]{2,1,0:T(4,128)} %reshape_reshape.4.part_ref), custom_call_target="tpu_custom_call" | custom-call | flops 1000000000 | bytes 1000000 | tf_op jit(solution)/shard_map/sum_devices/pallas_call | solution.py:67
  201.5 17.0 %convolution_convert_fusion.1.v_ref = bf16[2,2048,256]{2,1,0:T(8,128)(2,1)} fusion(bf16[2,2048,4096]{2,1,0:T(8,128)(2,1)} %all-gather.4.cloned.1.call-done, bf16[4096,256]{1,0:T(8,128)(2,1)S(1)} %copy-done.21), kind=kOutput, calls=%fused_computation.28 | convolution fusion | flops 8590983168 | bytes 37748736 | tf_op jit(solution)/shard_map/bsd,de->bse/dot_general | solution.py:297
  218.5 34.1 %attention_fwd.1 = (bf16[2,2048,256]{2,1,0:T(8,128)(2,1)}, bf16[2,2048,256]{2,1,0:T(8,128)(2,1)}, bf16[2,2048,256]{2,1,0:T(8,128)(2,1)}, f32[2,2,1,2048]{3,2,1,0:T(1,128)}) custom-call(f32[2,2048,256]{2,1,0:T(8,128)} %copy-done.1, f32[2,2048,256]{2,1,0:T(8,128)} %copy-done.4, bf16[2,2048,256]{2,1,0:T(8,128)(2,1)} %convolution_convert_fusion.1.v_ref, ...), custom_call_target="tpu_custom_call" | custom-call | flops 8000000000 | bytes 10000000 | tf_op jit(solution)/shard_map/attention_fwd/pallas_call | solution.py:178
  252.6 44.4 %shard_map.160 = bf16[2,128,4096]{2,1,0:T(8,128)(2,1)} custom-call(bf16[2,2048,256]{2,1,0:T(8,128)(2,1)} %get-tuple-element.62.in_ref), custom_call_target="tpu_custom_call" | custom-call | flops 10000000000 | bytes 8000000 | tf_op jit(solution)/shard_map/pallas_call | solution.py:115
  297.0 4.3 all-gather.6.cloned.1.call-done
  301.3 16.0 %multiply_reduce_fusion.4 = (f32[256]{0:T(256)S(1)}, f32[256,4096]{1,0:T(8,128)S(1)}) fusion(bf16[256,4096]{1,0:T(8,128)(2,1)} %bitcast.110, bf16[4096,4096]{1,0:T(8,128)(2,1)} %all-gather.6.cloned.1.call-done), kind=kOutput, calls=%fused_computation.25 | convolution fusion | flops 8592031744 | bytes 39846912 | tf_op jit(solution)/shard_map/te,ed->td/dot_general | solution.py:297
  319.1 3.4 fusion.8
  322.5 16.6 %convolution_convert_fusion = bf16[256,4096]{1,0:T(8,128)(2,1)} fusion(bf16[256,4096]{1,0:T(8,128)(2,1)S(1)} %get-tuple-element.139, bf16[4096,4096]{1,0:T(8,128)(2,1)} %all-gather.6.cloned.1.call-done), kind=kOutput, calls=%fused_computation.10 | convolution fusion | flops 8590983168 | bytes 37748736 | tf_op jit(solution)/shard_map/td,ed->te/dot_general | solution.py:297
  339.1 31.8 %shard_map.161.do_ref = bf16[2,2048,256]{2,1,0:T(8,128)(2,1)} custom-call(bf16[2,128,4096]{2,1,0:T(8,128)(2,1)} %bitcast.111), custom_call_target="tpu_custom_call" | custom-call | flops 10000000000 | bytes 8000000 | tf_op jit(solution)/shard_map/pallas_call | solution.py:115
  371.1 35.6 %attention_bwd.1 = (f32[2,2048,256]{2,1,0:T(8,128)}, f32[2,2048,256]{2,1,0:T(8,128)}, bf16[2,2048,256]{2,1,0:T(8,128)(2,1)}) custom-call(bf16[2,2048,256]{2,1,0:T(8,128)(2,1)} %get-tuple-element.63.q_ref, bf16[2,2048,256]{2,1,0:T(8,128)(2,1)} %get-tuple-element.64.k_ref, bf16[2,2048,256]{2,1,0:T(8,128)(2,1)} %convolution_convert_fusion.1.v_ref, ...), custom_call_target="tpu_custom_call" | custom-call | flops 20000000000 | bytes 10000000 | tf_op jit(solution)/shard_map/attention_bwd/pallas_call | solution.py:223
  406.7 6.8 multiply_reduce_fusion
  414.1 16.1 %sum_devices.3 = f32[16,6,128]{2,1,0:T(8,128)} custom-call(f32[16,6,128]{2,1,0:T(8,128)} %reshape.252.part_ref), custom_call_target="tpu_custom_call" | custom-call | flops 1000000000 | bytes 1000000 | tf_op jit(solution)/shard_map/sum_devices/pallas_call | solution.py:67
  431.2 4.7 multiply_convert_fusion.dk_ref
  439.1 3.9 fusion.38
  443.1 6.8 fusion.22
  450.4 6.1 fusion.30
  456.5 6.0 fusion.40
  462.6 6.0 fusion.24
  468.6 6.1 fusion.32
  474.6 7.0 slice_add_fusion.11
  481.7 6.5 slice_add_fusion.5
  488.2 6.6 slice_add_fusion.7
  494.7 3.8 fusion.36
  498.6 6.4 fusion.20
  505.4 6.0 fusion.28
  514.8 6.0 fusion.34
  520.9 6.0 fusion.18
  526.9 6.0 fusion.26
  534.3 7.1 slice_add_fusion.9
  542.1 7.4 slice_add_fusion.2
  550.1 6.0 slice_add_fusion.3
  556.1 17.6 %fusion.2 = bf16[4096,256]{1,0:T(8,128)(2,1)} fusion(bf16[2,2048,4096]{2,1,0:T(8,128)(2,1)} %all-gather.4.cloned.1.call-done, bf16[2,2048,256]{2,1,0:T(8,128)(2,1)S(1)} %multiply_convert_fusion.dk_ref), kind=kOutput, calls=%fused_computation.8 | convolution fusion | flops 8590983168 | bytes 37748736 | tf_op jit(solution)/shard_map/bsd,bse->de/dot_general | solution.py:297
  573.7 17.4 %fusion.1 = bf16[4096,256]{1,0:T(8,128)(2,1)} fusion(bf16[2,2048,4096]{2,1,0:T(8,128)(2,1)} %all-gather.4.cloned.1.call-done, bf16[2,2048,256]{2,1,0:T(8,128)(2,1)S(1)} %multiply_convert_fusion.1.dq_ref), kind=kOutput, calls=%fused_computation.7 | convolution fusion | flops 8590983168 | bytes 37748736 | tf_op jit(solution)/shard_map/bsd,bse->de/dot_general | solution.py:297
  591.7 6.9 collective-permute-done.3
  598.6 3.9 slice_add_fusion.17
  603.1 3.9 slice_add_fusion.19
  607.5 3.5 slice_add_fusion.23
  611.1 17.6 %fusion.3 = bf16[4096,256]{1,0:T(8,128)(2,1)} fusion(bf16[2,2048,4096]{2,1,0:T(8,128)(2,1)} %all-gather.4.cloned.1.call-done, bf16[2,2048,256]{2,1,0:T(8,128)(2,1)S(1)} %copy-done), kind=kOutput, calls=%fused_computation.9 | convolution fusion | flops 8590983168 | bytes 37748736 | tf_op jit(solution)/shard_map/bsd,bse->de/dot_general | solution.py:297
  628.7 17.1 %fusion = bf16[256,4096]{1,0:T(8,128)(2,1)} fusion(bf16[2,2048,256]{2,1,0:T(8,128)(2,1)} %get-tuple-element.62.in_ref, bf16[2,2048,4096]{2,1,0:T(8,128)(2,1)} %all-gather.8.cloned.1.call-done), kind=kOutput, calls=%fused_computation.6 | convolution fusion | flops 8590983168 | bytes 37748736 | tf_op jit(solution)/shard_map/bse,bsd->ed/dot_general | solution.py:297
  647.2 13.2 %collective-permute-done.13 = f32[2,1,2,128,1408]{4,3,2,1,0:T(8,128)} collective-permute-done((f32[2,1,2,128,1408]{4,3,2,1,0:T(8,128)}, f32[2,1,2,128,1408]{4,3,2,1,0:T(8,128)}, u32[]{:S(2)}, u32[]{:S(2)}) %collective-permute-start.13) | collective-permute-done | bytes 2883616 | tf_op jit(solution)/shard_map/ppermute | solution.py:267
  668.1 18.8 %collective-permute-done.9 = f32[1,1,2,128,1280]{4,3,2,1,0:T(8,128)S(1)} collective-permute-done((f32[1,1,2,128,1280]{4,3,2,1,0:T(8,128)S(1)}, f32[1,1,2,128,1280]{4,3,2,1,0:T(8,128)S(1)}, u32[]{:S(2)}, u32[]{:S(2)}) %collective-permute-start.9) | collective-permute-done | bytes 1310752 | tf_op jit(solution)/shard_map/ppermute | solution.py:267
  693.3 25.2 %collective-permute-done.18 = f32[1,1,2,128,1280]{4,3,2,1,0:T(8,128)S(1)} collective-permute-done((f32[1,1,2,128,1280]{4,3,2,1,0:T(8,128)S(1)}, f32[1,1,2,128,1280]{4,3,2,1,0:T(8,128)S(1)}, u32[]{:S(2)}, u32[]{:S(2)}) %collective-permute-start.18) | collective-permute-done | bytes 1310752 | tf_op jit(solution)/shard_map/ppermute | solution.py:267
  721.9 14.2 %collective-permute-done.15 = f32[1,1,1,128,1280]{4,3,2,1,0:T(8,128)S(1)} collective-permute-done((f32[1,1,1,128,1280]{4,3,2,1,0:T(8,128)S(1)}, f32[1,1,1,128,1280]{4,3,2,1,0:T(8,128)S(1)}, u32[]{:S(2)}, u32[]{:S(2)}) %collective-permute-start.15) | collective-permute-done | bytes 655392 | tf_op jit(solution)/shard_map/ppermute | solution.py:267
  737.8 6.8 collective-permute-done.21
  (158 shorter events, 63.3 us)
Async XLA Ops:
  7.2 2.7 copy-start.23
  7.2 137.3 %all-gather.4.cloned.1.call-start = ((), (), s32[]{:S(2)}) async-start(), calls=%async_computation | async-start | bytes 35651584 | tf_op jit(solution)/shard_map/all_gather | solution.py:311
  7.9 293.3 %all-gather.6.cloned.1.call-start = ((), (), s32[]{:S(2)}) async-start(), calls=%async_computation.1 | async-start | bytes 35651584 | tf_op jit(solution)/shard_map/all_gather | solution.py:312
  8.7 620.0 %all-gather.8.cloned.1.call-start = ((), (), s32[]{:S(2)}) async-start(), calls=%async_computation.2 | async-start | bytes 35651584 | tf_op jit(solution)/shard_map/all_gather | solution.py:337
  13.8 2.8 copy-start.19
  161.3 17.8 %copy-start.4 = (f32[2,2048,256]{2,1,0:T(8,128)}, f32[2,2048,256]{2,1,0:T(8,128)S(1)}, u32[]{:S(2)}) copy-start(f32[2,2048,256]{2,1,0:T(8,128)S(1)} %fusion.14.k_ref) | copy-start | bytes 12582916
  194.0 7.5 copy-start.21
  301.3 16.0 %copy-start.5 = (bf16[2,128,4096]{2,1,0:T(8,128)(2,1)S(1)}, bf16[2,128,4096]{2,1,0:T(8,128)(2,1)}, u32[]{:S(2)}) copy-start(bf16[2,128,4096]{2,1,0:T(8,128)(2,1)} %param.17) | copy-start | bytes 6291460
  322.5 16.6 %copy-start.14 = (bf16[256,4096]{1,0:T(8,128)(2,1)}, bf16[256,4096]{1,0:T(8,128)(2,1)S(1)}, u32[]{:S(2)}) copy-start(bf16[256,4096]{1,0:T(8,128)(2,1)S(1)} %get-tuple-element.139) | copy-start | bytes 6291460
  339.1 31.8 %copy-start.25 = (bf16[256]{0:T(256)(128)(2,1)S(1)}, bf16[256]{0:T(256)(128)(2,1)}, u32[]{:S(2)}) copy-start(bf16[256]{0:T(256)(128)(2,1)} %param.14) | copy-start | bytes 1540
  339.1 31.9 %copy-start.27 = (bf16[256]{0:T(256)(128)(2,1)S(1)}, bf16[256]{0:T(256)(128)(2,1)}, u32[]{:S(2)}) copy-start(bf16[256]{0:T(256)(128)(2,1)} %param.15) | copy-start | bytes 1540
  371.1 35.6 %copy-start.2 = (f32[2,2048,256]{2,1,0:T(8,128)S(1)}, f32[2,2048,256]{2,1,0:T(8,128)}, u32[]{:S(2)}) copy-start(f32[2,2048,256]{2,1,0:T(8,128)} %copy-done.1) | copy-start | bytes 12582916
  431.2 4.8 copy-start.3
  431.2 5.9 copy-start.7
  443.0 31.6 %collective-permute-start = (f32[1024,1280]{1,0:T(8,128)S(1)}, f32[1024,1280]{1,0:T(8,128)}, u32[]{:S(2)}, u32[]{:S(2)}) collective-permute-start(f32[1024,1280]{1,0:T(8,128)S(1)} %fusion.38), channel_id=1, source_target_pairs={{0,1},{1,0},{2,3},{3,2},{4,5},{5,4},{6,7},{7,6},{8,9},{9,8},{10,11... | collective-permute-start | bytes 15728648 | tf_op jit(solution)/shard_map/ppermute | solution.py:267
  449.9 31.7 %collective-permute-start.4 = (f32[1024,1408]{1,0:T(8,128)}, f32[1024,1408]{1,0:T(8,128)}, u32[]{:S(2)}, u32[]{:S(2)}) collective-permute-start(f32[1024,1408]{1,0:T(8,128)} %fusion.22), channel_id=1, source_target_pairs={{0,1},{1,0},{2,3},{3,2},{4,5},{5,4},{6,7},{7,6},{8,9},{9,8},{10,11... | collective-permute-start | bytes 17301512 | tf_op jit(solution)/shard_map/ppermute | solution.py:267
  456.5 31.6 %collective-permute-start.2 = (f32[1024,1408]{1,0:T(8,128)}, f32[1024,1408]{1,0:T(8,128)S(1)}, u32[]{:S(2)}, u32[]{:S(2)}) collective-permute-start(f32[1024,1408]{1,0:T(8,128)} %fusion.30), channel_id=1, source_target_pairs={{0,1},{1,0},{2,3},{3,2},{4,5},{5,4},{6,7},{7,6},{8,9},{9,8},{10,11... | collective-permute-start | bytes 17301512 | tf_op jit(solution)/shard_map/ppermute | solution.py:267
  498.5 34.4 %collective-permute-start.6 = (f32[1024,1280]{1,0:T(8,128)S(1)}, f32[1024,1280]{1,0:T(8,128)}, u32[]{:S(2)}, u32[]{:S(2)}) collective-permute-start(f32[1024,1280]{1,0:T(8,128)S(1)} %fusion.36), channel_id=1, source_target_pairs={{0,1},{1,0},{2,3},{3,2},{4,5},{5,4},{6,7},{7,6},{8,9},{9,8},{10,11... | collective-permute-start | bytes 15728648 | tf_op jit(solution)/shard_map/ppermute | solution.py:267
  504.9 36.5 %collective-permute-start.8 = (f32[1024,1408]{1,0:T(8,128)}, f32[1024,1408]{1,0:T(8,128)}, u32[]{:S(2)}, u32[]{:S(2)}) collective-permute-start(f32[1024,1408]{1,0:T(8,128)} %fusion.20), channel_id=1, source_target_pairs={{0,1},{1,0},{2,3},{3,2},{4,5},{5,4},{6,7},{7,6},{8,9},{9,8},{10,11... | collective-permute-start | bytes 17301512 | tf_op jit(solution)/shard_map/ppermute | solution.py:267
  511.4 38.1 %collective-permute-start.7 = (f32[1024,1408]{1,0:T(8,128)}, f32[1024,1408]{1,0:T(8,128)S(1)}, u32[]{:S(2)}, u32[]{:S(2)}) collective-permute-start(f32[1024,1408]{1,0:T(8,128)} %fusion.28), channel_id=1, source_target_pairs={{0,1},{1,0},{2,3},{3,2},{4,5},{5,4},{6,7},{7,6},{8,9},{9,8},{10,11... | collective-permute-start | bytes 17301512 | tf_op jit(solution)/shard_map/ppermute | solution.py:267
  512.1 79.0 %collective-permute-start.1 = (f32[1,2,2,128,1280]{4,3,2,1,0:T(8,128)}, f32[1,2,2,128,1280]{4,3,2,1,0:T(8,128)}, u32[]{:S(2)}, u32[]{:S(2)}) collective-permute-start(f32[1,2,2,128,1280]{4,3,2,1,0:T(8,128)} %bitcast.15), channel_id=1, source_target_pairs={{0,8},{1,9},{2,10},{3,11},{4,12},{5,13},{6,14},{7,15},{8,0},{9,1},... | collective-permute-start | bytes 7864328 | tf_op jit(solution)/shard_map/ppermute | solution.py:267
  513.1 78.6 %collective-permute-start.5 = (f32[2,2,1,128,1408]{4,3,2,1,0:T(8,128)}, f32[2,2,1,128,1408]{4,3,2,1,0:T(8,128)}, u32[]{:S(2)}, u32[]{:S(2)}) collective-permute-start(f32[2,2,1,128,1408]{4,3,2,1,0:T(8,128)} %get-tuple-element.116), channel_id=1, source_target_pairs={{0,2},{1,3},{2,0},{3,1},{4,6},{5,7},{6,4},{7,5},{8,10},{9,11},{10,... | collective-permute-start | bytes 8650760 | tf_op jit(solution)/shard_map/ppermute | solution.py:267
  532.9 65.7 %collective-permute-start.3 = (f32[2,1,2,128,1408]{4,3,2,1,0:T(8,128)}, f32[2,1,2,128,1408]{4,3,2,1,0:T(8,128)}, u32[]{:S(2)}, u32[]{:S(2)}) collective-permute-start(f32[2,1,2,128,1408]{4,3,2,1,0:T(8,128)} %get-tuple-element.118), channel_id=1, source_target_pairs={{0,4},{1,5},{2,6},{3,7},{4,0},{5,1},{6,2},{7,3},{8,12},{9,13},{10,... | collective-permute-start | bytes 8650760 | tf_op jit(solution)/shard_map/ppermute | solution.py:267
  541.4 104.3 %collective-permute-start.12 = (f32[1,2,2,128,1280]{4,3,2,1,0:T(8,128)}, f32[1,2,2,128,1280]{4,3,2,1,0:T(8,128)}, u32[]{:S(2)}, u32[]{:S(2)}) collective-permute-start(f32[1,2,2,128,1280]{4,3,2,1,0:T(8,128)} %bitcast.20), channel_id=1, source_target_pairs={{0,8},{1,9},{2,10},{3,11},{4,12},{5,13},{6,14},{7,15},{8,0},{9,1},... | collective-permute-start | bytes 7864328 | tf_op jit(solution)/shard_map/ppermute | solution.py:267
  549.6 97.6 %collective-permute-start.14 = (f32[2,2,1,128,1408]{4,3,2,1,0:T(8,128)}, f32[2,2,1,128,1408]{4,3,2,1,0:T(8,128)}, u32[]{:S(2)}, u32[]{:S(2)}) collective-permute-start(f32[2,2,1,128,1408]{4,3,2,1,0:T(8,128)} %get-tuple-element.119), channel_id=1, source_target_pairs={{0,2},{1,3},{2,0},{3,1},{4,6},{5,7},{6,4},{7,5},{8,10},{9,11},{10,... | collective-permute-start | bytes 8650760 | tf_op jit(solution)/shard_map/ppermute | solution.py:267
  591.0 69.3 %collective-permute-start.13 = (f32[2,1,2,128,1408]{4,3,2,1,0:T(8,128)}, f32[2,1,2,128,1408]{4,3,2,1,0:T(8,128)}, u32[]{:S(2)}, u32[]{:S(2)}) collective-permute-start(f32[2,1,2,128,1408]{4,3,2,1,0:T(8,128)} %get-tuple-element.121), channel_id=1, source_target_pairs={{0,4},{1,5},{2,6},{3,7},{4,0},{5,1},{6,2},{7,3},{8,12},{9,13},{10,... | collective-permute-start | bytes 8650760 | tf_op jit(solution)/shard_map/ppermute | solution.py:267
  598.6 4.5 copy-start.8
  602.4 5.1 copy-start.11
  602.4 85.8 %collective-permute-start.11 = (f32[1,2,1,128,1408]{4,3,2,1,0:T(8,128)}, f32[1,2,1,128,1408]{4,3,2,1,0:T(8,128)}, u32[]{:S(2)}, u32[]{:S(2)}) collective-permute-start(f32[1,2,1,128,1408]{4,3,2,1,0:T(8,128)} %get-tuple-element.128), channel_id=1, source_target_pairs={{0,8},{1,9},{2,10},{3,11},{4,12},{5,13},{6,14},{7,15},{8,0},{9,1},... | collective-permute-start | bytes 4325384 | tf_op jit(solution)/shard_map/ppermute | solution.py:267
  607.0 81.2 %collective-permute-start.10 = (f32[2,1,1,128,1408]{4,3,2,1,0:T(8,128)}, f32[2,1,1,128,1408]{4,3,2,1,0:T(8,128)}, u32[]{:S(2)}, u32[]{:S(2)}) collective-permute-start(f32[2,1,1,128,1408]{4,3,2,1,0:T(8,128)} %get-tuple-element.130), channel_id=1, source_target_pairs={{0,2},{1,3},{2,0},{3,1},{4,6},{5,7},{6,4},{7,5},{8,10},{9,11},{10,... | collective-permute-start | bytes 4325384 | tf_op jit(solution)/shard_map/ppermute | solution.py:267
  628.6 31.7 %copy-start.9 = (f32[2,2,1,128,1408]{4,3,2,1,0:T(8,128)S(1)}, f32[2,2,1,128,1408]{4,3,2,1,0:T(8,128)}, u32[]{:S(2)}) copy-start(f32[2,2,1,128,1408]{4,3,2,1,0:T(8,128)} %get-tuple-element.89) | copy-start | bytes 8650756
  628.7 17.1 %copy-start.22 = (f32[1,1,2,128,1280]{4,3,2,1,0:T(8,128)S(1)}, f32[1,1,2,128,1280]{4,3,2,1,0:T(8,128)}, u32[]{:S(2)}) copy-start(f32[1,1,2,128,1280]{4,3,2,1,0:T(8,128)} %get-tuple-element.136) | copy-start | bytes 3932164
  645.7 41.1 %collective-permute-start.9 = (f32[1,1,2,128,1280]{4,3,2,1,0:T(8,128)S(1)}, f32[1,1,2,128,1280]{4,3,2,1,0:T(8,128)S(1)}, u32[]{:S(2)}, u32[]{:S(2)}) collective-permute-start(f32[1,1,2,128,1280]{4,3,2,1,0:T(8,128)S(1)} %copy-done.22), channel_id=1, source_target_pairs={{0,4},{1,5},{2,6},{3,7},{4,0},{5,1},{6,2},{7,3},{8,12},{9,13},{10,... | collective-permute-start | bytes 3932168 | tf_op jit(solution)/shard_map/ppermute | solution.py:267
  660.4 2.9 copy-start.10
  662.6 3.5 copy-start.12
  662.6 56.3 %collective-permute-start.20 = (f32[1,2,1,128,1408]{4,3,2,1,0:T(8,128)S(1)}, f32[1,2,1,128,1408]{4,3,2,1,0:T(8,128)S(1)}, u32[]{:S(2)}, u32[]{:S(2)}) collective-permute-start(f32[1,2,1,128,1408]{4,3,2,1,0:T(8,128)S(1)} %get-tuple-element.131), channel_id=1, source_target_pairs={{0,8},{1,9},{2,10},{3,11},{4,12},{5,13},{6,14},{7,15},{8,0},{9,1},... | collective-permute-start | bytes 4325384 | tf_op jit(solution)/shard_map/ppermute | solution.py:267
  665.4 22.8 %copy-start.15 = (f32[1,2,1,128,1408]{4,3,2,1,0:T(8,128)S(1)}, f32[1,2,1,128,1408]{4,3,2,1,0:T(8,128)}, u32[]{:S(2)}) copy-start(f32[1,2,1,128,1408]{4,3,2,1,0:T(8,128)} %get-tuple-element.95) | copy-start | bytes 4325380
  665.5 53.5 %collective-permute-start.19 = (f32[2,1,1,128,1408]{4,3,2,1,0:T(8,128)S(1)}, f32[2,1,1,128,1408]{4,3,2,1,0:T(8,128)S(1)}, u32[]{:S(2)}, u32[]{:S(2)}) collective-permute-start(f32[2,1,1,128,1408]{4,3,2,1,0:T(8,128)S(1)} %get-tuple-element.133), channel_id=1, source_target_pairs={{0,2},{1,3},{2,0},{3,1},{4,6},{5,7},{6,4},{7,5},{8,10},{9,11},{10,... | collective-permute-start | bytes 4325384 | tf_op jit(solution)/shard_map/ppermute | solution.py:267
  668.1 22.4 %copy-start.16 = (f32[2,1,1,128,1408]{4,3,2,1,0:T(8,128)S(1)}, f32[2,1,1,128,1408]{4,3,2,1,0:T(8,128)}, u32[]{:S(2)}) copy-start(f32[2,1,1,128,1408]{4,3,2,1,0:T(8,128)} %get-tuple-element.93) | copy-start | bytes 4325380
  686.8 31.6 %collective-permute-start.18 = (f32[1,1,2,128,1280]{4,3,2,1,0:T(8,128)S(1)}, f32[1,1,2,128,1280]{4,3,2,1,0:T(8,128)S(1)}, u32[]{:S(2)}, u32[]{:S(2)}) collective-permute-start(f32[1,1,2,128,1280]{4,3,2,1,0:T(8,128)S(1)} %get-tuple-element.137), channel_id=1, source_target_pairs={{0,4},{1,5},{2,6},{3,7},{4,0},{5,1},{6,2},{7,3},{8,12},{9,13},{10,... | collective-permute-start | bytes 3932168 | tf_op jit(solution)/shard_map/ppermute | solution.py:267
  689.8 3.3 copy-start.17
  689.8 47.7 %collective-permute-start.17 = (f32[1,1,1,128,1408]{4,3,2,1,0:T(8,128)S(1)}, f32[1,1,1,128,1408]{4,3,2,1,0:T(8,128)S(1)}, u32[]{:S(2)}, u32[]{:S(2)}) collective-permute-start(f32[1,1,1,128,1408]{4,3,2,1,0:T(8,128)S(1)} %get-tuple-element.142), channel_id=1, source_target_pairs={{0,4},{1,5},{2,6},{3,7},{4,0},{5,1},{6,2},{7,3},{8,12},{9,13},{10,... | collective-permute-start | bytes 2162696 | tf_op jit(solution)/shard_map/ppermute | solution.py:267
  692.0 45.5 %collective-permute-start.16 = (f32[1,1,1,128,1408]{4,3,2,1,0:T(8,128)S(1)}, f32[1,1,1,128,1408]{4,3,2,1,0:T(8,128)S(1)}, u32[]{:S(2)}, u32[]{:S(2)}) collective-permute-start(f32[1,1,1,128,1408]{4,3,2,1,0:T(8,128)S(1)} %get-tuple-element.144), channel_id=1, source_target_pairs={{0,8},{1,9},{2,10},{3,11},{4,12},{5,13},{6,14},{7,15},{8,0},{9,1},... | collective-permute-start | bytes 2162696 | tf_op jit(solution)/shard_map/ppermute | solution.py:267
  718.5 17.6 %collective-permute-start.15 = (f32[1,1,1,128,1280]{4,3,2,1,0:T(8,128)S(1)}, f32[1,1,1,128,1280]{4,3,2,1,0:T(8,128)S(1)}, u32[]{:S(2)}, u32[]{:S(2)}) collective-permute-start(f32[1,1,1,128,1280]{4,3,2,1,0:T(8,128)S(1)} %get-tuple-element.146), channel_id=1, source_target_pairs={{0,2},{1,3},{2,0},{3,1},{4,6},{5,7},{6,4},{7,5},{8,10},{9,11},{10,... | collective-permute-start | bytes 1966088 | tf_op jit(solution)/shard_map/ppermute | solution.py:267
  719.0 25.6 %collective-permute-start.21 = (f32[1,1,1,128,1280]{4,3,2,1,0:T(8,128)S(1)}, f32[1,1,1,128,1280]{4,3,2,1,0:T(8,128)S(1)}, u32[]{:S(2)}, u32[]{:S(2)}) collective-permute-start(f32[1,1,1,128,1280]{4,3,2,1,0:T(8,128)S(1)} %slice_add_fusion.30), channel_id=1, source_target_pairs={{0,2},{1,3},{2,0},{3,1},{4,6},{5,7},{6,4},{7,5},{8,10},{9,11},{10,... | collective-permute-start | bytes 1966088 | tf_op jit(solution)/shard_map/ppermute | solution.py:267
  720.7 24.0 %collective-permute-start.22 = (f32[1,1,1,128,1408]{4,3,2,1,0:T(8,128)S(1)}, f32[1,1,1,128,1408]{4,3,2,1,0:T(8,128)S(1)}, u32[]{:S(2)}, u32[]{:S(2)}) collective-permute-start(f32[1,1,1,128,1408]{4,3,2,1,0:T(8,128)S(1)} %slice_add_fusion.25), channel_id=1, source_target_pairs={{0,8},{1,9},{2,10},{3,11},{4,12},{5,13},{6,14},{7,15},{8,0},{9,1},... | collective-permute-start | bytes 2162696 | tf_op jit(solution)/shard_map/ppermute | solution.py:267
  736.1 11.3 %collective-permute-start.23 = (f32[1,1,1,128,1408]{4,3,2,1,0:T(8,128)S(1)}, f32[1,1,1,128,1408]{4,3,2,1,0:T(8,128)S(1)}, u32[]{:S(2)}, u32[]{:S(2)}) collective-permute-start(f32[1,1,1,128,1408]{4,3,2,1,0:T(8,128)S(1)} %slice_add_fusion.24), channel_id=1, source_target_pairs={{0,4},{1,5},{2,6},{3,7},{4,0},{5,1},{6,2},{7,3},{8,12},{9,13},{10,... | collective-permute-start | bytes 2162696 | tf_op jit(solution)/shard_map/ppermute | solution.py:267
  744.7 2.8 copy-start.6
  (7 other events, 14.2 us)
Sparse Core Ops, SparseCore 0:
  10.3 134.2 all-gather.3
  146.8 154.4 all-gather.5
  371.1 137.7 all-gather.7
